TPU v7x, 8 devices: a whole 2x2x1 slice. The times are simulated.
8 devices in a mesh: rep: 2 (over z, y), kv: 4 (over x, core).
Axes of the slice: x: 2, y: 2, z: 1, core: 2. Of those that a mesh axis runs over, the one named last changes fastest.
Arguments:
- embeds: bfloat16 [2, 128, 4096], P(None, ('rep', 'kv')), parts along dimension 1
- w_query: bfloat16 [2, 4096, 4096], replicated
- w_key: bfloat16 [2, 4096, 1024], replicated
- w_value: bfloat16 [2, 4096, 1024], replicated
- w_out: bfloat16 [2, 4096, 4096], replicated
- w_up: bfloat16 [2, 4096, 14336], replicated
- w_down: bfloat16 [2, 14336, 4096], replicated
- k_pool: bfloat16 [768, 2, 32, 8, 128], P(('rep', 'kv')), parts along dimension 0
- v_pool: bfloat16 [768, 2, 32, 8, 128], P(('rep', 'kv')), parts along dimension 0
- new_table: int32 [128, 2], P('rep'), parts along dimension 0
- seq_lens: int32 [128], P('rep'), parts along dimension 0
- mig_src: int32 [128], P('rep'), parts along dimension 0
- mig_dst: int32 [128], P('rep'), parts along dimension 0
Outputs:
- output 1: bfloat16 [2, 128, 4096], P(None, ('rep', 'kv')), parts along dimension 1
- output 2: bfloat16 [768, 2, 32, 8, 128], P(('rep', 'kv')), parts along dimension 0
- output 3: bfloat16 [768, 2, 32, 8, 128], P(('rep', 'kv')), parts along dimension 0
There are 2 independent parts. A program takes and returns all parts, laid end to end along the dimension named above; an argument that names none is the same for every part.
All inputs are finite; a program needn't handle non-finite values.
Results may differ from a plain program's by a relative error of at most 0.0163449.
Values are sent between devices in bfloat16 or wider.
A program may use at most 2.75 GiB of HBM per device.

v0:
```python
import jax
import jax.numpy as jnp
from jax import lax
from jax.sharding import PartitionSpec as P


def local_index(slot_ids, dev_idx, slots):
    local_ids = slot_ids - dev_idx * slots
    return jnp.where((local_ids >= 0) & (local_ids < slots), local_ids, slots)


def slot_owners(page_table, dev_idx, slots):
    seq_count, page_count = page_table.shape
    seg_ids = local_index(page_table, dev_idx, slots).reshape(-1)
    seq_plus = jnp.broadcast_to(jnp.arange(1, seq_count + 1)[:, None], page_table.shape).reshape(-1)
    page_plus = jnp.broadcast_to(jnp.arange(1, page_count + 1)[None, :], page_table.shape).reshape(-1)
    owner_seq = jax.ops.segment_sum(seq_plus, seg_ids, num_segments=slots + 1)[:slots] - 1
    owner_page = jax.ops.segment_sum(page_plus, seg_ids, num_segments=slots + 1)[:slots] - 1
    return owner_seq, owner_page


def local_partials(queries_all, k_layer, v_layer, owner_seq, owner_page, seq_lens, step_idx):
    seq_count = queries_all.shape[0]
    page_len = k_layer.shape[1]
    head_dim = k_layer.shape[3]
    is_owned = owner_seq >= 0
    safe_seq = jnp.maximum(owner_seq, 0)
    q_slots = jnp.take(queries_all, safe_seq, axis=0)
    scores = jnp.einsum('skgd,sikd->skgi', q_slots, k_layer, preferred_element_type=jnp.float32) * head_dim ** -0.5
    positions = owner_page[:, None] * page_len + jnp.arange(page_len)[None, :]
    limits = jnp.take(seq_lens, safe_seq) + step_idx
    valid_mask = (is_owned[:, None] & (positions <= limits[:, None]))[:, None, None, :]
    scores = jnp.where(valid_mask, scores, -1e30)
    slot_max = jnp.max(scores, axis=-1)
    prob_vals = jnp.where(valid_mask, jnp.exp(scores - slot_max[..., None]), 0.0)
    slot_sum = jnp.sum(prob_vals, axis=-1)
    slot_out = jnp.einsum('skgi,sikd->skgd', prob_vals.astype(jnp.bfloat16), v_layer, preferred_element_type=jnp.float32)
    seg_ids = jnp.where(is_owned, owner_seq, seq_count)
    seq_max = jax.ops.segment_max(slot_max, seg_ids, num_segments=seq_count + 1)[:seq_count]
    seq_max = jnp.maximum(seq_max, -1e30)
    rescale = jnp.exp(slot_max - jnp.take(seq_max, safe_seq, axis=0))
    seq_sum = jax.ops.segment_sum(slot_sum * rescale, seg_ids, num_segments=seq_count + 1)[:seq_count]
    seq_out = jax.ops.segment_sum(slot_out * rescale[..., None], seg_ids, num_segments=seq_count + 1)[:seq_count]
    return jnp.concatenate([seq_out, seq_max[..., None], seq_sum[..., None]], axis=-1)


def merge_partials(packed, group_size):
    head_dim = packed.shape[-1] - 2
    received = lax.all_to_all(packed, 'kv', 0, 0, tiled=True)
    received = received.reshape((group_size, -1) + packed.shape[1:])
    part_out = received[..., :head_dim]
    part_max = received[..., head_dim]
    part_sum = received[..., head_dim + 1]
    glob_max = jnp.max(part_max, axis=0)
    scale_w = jnp.exp(part_max - glob_max)
    total_sum = jnp.sum(scale_w * part_sum, axis=0)
    merged = jnp.sum(scale_w[..., None] * part_out, axis=0) / total_sum[..., None]
    return merged.reshape(merged.shape[0], -1).astype(jnp.bfloat16)


def decode_layer(hidden, layer_idx, step_idx, pools, owners, page_table, seq_lens, weights, dev_idx, group_size):
    w_query, w_key, w_value, w_out, w_up, w_down = weights
    k_pool, v_pool = pools
    owner_seq, owner_page = owners
    slots = k_pool.shape[0]
    page_len = k_pool.shape[2]
    kv_heads = k_pool.shape[3]
    head_dim = k_pool.shape[4]
    num_heads = w_query.shape[2] // head_dim
    queries = jnp.dot(hidden, w_query[layer_idx], preferred_element_type=jnp.float32).astype(jnp.bfloat16)
    new_keys = jnp.dot(hidden, w_key[layer_idx], preferred_element_type=jnp.float32).astype(jnp.bfloat16)
    new_vals = jnp.dot(hidden, w_value[layer_idx], preferred_element_type=jnp.float32).astype(jnp.bfloat16)
    queries_all = lax.all_gather(queries, 'kv', axis=0, tiled=True)
    kv_all = lax.all_gather(jnp.stack([new_keys, new_vals]), 'kv', axis=1, tiled=True)
    seq_count = queries_all.shape[0]
    positions = seq_lens + step_idx
    slot_ids = jnp.take_along_axis(page_table, (positions // page_len)[:, None], axis=1)[:, 0]
    local_ids = local_index(slot_ids, dev_idx, slots)
    offsets = positions % page_len
    kv_rows = kv_all.reshape(2, seq_count, kv_heads, head_dim)
    k_pool = k_pool.at[local_ids, layer_idx, offsets].set(kv_rows[0], mode='drop')
    v_pool = v_pool.at[local_ids, layer_idx, offsets].set(kv_rows[1], mode='drop')
    packed = local_partials(queries_all.reshape(seq_count, kv_heads, num_heads // kv_heads, head_dim), k_pool[:, layer_idx], v_pool[:, layer_idx], owner_seq, owner_page, seq_lens, step_idx)
    attn_out = merge_partials(packed, group_size)
    hidden = (hidden.astype(jnp.float32) + jnp.dot(attn_out, w_out[layer_idx], preferred_element_type=jnp.float32)).astype(jnp.bfloat16)
    up_proj = jnp.dot(hidden, w_up[layer_idx], preferred_element_type=jnp.float32).astype(jnp.bfloat16)
    act_vals = jax.nn.gelu(up_proj.astype(jnp.float32), approximate=True).astype(jnp.bfloat16)
    hidden = (hidden.astype(jnp.float32) + jnp.dot(act_vals, w_down[layer_idx], preferred_element_type=jnp.float32)).astype(jnp.bfloat16)
    return hidden, (k_pool, v_pool)


def decode_step(hidden, step_idx, pools, page_table, seq_lens, weights, dev_idx, group_size):
    owners = slot_owners(page_table, dev_idx, pools[0].shape[0])
    for layer_idx in range(pools[0].shape[1]):
        hidden, pools = decode_layer(hidden, layer_idx, step_idx, pools, owners, page_table, seq_lens, weights, dev_idx, group_size)
    return hidden, pools


def migrate(pools, mig_src, mig_dst, dev_idx):
    k_pool, v_pool = pools
    slots = k_pool.shape[0]
    src_local = local_index(mig_src, dev_idx, slots)
    dst_local = local_index(mig_dst, dev_idx, slots)
    k_pages = jnp.take(k_pool, src_local, axis=0, mode='fill', fill_value=0)
    v_pages = jnp.take(v_pool, src_local, axis=0, mode='fill', fill_value=0)
    k_pages, v_pages = lax.psum((k_pages, v_pages), 'kv')
    k_pool = k_pool.at[dst_local].set(k_pages, mode='drop').at[src_local].set(0, mode='drop')
    v_pool = v_pool.at[dst_local].set(v_pages, mode='drop').at[src_local].set(0, mode='drop')
    return k_pool, v_pool


def solution(mesh):
    group_size = mesh.shape['kv']
    pool_spec = P(('rep', 'kv'))
    tok_spec = P(None, ('rep', 'kv'), None)

    def device_fn(embeds, w_query, w_key, w_value, w_out, w_up, w_down, k_pool, v_pool, new_table, seq_lens, mig_src, mig_dst):
        dev_idx = lax.axis_index('kv')
        slots = k_pool.shape[0]
        weights = (w_query, w_key, w_value, w_out, w_up, w_down)
        slot_remap = jnp.arange(slots * group_size, dtype=jnp.int32).at[mig_dst].set(mig_src)
        old_table = jnp.take(slot_remap, new_table, axis=0)
        pools = (k_pool, v_pool)
        first_out, pools = decode_step(embeds[0], 0, pools, old_table, seq_lens, weights, dev_idx, group_size)
        pools = migrate(pools, mig_src, mig_dst, dev_idx)
        second_out, pools = decode_step(embeds[1], 1, pools, new_table, seq_lens, weights, dev_idx, group_size)
        return jnp.stack([first_out, second_out]), pools[0], pools[1]

    return jax.shard_map(device_fn, mesh=mesh, in_specs=(tok_spec, P(), P(), P(), P(), P(), P(), pool_spec, pool_spec, P('rep', None), P('rep'), P('rep'), P('rep')), out_specs=(tok_spec, pool_spec, pool_spec), check_vma=False)
```

profile of v0, /device:TPU:0, one launch (start us, length us, event | category | flops | bytes accessed | tf_op | source)
XLA Modules:
  0.0 1227.4 jit_solution(16838774369344838026)
XLA Ops:
  150.8 21.5 %all-to-all-done = f32[64,8,4,130]{3,1,2,0:T(8,128)S(1)} async-done(((f32[64,8,4,130]{3,1,2,0:T(8,128)}), f32[64,8,4,130]{3,1,2,0:T(8,128)S(1)}, u32[]{:S(2)}, u32[]{:S(2)}) %all-to-all-start) | async-done | bytes 1064992 | tf_op jit(solution)/shard_map/all_to_all | solution.py:49
  177.5 12.9 %fusion.149 = bf16[16,4096]{1,0:T(8,128)(2,1)S(1)} fusion(bf16[16,4096]{1,0:T(8,128)(2,1)S(1)} %convert_element_type.186, bf16[2,4096,4096]{2,1,0:T(8,128)(2,1)} %param.27, bf16[2,16,4096]{2,1,0:T(8,128)(2,1)} %param.23), kind=kOutput, calls=%fused_computation.157 | convolution fusion | flops 537067520 | bytes 33947648 | tf_op jit(solution)/shard_map/dot_general | solution.py:85
  190.4 37.6 %fusion.243.clone.2 = bf16[16,14336]{1,0:T(8,128)(2,1)S(1)} fusion(bf16[16,4096]{1,0:T(8,128)(2,1)S(1)} %fusion.149, bf16[2,4096,14336]{2,1,0:T(8,128)(2,1)} %param.28), kind=kOutput, calls=%fused_computation.223.clone.clone.clone | convolution fusion | flops 1881571328 | bytes 118030336 | tf_op jit(solution)/shard_map/dot_general | solution.py:86
  228.0 37.6 %fusion.137 = bf16[16,4096]{1,0:T(8,128)(2,1)S(1)} fusion(bf16[2,14336,4096]{2,1,0:T(8,128)(2,1)} %param.29, bf16[16,4096]{1,0:T(8,128)(2,1)S(1)} %fusion.149, bf16[16,14336]{1,0:T(8,128)(2,1)S(1)} %fusion.243.clone.2), kind=kOutput, calls=%fused_computation.153 | convolution fusion | flops 1879244800 | bytes 118161408 | tf_op jit(solution)/shard_map/dot_general | solution.py:88
  351.5 12.8 %fusion.155 = bf16[16,4096]{1,0:T(8,128)(2,1)S(1)} fusion(bf16[2,4096,4096]{2,1,0:T(8,128)(2,1)} %param.24, bf16[2,16,4096]{2,1,0:T(8,128)(2,1)S(1)} %copy-done.37), kind=kOutput, calls=%fused_computation.159 | convolution fusion | flops 536936448 | bytes 33816576 | tf_op jit(solution)/shard_map/dot_general | solution.py:70
  364.3 15.1 %all_gather.28 = bf16[64,4096]{1,0:T(8,128)(2,1)S(1)} all-gather(bf16[16,4096]{1,0:T(8,128)(2,1)S(1)} %fusion.155), channel_id=1, replica_groups=mesh['rep'=2,'kv'=4] {'kv'}, dimensions={0}, use_global_device_ids=true | all-gather | bytes 655360 | tf_op jit(solution)/shard_map/all_gather | solution.py:73
  388.3 12.8 %fusion.158 = bf16[16,4096]{1,0:T(8,128)(2,1)S(1)} fusion(bf16[16,4096]{1,0:T(8,128)(2,1)S(1)} %fusion.137, bf16[2,4096,4096]{2,1,0:T(8,128)(2,1)} %param.24), kind=kOutput, calls=%fused_computation.160 | convolution fusion | flops 536936448 | bytes 33816576 | tf_op jit(solution)/shard_map/dot_general | solution.py:70
  401.2 14.9 %all_gather.26 = bf16[64,4096]{1,0:T(8,128)(2,1)S(1)} all-gather(bf16[16,4096]{1,0:T(8,128)(2,1)S(1)} %fusion.158), channel_id=1, replica_groups=mesh['rep'=2,'kv'=4] {'kv'}, dimensions={0}, use_global_device_ids=true | all-gather | bytes 655360 | tf_op jit(solution)/shard_map/all_gather | solution.py:73
  440.7 181.4 %all-reduce.3.cloned.1.call-done = (bf16[64,2,32,8,128]{4,3,2,1,0:T(8,128)(2,1)}, bf16[64,2,32,8,128]{4,3,2,1,0:T(8,128)(2,1)}) async-done(((bf16[64,2,32,8,128]{4,3,2,1,0:T(8,128)(2,1)}, bf16[64,2,32,8,128]{4,3,2,1,0:T(8,128)(2,1)}), (bf16[64,2,32,8,128]{4,3,2,1,0:T(8,128)(2,1)}, bf16[64,2,32,8,128]{4,3,2,1,0:T(8,128)(2,1)})) %all-reduce.3.cloned.1.call-update) | async-done | bytes 16777232 | tf_op jit(solution)/shard_map/psum | solution.py:106
  622.1 17.9 %scatter_fusion.11 = bf16[96,2,32,8,128]{4,3,2,1,0:T(8,128)(2,1)} fusion(bf16[96,2,32,8,128]{4,3,2,1,0:T(8,128)(2,1)} %scatter_fusion.6, s32[64]{0:T(128)S(1)} %copy-done.29, bf16[64,2,32,8,128]{4,3,2,1,0:T(8,128)(2,1)} %get-tuple-element.11), kind=kCustom, calls=%fused_computation.30 | custom fusion | bytes 25166080 | tf_op jit(solution)/shard_map/scatter | solution.py:107
  645.3 22.1 %scatter_fusion.12 = bf16[96,2,32,8,128]{4,3,2,1,0:T(8,128)(2,1)} fusion(bf16[96,2,32,8,128]{4,3,2,1,0:T(8,128)(2,1)} %scatter_fusion.11, s32[64]{0:T(128)S(1)} %copy-done.28, bf16[64,2,32,8,128]{4,3,2,1,0:T(8,128)(2,1)} %broadcast_in_dim.312), kind=kCustom, calls=%fused_computation.31 | custom fusion | bytes 25166080 | tf_op jit(solution)/shard_map/scatter | solution.py:107
  681.8 16.3 %scatter_fusion.14 = bf16[96,2,32,8,128]{4,3,2,1,0:T(8,128)(2,1)} fusion(bf16[96,2,32,8,128]{4,3,2,1,0:T(8,128)(2,1)} %scatter_fusion.7, s32[64]{0:T(128)S(1)} %copy-done.29, bf16[64,2,32,8,128]{4,3,2,1,0:T(8,128)(2,1)} %get-tuple-element.12), kind=kCustom, calls=%fused_computation.33 | custom fusion | bytes 25166080 | tf_op jit(solution)/shard_map/scatter | solution.py:108
  698.1 20.8 %scatter_fusion.15 = bf16[96,2,32,8,128]{4,3,2,1,0:T(8,128)(2,1)} fusion(bf16[96,2,32,8,128]{4,3,2,1,0:T(8,128)(2,1)} %scatter_fusion.14, s32[64]{0:T(128)S(1)} %copy-done.28, bf16[64,2,32,8,128]{4,3,2,1,0:T(8,128)(2,1)} %broadcast_in_dim.312), kind=kCustom, calls=%fused_computation.34 | custom fusion | bytes 25166080 | tf_op jit(solution)/shard_map/scatter | solution.py:108
  800.6 12.9 %fusion.146 = bf16[16,4096]{1,0:T(8,128)(2,1)S(1)} fusion(bf16[16,4096]{1,0:T(8,128)(2,1)S(1)} %convert_element_type.212, bf16[2,4096,4096]{2,1,0:T(8,128)(2,1)} %param.27, bf16[2,16,4096]{2,1,0:T(8,128)(2,1)} %param.23), kind=kOutput, calls=%fused_computation.156 | convolution fusion | flops 537067520 | bytes 33947648 | tf_op jit(solution)/shard_map/dot_general | solution.py:85
  813.5 37.6 %fusion.271.clone.5 = bf16[16,14336]{1,0:T(8,128)(2,1)S(1)} fusion(bf16[16,4096]{1,0:T(8,128)(2,1)S(1)} %fusion.146, bf16[2,4096,14336]{2,1,0:T(8,128)(2,1)} %param.28), kind=kOutput, calls=%fused_computation.239.clone.clone.clone.2 | convolution fusion | flops 1881571328 | bytes 118030336 | tf_op jit(solution)/shard_map/dot_general | solution.py:86
  851.0 37.6 %fusion.134 = bf16[16,4096]{1,0:T(8,128)(2,1)S(1)} fusion(bf16[2,14336,4096]{2,1,0:T(8,128)(2,1)} %param.29, bf16[16,4096]{1,0:T(8,128)(2,1)S(1)} %fusion.146, bf16[16,14336]{1,0:T(8,128)(2,1)S(1)} %fusion.271.clone.5), kind=kOutput, calls=%fused_computation.152 | convolution fusion | flops 1879244800 | bytes 118161408 | tf_op jit(solution)/shard_map/dot_general | solution.py:88
  897.8 13.2 %fusion.161 = bf16[16,4096]{1,0:T(8,128)(2,1)S(1)} fusion(bf16[16,4096]{1,0:T(8,128)(2,1)S(1)} %fusion.134, bf16[2,4096,4096]{2,1,0:T(8,128)(2,1)} %param.24), kind=kOutput, calls=%fused_computation.161 | convolution fusion | flops 536936448 | bytes 33816576 | tf_op jit(solution)/shard_map/dot_general | solution.py:70
  990.9 29.2 %all_to_all.20 = f32[64,8,4,130]{3,1,2,0:T(8,128)S(1)} all-to-all(f32[64,8,4,130]{3,1,2,0:T(8,128)} %pad_maximum_fusion.3), channel_id=1, replica_groups=mesh['rep'=2,'kv'=4] {'kv'}, dimensions={0} | all-to-all | bytes 2129920 | tf_op jit(solution)/shard_map/all_to_all | solution.py:49
  1036.7 13.5 %fusion.143 = bf16[16,4096]{1,0:T(8,128)(2,1)} fusion(bf16[16,4096]{1,0:T(8,128)(2,1)} %convert_element_type.199, bf16[2,4096,4096]{2,1,0:T(8,128)(2,1)} %param.27, bf16[16,4096]{1,0:T(8,128)(2,1)S(1)} %copy-done.10), kind=kOutput, calls=%fused_computation.155 | convolution fusion | flops 537067520 | bytes 33947648 | tf_op jit(solution)/shard_map/dot_general | solution.py:85
  1050.2 38.6 %fusion.257.clone.5 = bf16[16,14336]{1,0:T(8,128)(2,1)} fusion(bf16[16,4096]{1,0:T(8,128)(2,1)} %fusion.143, bf16[2,4096,14336]{2,1,0:T(8,128)(2,1)} %param.28), kind=kOutput, calls=%fused_computation.231.clone.clone.clone.2 | convolution fusion | flops 1881571328 | bytes 118030336 | tf_op jit(solution)/shard_map/dot_general | solution.py:86
  1088.8 38.7 %fusion.164 = bf16[1,16,4096]{2,1,0:T(8,128)(2,1)} fusion(bf16[2,14336,4096]{2,1,0:T(8,128)(2,1)} %param.29, bf16[16,4096]{1,0:T(8,128)(2,1)S(1)} %copy-done.38, bf16[16,14336]{1,0:T(8,128)(2,1)} %fusion.257.clone.5), kind=kOutput, calls=%fused_computation.162 | convolution fusion | flops 1879244800 | bytes 118161408 | tf_op jit(solution)/shard_map/dot_general | solution.py:88
  1131.4 13.1 %fusion.140 = bf16[16,4096]{1,0:T(8,128)(2,1)S(1)} fusion(bf16[16,4096]{1,0:T(8,128)(2,1)S(1)} %convert_element_type.225, bf16[2,4096,4096]{2,1,0:T(8,128)(2,1)} %param.27, bf16[16,4096]{1,0:T(8,128)(2,1)S(1)} %fusion.134), kind=kOutput, calls=%fused_computation.154 | convolution fusion | flops 537067520 | bytes 33947648 | tf_op jit(solution)/shard_map/dot_general | solution.py:85
  1144.5 37.6 %fusion.285.clone.2 = bf16[16,14336]{1,0:T(8,128)(2,1)S(1)} fusion(bf16[16,4096]{1,0:T(8,128)(2,1)S(1)} %fusion.140, bf16[2,4096,14336]{2,1,0:T(8,128)(2,1)} %param.28), kind=kOutput, calls=%fused_computation.247.clone.clone.clone | convolution fusion | flops 1881571328 | bytes 118030336 | tf_op jit(solution)/shard_map/dot_general | solution.py:86
  1182.0 37.6 %fusion.167 = bf16[1,16,4096]{2,1,0:T(8,128)(2,1)S(1)} fusion(bf16[2,14336,4096]{2,1,0:T(8,128)(2,1)} %param.29, bf16[16,4096]{1,0:T(8,128)(2,1)S(1)} %fusion.140, bf16[16,14336]{1,0:T(8,128)(2,1)S(1)} %fusion.285.clone.2), kind=kOutput, calls=%fused_computation.163 | convolution fusion | flops 1879244800 | bytes 118161408 | tf_op jit(solution)/shard_map/dot_general | solution.py:88
  (342 shorter events, 478.5 us)
Async XLA Ops:
  30.0 79.8 %copy-start.31 = (pred[96]{0:T(512)(128)(4,1)}, pred[96]{0:T(512)(128)(4,1)S(1)}, u32[]{:S(2)}) copy-start(pred[96]{0:T(512)(128)(4,1)S(1)} %get-tuple-element.68) | copy-start | bytes 292
  30.0 79.0 %copy-start.25 = (s32[1024]{0:T(1024)}, s32[1024]{0:T(1024)S(1)}, u32[]{:S(2)}) copy-start(s32[1024]{0:T(1024)S(1)} %pad_clamp_fusion.2) | copy-start | bytes 12292
  31.3 103.1 %copy-start.20 = (s32[96]{0:T(128)}, s32[96]{0:T(128)S(1)}, u32[]{:S(2)}) copy-start(s32[96]{0:T(128)S(1)} %get-tuple-element.70) | copy-start | bytes 1156
  93.4 27.4 %copy-start.15 = (pred[96,32]{1,0:T(8,128)(4,1)}, pred[96,32]{1,0:T(8,128)(4,1)S(1)}, u32[]{:S(2)}) copy-start(pred[96,32]{1,0:T(8,128)(4,1)S(1)} %fusion.354) | copy-start | bytes 9220
  143.2 29.0 %all-to-all-start = ((f32[64,8,4,130]{3,1,2,0:T(8,128)}), f32[64,8,4,130]{3,1,2,0:T(8,128)S(1)}, u32[]{:S(2)}, u32[]{:S(2)}) async-start(f32[64,8,4,130]{3,1,2,0:T(8,128)} %pad_maximum_fusion), calls=%async_computation | async-start | bytes 4194304 | tf_op jit(solution)/shard_map/all_to_all | solution.py:49
  146.8 475.3 %all-reduce.3.cloned.1.call-start = ((), (), s32[]{:S(2)}) async-start(), calls=%async_computation.4 | async-start | bytes 33554432 | tf_op jit(solution)/shard_map/psum | solution.py:106
  265.6 122.7 %copy-start.9 = (bf16[16,4096]{1,0:T(8,128)(2,1)}, bf16[16,4096]{1,0:T(8,128)(2,1)S(1)}, u32[]{:S(2)}) copy-start(bf16[16,4096]{1,0:T(8,128)(2,1)S(1)} %fusion.137) | copy-start | bytes 393220
  350.2 386.2 %copy-start.26 = (s32[1024]{0:T(1024)}, s32[1024]{0:T(1024)S(1)}, u32[]{:S(2)}) copy-start(s32[1024]{0:T(1024)S(1)} %pad_clamp_fusion.1) | copy-start | bytes 12292
  382.0 357.8 %copy-start.33 = (pred[96]{0:T(512)(128)(4,1)}, pred[96]{0:T(512)(128)(4,1)S(1)}, u32[]{:S(2)}) copy-start(pred[96]{0:T(512)(128)(4,1)S(1)} %get-tuple-element.59) | copy-start | bytes 292
  382.0 367.4 %copy-start.23 = (s32[96]{0:T(128)}, s32[96]{0:T(128)S(1)}, u32[]{:S(2)}) copy-start(s32[96]{0:T(128)S(1)} %get-tuple-element.61) | copy-start | bytes 1156
  382.1 357.9 %copy-start.17 = (pred[96,32]{1,0:T(8,128)(4,1)}, pred[96,32]{1,0:T(8,128)(4,1)S(1)}, u32[]{:S(2)}) copy-start(pred[96,32]{1,0:T(8,128)(4,1)S(1)} %fusion.355) | copy-start | bytes 9220
  388.3 29.5 %copy-start.16 = (pred[96,32]{1,0:T(8,128)(4,1)S(1)}, pred[96,32]{1,0:T(8,128)(4,1)}, u32[]{:S(2)}) copy-start(pred[96,32]{1,0:T(8,128)(4,1)} %copy-done.15) | copy-start | bytes 9220
  388.3 29.5 %copy-start.32 = (pred[96]{0:T(512)(128)(4,1)S(1)}, pred[96]{0:T(512)(128)(4,1)}, u32[]{:S(2)}) copy-start(pred[96]{0:T(512)(128)(4,1)} %copy-done.31) | copy-start | bytes 292
  425.0 197.1 %copy-start.29 = (s32[64]{0:T(128)S(1)}, s32[64]{0:T(128)}, u32[]{:S(2)}) copy-start(s32[64]{0:T(128)} %get-tuple-element.65) | copy-start | bytes 772
  645.3 22.1 %copy-start.5 = (s32[64]{0:T(128)S(1)}, s32[64]{0:T(128)}, u32[]{:S(2)}) copy-start(s32[64]{0:T(128)} %get-tuple-element.54) | copy-start | bytes 772
  759.2 31.5 %all-to-all-start.2 = ((f32[64,8,4,130]{3,1,2,0:T(8,128)}), f32[64,8,4,130]{3,1,2,0:T(8,128)S(1)}, u32[]{:S(2)}, u32[]{:S(2)}) async-start(f32[64,8,4,130]{3,1,2,0:T(8,128)} %pad_maximum_fusion.2), calls=%async_computation.2 | async-start | bytes 4194304 | tf_op jit(solution)/shard_map/all_to_all | solution.py:49
  767.5 17.3 %copy-start.11 = (f32[64,8,4,1]{1,2,0,3:T(4,128)S(1)}, f32[64,8,4,1]{1,2,0,3:T(4,128)}, u32[]{:S(2)}) copy-start(f32[64,8,4,1]{1,2,0,3:T(4,128)} %get-tuple-element.45) | copy-start | bytes 24580
  790.7 200.3 %all-to-all-start.1 = ((f32[64,8,4,130]{3,1,2,0:T(8,128)}), f32[64,8,4,130]{3,1,2,0:T(8,128)}, u32[]{:S(2)}, u32[]{:S(2)}) async-start(f32[64,8,4,130]{3,1,2,0:T(8,128)} %pad_maximum_fusion.1), calls=%async_computation.1 | async-start | bytes 4194304 | tf_op jit(solution)/shard_map/all_to_all | solution.py:49
  897.8 23.4 %copy-start.4 = (s32[64]{0:T(128)S(1)}, s32[64]{0:T(128)}, u32[]{:S(2)}) copy-start(s32[64]{0:T(128)} %get-tuple-element.53) | copy-start | bytes 772
  927.8 17.4 %copy-start.18 = (pred[96,32]{1,0:T(8,128)(4,1)S(1)}, pred[96,32]{1,0:T(8,128)(4,1)}, u32[]{:S(2)}) copy-start(pred[96,32]{1,0:T(8,128)(4,1)} %copy-done.17) | copy-start | bytes 9220
  927.8 17.4 %copy-start.34 = (pred[96]{0:T(512)(128)(4,1)S(1)}, pred[96]{0:T(512)(128)(4,1)}, u32[]{:S(2)}) copy-start(pred[96]{0:T(512)(128)(4,1)} %copy-done.33) | copy-start | bytes 292
  1050.2 38.6 %copy-start.38 = (bf16[16,4096]{1,0:T(8,128)(2,1)S(1)}, bf16[16,4096]{1,0:T(8,128)(2,1)}, u32[]{:S(2)}) copy-start(bf16[16,4096]{1,0:T(8,128)(2,1)} %fusion.143) | copy-start | bytes 393220
  1088.8 41.6 %copy-start.13 = (f32[16,8,4]{1,2,0:T(4,128)S(1)}, f32[16,8,4]{1,2,0:T(4,128)}, u32[]{:S(2)}) copy-start(f32[16,8,4]{1,2,0:T(4,128)} %get-tuple-element.80) | copy-start | bytes 6148
  1182.0 37.6 %copy-start.14 = (bf16[1,16,4096]{2,1,0:T(8,128)(2,1)S(1)}, bf16[1,16,4096]{2,1,0:T(8,128)(2,1)}, u32[]{:S(2)}) copy-start(bf16[1,16,4096]{2,1,0:T(8,128)(2,1)} %fusion.164) | copy-start | bytes 393220
  (19 other events, 138.6 us)
Sparse Core Ops, SparseCore 0:
  329.3 292.7 all-reduce.2
where the time goes:
time: 1240 us; the launch traced here: 1230 us
  matrix products  483 us (39%)
  local copies, waits for them, and re-layouts  285 us (23%)
  waiting for transfers between devices  203 us (16%)
  blocking collectives  118 us (10%)
  other arithmetic  111 us (9%)
  between operations  15.8 us (1%)
    psum x1, waiting for transfers between devices, migrate(): k_pages, v_pages = lax.psum((k_pages, v_pages), 'kv')  181 us
    dot_general x4, matrix products, decode_layer(): jnp.dot(act_vals, w_down[layer_idx], preferred_element_type=jnp.float32)  151 us
    dot_general x4, matrix products, decode_layer(): jnp.dot(hidden, w_up[layer_idx], preferred_element_type=jnp.float32)  151 us
    dot_general x4, matrix products, decode_layer(): jnp.dot(attn_out, w_out[layer_idx], preferred_element_type=jnp.float32)  52.4 us
    dot_general x4, matrix products, decode_layer(): jnp.dot(hidden, w_query[layer_idx], preferred_element_type=jnp.float32)  51.7 us
    all_gather x4, blocking collectives, decode_layer(): queries_all = lax.all_gather(queries, 'kv', axis=0, tiled=True)  49.1 us
    scatter x2, local copies, waits for them, and re-layouts, migrate(): k_pool.at[dst_local].set(k_pages, mode='drop').at[src_local]  40 us
    all_gather x4, blocking collectives, decode_layer(): lax.all_gather(jnp.stack([new_keys, new_vals]), 'kv', axis=1, tiled=True)  39.4 us
  transfers between devices with their start and end apart: 4, of which 2 were waited for; matrix products, arithmetic and copies ran while one was open for 23% of the time, Pallas kernels for 0%

commit v1 on v0

v1 whole, which is shorter than its diff:
```python
import functools

import jax
import jax.numpy as jnp
from jax import lax
from jax.experimental import pallas as pl
from jax.experimental.pallas import tpu as pltpu
from jax.sharding import PartitionSpec as P

BF16 = jnp.bfloat16
F32 = jnp.float32
MESH = pl.DeviceIdType.MESH
NEG = -3.0e38
VMEM_LIMIT = 60 * 1024 * 1024

D = 4096
HEADS = 32
KV_HEADS = 8
HEAD = 128
FF = 14336
PAGE = 32
LAYERS = 2
SEQS = 64
TOK = 64
HALF_HEADS = HEADS // 2
ROWS = TOK * HALF_HEADS
TN = 512
SCALE = HEAD ** -0.5


def dot(a, b):
    return jnp.dot(a, b, preferred_element_type=F32)


def places():
    me = lax.axis_index('kv')
    core = lax.rem(me, 2)
    chip = me // 2
    partner = me + 1 - 2 * core
    across = lax.rem(me + 2, 4)
    diag = lax.rem(partner + 2, 4)
    return me, chip, core, partner, across, diag


def meet(peers):
    barrier = pltpu.get_barrier_semaphore()
    for peer in peers:
        pl.semaphore_signal(barrier, inc=1, device_id={'kv': peer}, device_id_type=MESH)
    pl.semaphore_wait(barrier, len(peers))


def send(src, dst, send_sem, recv_sem, peer):
    return pltpu.make_async_remote_copy(src_ref=src, dst_ref=dst, send_sem=send_sem, recv_sem=recv_sem, device_id={'kv': peer}, device_id_type=MESH)


VMEM = pl.BlockSpec(memory_space=pltpu.VMEM)
ANY = pl.BlockSpec(memory_space=pl.ANY)
DMA = pltpu.SemaphoreType.DMA


def qkv_kernel(layer, first, *refs):
    if first:
        emb, wq, wk, wv, q_all, kv, h, wbuf, wsem, psend, precv, xsend, xrecv, fsend, frecv, hsend, hrecv = refs
    else:
        h, wq, wk, wv, q_all, kv, wbuf, wsem, psend, precv, xsend, xrecv, fsend, frecv = refs
    me, chip, core, partner, across, diag = places()

    def fetch(j):
        if j < 4:
            src = wq.at[layer, :, pl.ds(pl.multiple_of(core * 2048 + j * TN, TN), TN)]
        else:
            src = (wk, wv)[j - 4].at[layer, :, pl.ds(pl.multiple_of(core * TN, TN), TN)]
        return pltpu.make_async_copy(src, wbuf.at[j], wsem.at[j])

    for j in range(6):
        fetch(j).start()
    meet((partner, across))
    if first:
        copies = []
        for t in range(2):
            rows = pl.ds(pl.multiple_of(t * 32 + core * 16, 16), 16)
            h[rows, :] = emb[t]
            copies.append(send(emb.at[t], h.at[rows, :], hsend.at[t], hrecv.at[t], partner))
        for copy in copies:
            copy.start()
        for copy in copies:
            copy.wait()

    def to_partner(j):
        ref = q_all.at[chip, core * 4 + j]
        return send(ref, ref, psend.at[j], precv.at[j], partner)

    def to_across(j):
        ref = q_all.at[chip, core * 4 + j]
        return send(ref, ref, xsend.at[j], xrecv.at[j], across)

    def forward(j):
        ref = q_all.at[1 - chip, core * 4 + j]
        return send(ref, ref, fsend.at[j], frecv.at[j], partner)

    for j in range(6):
        fetch(j).wait()
        tile = dot(h[...], wbuf[j]).astype(BF16)
        if j < 4:
            q_all[chip, core * 4 + j] = tile
        else:
            kv[:, (j - 4) * TN:(j - 3) * TN] = tile
        if 1 <= j <= 4:
            to_across(j - 1).start()
            to_partner(j - 1).start()
    for j in range(4):
        to_across(j).wait_recv()
        forward(j).start()
    for j in range(4):
        to_across(j).wait_send()
        to_partner(j).wait()
        forward(j).wait()


def run_qkv(layer, h, weights, first):
    wq, wk, wv = weights[:3]
    out_shape = [jax.ShapeDtypeStruct((2, 8, TOK, TN), BF16), jax.ShapeDtypeStruct((TOK, 2 * TN), BF16)]
    if first:
        out_shape.append(jax.ShapeDtypeStruct((TOK, D), BF16))
    scratch = [pltpu.VMEM((6, D, TN), BF16), DMA((6,))] + [DMA((4,))] * 6
    if first:
        scratch += [DMA((2,))] * 2
    return pl.pallas_call(
        functools.partial(qkv_kernel, layer, first),
        name=f'qkv{layer}',
        out_shape=out_shape,
        in_specs=[VMEM, ANY, ANY, ANY],
        out_specs=[VMEM] * len(out_shape),
        scratch_shapes=scratch,
        cost_estimate=pl.CostEstimate(flops=2 * TOK * D * 6 * TN * 8, bytes_accessed=D * 6 * TN * 2, transcendentals=0),
        compiler_params=pltpu.CompilerParams(collective_id=layer * 3, has_side_effects=True, vmem_limit_bytes=VMEM_LIMIT),
    )(h, wq, wk, wv)


UNROLL = 2
NBUF = 3


def attend_kernel(layer, count, table, q_all, k_pool, v_pool, part_o, part_l, q_rows, kbuf, vbuf, sems):
    part_o[...] = jnp.zeros_like(part_o)
    part_l[...] = jnp.full_like(part_l, NEG)
    groups = (count[0] + UNROLL - 1) // UNROLL

    def copies(g, start):
        slot = lax.rem(g, NBUF)
        for u in range(UNROLL):
            for j in range(2):
                page = table[1 + j, g * UNROLL + u]
                for pool, buf in ((k_pool, kbuf), (v_pool, vbuf)):
                    copy = pltpu.make_async_copy(pool.at[page, layer], buf.at[slot, u, j], sems.at[slot])
                    copy.start() if start else copy.wait()

    for g in range(NBUF - 1):
        @pl.when(g < groups)
        def _():
            copies(g, True)

    for chip in range(2):
        for tile in range(8):
            for i in range(4):
                rows = q_all[chip, tile, :, i * HEAD:(i + 1) * HEAD].astype(F32)
                q_rows[pl.ds(chip * TOK * HEADS + tile * 4 + i, TOK, stride=HEADS), :] = rows

    row = lax.broadcasted_iota(jnp.int32, (2 * HEADS, 256), 0)
    col = lax.broadcasted_iota(jnp.int32, (2 * HEADS, 256), 1)
    pos = jnp.where((row % HEADS) // 4 == col % KV_HEADS, col // KV_HEADS, PAGE)

    def step(g, carry):
        slot = lax.rem(g, NBUF)
        copies(g, False)

        @pl.when(g + NBUF - 1 < groups)
        def _():
            copies(g + NBUF - 1, True)

        outs = []
        for u in range(UNROLL):
            item = g * UNROLL + u
            seq = table[0, item]
            base = (seq // 32) * TOK * HEADS + (seq % 32) * HEADS
            q0 = q_rows[pl.ds(pl.multiple_of(base, HEADS), HEADS), :]
            q1 = q_rows[pl.ds(pl.multiple_of(base + 32 * HEADS, HEADS), HEADS), :]
            q = jnp.concatenate([q0, q1], axis=0).astype(BF16)
            scores = []
            for j in range(2):
                s = lax.dot_general(q, kbuf[slot, u, j], (((1,), (1,)), ((), ())), preferred_element_type=F32) * SCALE
                scores.append(jnp.where(pos < table[3 + j, item], s, NEG))
            top = jnp.max(jnp.maximum(scores[0], scores[1]), axis=1, keepdims=True)
            probs = [jnp.where(s > NEG, jnp.exp(s - top), 0.0) for s in scores]
            total = jnp.sum(probs[0] + probs[1], axis=1, keepdims=True)
            out = sum(dot(p.astype(BF16), vbuf[slot, u, j]) for j, p in enumerate(probs))
            live = total > 0.0
            safe = jnp.where(live, total, 1.0)
            lse = jnp.where(live, top + jnp.log(safe), NEG)
            outs.append((seq, out / safe, jnp.broadcast_to(lse, (2 * HEADS, HEAD))))
        for seq, out, lse in outs:
            for t in range(2):
                for half in range(2):
                    rows = slice(t * HEADS + half * HALF_HEADS, t * HEADS + (half + 1) * HALF_HEADS)
                    part_o[seq // 32, half, t * 32 + seq % 32] = out[rows]
                    part_l[seq // 32, half, t * 32 + seq % 32] = lse[rows]
        return carry

    lax.fori_loop(0, groups, step, 0)


def run_attend(layer, count, table, q_all, k_pool, v_pool):
    slots = k_pool.shape[0]
    shape = jax.ShapeDtypeStruct((2, 2, TOK, HALF_HEADS, HEAD), F32)
    page = (UNROLL, 2, PAGE * KV_HEADS, HEAD)
    smem = pl.BlockSpec(memory_space=pltpu.SMEM)
    return pl.pallas_call(
        functools.partial(attend_kernel, layer),
        name=f'attend{layer}',
        out_shape=[shape, shape],
        in_specs=[smem, smem, VMEM, ANY, ANY],
        out_specs=[VMEM, VMEM],
        scratch_shapes=[
            pltpu.VMEM((2 * TOK * HEADS, HEAD), F32),
            pltpu.VMEM((NBUF,) + page, BF16),
            pltpu.VMEM((NBUF,) + page, BF16),
            DMA((NBUF,)),
        ],
        cost_estimate=pl.CostEstimate(flops=2 * 10 ** 10, bytes_accessed=16 * 2 ** 20, transcendentals=0),
        compiler_params=pltpu.CompilerParams(vmem_limit_bytes=VMEM_LIMIT),
    )(count, table, q_all, k_pool.reshape(slots, LAYERS, PAGE * KV_HEADS, HEAD), v_pool.reshape(slots, LAYERS, PAGE * KV_HEADS, HEAD))


def merge(parts):
    top = functools.reduce(jnp.maximum, [l for _, l in parts])
    weights = [jnp.exp(l - top) for _, l in parts]
    total = functools.reduce(jnp.add, weights)
    out = functools.reduce(jnp.add, [w * o for w, (o, _) in zip(weights, parts)]) / total
    return out, top + jnp.log(total)


CH = 64


def out_kernel(layer, h, q_all, kv, part_o, part_l, wo, out, wbuf, wsem, got_o, got_l, mine_o, mine_l, give_o, give_l, far_o, far_l,
               q_rows, k_rows, v_rows, attn, psend, precv, dsend, drecv, xsend, xrecv, ssem, rsem):
    me, chip, core, partner, across, diag = places()

    def fetch(j):
        src = wo.at[layer, pl.ds(pl.multiple_of(core * 2048, 2048), 2048), pl.ds(j * TN, TN)]
        return pltpu.make_async_copy(src, wbuf.at[j], wsem.at[j])

    for j in range(8):
        fetch(j).start()
    meet((partner, across))

    near = []
    for which in range(2):
        owner = 1 - chip if which == 0 else chip
        pair = [
            send(part_o.at[owner, 1 - core], got_o.at[which], dsend.at[which, 0], drecv.at[which, 0], partner),
            send(part_l.at[owner, 1 - core], got_l.at[which], dsend.at[which, 1], drecv.at[which, 1], partner),
        ]
        for copy in pair:
            copy.start()
        near.append(pair)

    lane = lax.broadcasted_iota(jnp.int32, (8, HEAD), 1)

    for copy in near[0]:
        copy.wait_recv()
    compact = jnp.zeros((8, HEAD), F32)
    for i in range(TOK):
        o, l = merge([(part_o[1 - chip, core, i], part_l[1 - chip, core, i]), (got_o[0, i], got_l[0, i])])
        give_o[i] = o
        compact = jnp.where(lane == 2 * i, l[:8], compact)
        compact = jnp.where(lane == 2 * i + 1, l[8:], compact)
    give_l[...] = compact
    far = [
        send(give_l, far_l, xsend.at[0], xrecv.at[0], across),
        send(give_o, far_o, xsend.at[1], xrecv.at[1], across),
    ]
    for copy in far:
        copy.start()

    for head in range(HALF_HEADS):
        tile = core * 4 + head // 4
        rows = pl.ds(head, TOK, stride=HALF_HEADS)
        q_rows[rows, :] = q_all[chip, tile, :, (head % 4) * HEAD:(head % 4 + 1) * HEAD].astype(F32)
        k_rows[rows, :] = kv[:, (head // 4) * HEAD:(head // 4 + 1) * HEAD].astype(F32)
        v_rows[rows, :] = kv[:, TN + (head // 4) * HEAD:TN + (head // 4 + 1) * HEAD].astype(F32)
    for copy in near[1]:
        copy.wait_recv()

    half = ROWS // 2

    def score(q, k):
        s = jnp.sum(q * k, axis=1, keepdims=True) * SCALE
        return jnp.broadcast_to(s, q.shape)

    def own(i, carry):
        a = pl.ds(pl.multiple_of(i * HALF_HEADS, HALF_HEADS), HALF_HEADS)
        b = pl.ds(pl.multiple_of(half + i * HALF_HEADS, HALF_HEADS), HALF_HEADS)
        k0, v0, k1, v1 = k_rows[a, :], v_rows[a, :], k_rows[b, :], v_rows[b, :]
        q0, q1 = q_rows[a, :], q_rows[b, :]
        j = i + TOK // 2
        o, l = merge([(part_o[chip, core, i], part_l[chip, core, i]), (got_o[1, i], got_l[1, i]), (v0, score(q0, k0))])
        mine_o[i] = o
        mine_l[i] = l
        o, l = merge([(part_o[chip, core, j], part_l[chip, core, j]), (got_o[1, j], got_l[1, j]), (v0, score(q1, k0)), (v1, score(q1, k1))])
        mine_o[j] = o
        mine_l[j] = l
        return carry

    lax.fori_loop(0, TOK // 2, own, 0)

    for copy in far:
        copy.wait_recv()
    spread = far_l[...]
    for i in range(TOK):
        l = jnp.concatenate([
            jnp.broadcast_to(spread[:, 2 * i:2 * i + 1], (8, HEAD)),
            jnp.broadcast_to(spread[:, 2 * i + 1:2 * i + 2], (8, HEAD)),
        ], axis=0)
        o, _ = merge([(mine_o[i], mine_l[i]), (far_o[i], l)])
        q_rows[i * HALF_HEADS:(i + 1) * HALF_HEADS, :] = o
    for head in range(HALF_HEADS):
        attn[:, head * HEAD:(head + 1) * HEAD] = q_rows[pl.ds(head, TOK, stride=HALF_HEADS), :].astype(BF16)

    def reduce(j):
        return send(psend.at[j], precv.at[j], ssem.at[j], rsem.at[j], partner)

    def project(j, carry):
        pltpu.make_async_copy(wo.at[layer, pl.ds(0, 2048), pl.ds(0, TN)], wbuf.at[j], wsem.at[j]).wait()
        psend[j] = dot(attn[...], wbuf[j])

        @pl.when(j > 0)
        def _():
            reduce(j - 1).start()
        return carry

    lax.fori_loop(0, 8, project, 0)
    reduce(7).start()
    for j in range(8):
        reduce(j).wait_recv()
        cols = slice(j * TN, (j + 1) * TN)
        out[:, cols] = (h[:, cols].astype(F32) + (psend[j] + precv[j])).astype(BF16)
    for j in range(8):
        reduce(j).wait_send()
    for pair in near:
        for copy in pair:
            copy.wait_send()
    for copy in far:
        copy.wait_send()


def run_out(layer, h, q_all, kv, part_o, part_l, w_out):
    token = (TOK, HALF_HEADS, HEAD)
    return pl.pallas_call(
        functools.partial(out_kernel, layer),
        name=f'out{layer}',
        out_shape=jax.ShapeDtypeStruct((TOK, D), BF16),
        in_specs=[VMEM] * 5 + [ANY],
        out_specs=VMEM,
        scratch_shapes=[
            pltpu.VMEM((8, 2048, TN), BF16),
            DMA((8,)),
            pltpu.VMEM((2,) + token, F32),
            pltpu.VMEM((2,) + token, F32),
            pltpu.VMEM(token, F32),
            pltpu.VMEM(token, F32),
            pltpu.VMEM(token, F32),
            pltpu.VMEM((8, HEAD), F32),
            pltpu.VMEM(token, F32),
            pltpu.VMEM((8, HEAD), F32),
            pltpu.VMEM((ROWS, HEAD), F32),
            pltpu.VMEM((ROWS, HEAD), F32),
            pltpu.VMEM((ROWS, HEAD), F32),
            pltpu.VMEM((TOK, 2048), BF16),
            pltpu.VMEM((8, TOK, TN), F32),
            pltpu.VMEM((8, TOK, TN), F32),
            DMA((2, 2)),
            DMA((2, 2)),
            DMA((2,)),
            DMA((2,)),
            DMA((8,)),
            DMA((8,)),
        ],
        cost_estimate=pl.CostEstimate(flops=10 ** 11, bytes_accessed=20 * 2 ** 20, transcendentals=0),
        compiler_params=pltpu.CompilerParams(collective_id=layer * 3 + 1, has_side_effects=True, vmem_limit_bytes=VMEM_LIMIT),
    )(h, q_all, kv, part_o, part_l, w_out)


NU = 4
ND = 4
UP_TILES = FF // 2 // TN
KROWS = FF // 4
DOWN_TILES = 2 * (D // TN)


def mlp_kernel(layer, h, kv, w_up, w_down, out, kv_all, ubuf, dbuf, act, psend, precv, usem, dsem, ssem, rsem, ksend, krecv):
    me, chip, core, partner, across, diag = places()

    def fetch_up(s):
        src = w_up.at[layer, :, pl.ds(pl.multiple_of(core * (FF // 2) + s * TN, TN), TN)]
        slot = lax.rem(s, NU)
        return pltpu.make_async_copy(src, ubuf.at[slot], usem.at[slot])

    def fetch_down(s):
        src = w_down.at[layer, pl.ds(pl.multiple_of(core * (FF // 2) + lax.rem(s, 2) * KROWS, KROWS), KROWS), pl.ds(pl.multiple_of((s // 2) * TN, TN), TN)]
        slot = lax.rem(s, ND)
        return pltpu.make_async_copy(src, dbuf.at[slot], dsem.at[slot])

    for s in range(NU):
        fetch_up(jnp.int32(s)).start()
    meet((partner, across, diag))
    kv_all[me] = kv[...]
    rows = [send(kv, kv_all.at[me], ksend.at[i], krecv.at[i], peer) for i, peer in enumerate((partner, across, diag))]
    for copy in rows:
        copy.start()

    def up(s, carry):
        fetch_up(s).wait()
        u = dot(h[...], ubuf[lax.rem(s, NU)]).astype(BF16)
        a = jax.nn.gelu(u.astype(F32), approximate=True).astype(BF16)
        act[s // 7, :, pl.ds(pl.multiple_of(lax.rem(s, 7) * TN, TN), TN)] = a

        @pl.when(s + NU < UP_TILES)
        def _():
            fetch_up(s + NU).start()

        @pl.when(s + NU >= UP_TILES)
        def _():
            fetch_down(s + NU - UP_TILES).start()
        return carry

    lax.fori_loop(0, UP_TILES, up, 0)

    def reduce(j):
        return send(psend.at[j], precv.at[j], ssem.at[j], rsem.at[j], partner)

    def down(j, carry):
        total = None
        for k in range(2):
            s = 2 * j + k
            fetch_down(s).wait()
            part = dot(act[k], dbuf[lax.rem(s, ND)])
            total = part if total is None else total + part

            @pl.when(s + ND < DOWN_TILES)
            def _():
                fetch_down(s + ND).start()
        psend[j] = total

        @pl.when(j > 0)
        def _():
            reduce(j - 1).start()
        return carry

    lax.fori_loop(0, 8, down, 0)
    reduce(7).start()
    for j in range(8):
        reduce(j).wait_recv()
        cols = slice(j * TN, (j + 1) * TN)
        out[:, cols] = (h[:, cols].astype(F32) + (psend[j] + precv[j])).astype(BF16)
    for j in range(8):
        reduce(j).wait_send()
    for copy in rows:
        copy.wait()


def run_mlp(layer, h, kv, w_up, w_down):
    return pl.pallas_call(
        functools.partial(mlp_kernel, layer),
        name=f'mlp{layer}',
        out_shape=[jax.ShapeDtypeStruct((TOK, D), BF16), jax.ShapeDtypeStruct((4, TOK, 2 * TN), BF16)],
        in_specs=[VMEM, VMEM, ANY, ANY],
        out_specs=[VMEM, VMEM],
        scratch_shapes=[
            pltpu.VMEM((NU, D, TN), BF16),
            pltpu.VMEM((ND, KROWS, TN), BF16),
            pltpu.VMEM((2, TOK, KROWS), BF16),
            pltpu.VMEM((8, TOK, TN), F32),
            pltpu.VMEM((8, TOK, TN), F32),
            DMA((NU,)),
            DMA((ND,)),
            DMA((8,)),
            DMA((8,)),
            DMA((3,)),
            DMA((3,)),
        ],
        cost_estimate=pl.CostEstimate(flops=2 * TOK * D * FF * 8, bytes_accessed=D * FF * 2, transcendentals=0),
        compiler_params=pltpu.CompilerParams(collective_id=layer * 3 + 2, has_side_effects=True, vmem_limit_bytes=VMEM_LIMIT),
    )(h, kv, w_up, w_down)


RING = 8


def pools_kernel(table, k_pool, v_pool, k_moved, v_moved, k_rows, v_rows, k_out, v_out, buf, in_sem, out_sem):
    slots = k_pool.shape[0]

    def load(i, wait):
        slot = lax.rem(i, RING)
        kind = table[0, i]
        for p, (pool, moved) in enumerate(((k_pool, k_moved), (v_pool, v_moved))):
            dst = buf.at[slot, p]
            if wait:
                pltpu.make_async_copy(pool.at[0], dst, in_sem.at[slot, p]).wait()
            else:
                @pl.when(kind < 0)
                def _():
                    pltpu.make_async_copy(pool.at[i], dst, in_sem.at[slot, p]).start()

                @pl.when(kind >= 0)
                def _():
                    pltpu.make_async_copy(moved.at[kind], dst, in_sem.at[slot, p]).start()

    def store(i):
        slot = lax.rem(i, RING)
        return [pltpu.make_async_copy(buf.at[slot, p], ref.at[i], out_sem.at[slot, p]) for p, ref in enumerate((k_out, v_out))]

    AHEAD = RING // 2
    for i in range(AHEAD):
        load(jnp.int32(i), False)

    def step(i, carry):
        @pl.when((i + AHEAD < slots) & (i + AHEAD >= RING))
        def _():
            for copy in store(i + AHEAD - RING):
                copy.wait()

        @pl.when(i + AHEAD < slots)
        def _():
            load(i + AHEAD, False)
        load(i, True)
        slot = lax.rem(i, RING)

        @pl.when(table[1, i] > 0)
        def _():
            buf[slot] = jnp.zeros(buf.shape[1:], BF16)
        for t in range(2):
            row = table[2 + t, i]

            @pl.when(row >= 0)
            def _():
                off = table[4 + t, i]
                for l in range(LAYERS):
                    buf[slot, 0, l, off] = k_rows[l, row]
                    buf[slot, 1, l, off] = v_rows[l, row]
        for copy in store(i):
            copy.start()
        return carry

    lax.fori_loop(0, slots, step, 0)

    def drain(i, carry):
        for copy in store(i):
            copy.wait()
        return carry

    lax.fori_loop(slots - RING, slots, drain, 0)


def run_pools(table, k_pool, v_pool, k_moved, v_moved, k_rows, v_rows):
    smem = pl.BlockSpec(memory_space=pltpu.SMEM)
    shape = jax.ShapeDtypeStruct(k_pool.shape, BF16)
    return pl.pallas_call(
        pools_kernel,
        name='pools',
        out_shape=[shape, shape],
        in_specs=[smem, ANY, ANY, ANY, ANY, VMEM, VMEM],
        out_specs=[ANY, ANY],
        scratch_shapes=[
            pltpu.VMEM((RING, 2) + k_pool.shape[1:], BF16),
            DMA((RING, 2)),
            DMA((RING, 2)),
        ],
        cost_estimate=pl.CostEstimate(flops=2 * 10 ** 10, bytes_accessed=50 * 2 ** 20, transcendentals=0),
        compiler_params=pltpu.CompilerParams(vmem_limit_bytes=VMEM_LIMIT),
    )(table, k_pool, v_pool, k_moved, v_moved, k_rows, v_rows)


def pick(mask, values, fallback):
    return jnp.where(jnp.any(mask, axis=1), jnp.sum(jnp.where(mask, values[None, :], 0), axis=1), fallback)


def attend_tables(old_table, seq_lens, me, slots):
    local = old_table - me * slots
    owned = (local >= 0) & (local < slots)
    some = owned[:, 0] | owned[:, 1]
    ids = jnp.arange(SEQS, dtype=jnp.int32)
    rank = jnp.sum(jnp.where(some[None, :] & (ids[None, :] < ids[:, None]), 1, 0), axis=1)
    count = jnp.sum(some.astype(jnp.int32))
    first = jnp.where(owned[:, 0], local[:, 0], local[:, 1])
    second = jnp.where(owned[:, 1], local[:, 1], local[:, 0])
    lim_a = jnp.where(owned[:, 0], jnp.minimum(seq_lens, PAGE), 0)
    lim_b = jnp.where(owned[:, 1], jnp.maximum(seq_lens - PAGE, 0), 0)
    want = jnp.minimum(ids, count - 1)
    hit = some[None, :] & (rank[None, :] == want[:, None])
    features = jnp.stack([ids, first, second, lim_a, lim_b])
    table = jnp.sum(jnp.where(hit[None], features[:, None, :], 0), axis=2)
    return count.reshape(1), table.astype(jnp.int32)


def pool_tables(new_table, seq_lens, mig_src, mig_dst, me, slots):
    ids = me * slots + jnp.arange(slots, dtype=jnp.int32)
    moved = pick(ids[:, None] == mig_dst[None, :], jnp.arange(mig_dst.shape[0], dtype=jnp.int32), -1)
    gone = jnp.any(ids[:, None] == mig_src[None, :], axis=1).astype(jnp.int32)
    out = [moved, gone]
    seqs = jnp.arange(SEQS, dtype=jnp.int32)
    offsets = []
    for t in range(2):
        pos = seq_lens + t
        page = pos // PAGE
        slot = jnp.where(page == 0, new_table[:, 0], new_table[:, 1])
        hit = ids[:, None] == slot[None, :]
        out.append(pick(hit, (seqs // 32) * TOK + t * 32 + seqs % 32, -1))
        offsets.append(pick(hit, pos - page * PAGE, 0))
    return jnp.stack(out + offsets).astype(jnp.int32)


def moved_pages(k_pool, v_pool, mig_src, me):
    slots = k_pool.shape[0]
    local = mig_src - me * slots
    local = jnp.where((local >= 0) & (local < slots), local, slots)
    k_pages = jnp.take(k_pool, local, axis=0, mode='fill', fill_value=0)
    v_pages = jnp.take(v_pool, local, axis=0, mode='fill', fill_value=0)
    return lax.psum((k_pages, v_pages), 'kv')


def by_token(kv_all):
    x = kv_all.reshape(2, 2, TOK, 2, 4, HEAD)
    return x.transpose(3, 0, 2, 1, 4, 5).reshape(2, 2 * TOK, KV_HEADS, HEAD)


def solution(mesh):
    pool_spec = P(('rep', 'kv'))
    tok_spec = P(None, ('rep', 'kv'), None)

    def device_fn(embeds, w_query, w_key, w_value, w_out, w_up, w_down, k_pool, v_pool, new_table, seq_lens, mig_src, mig_dst):
        me = lax.axis_index('kv')
        slots = k_pool.shape[0]
        weights = (w_query, w_key, w_value)
        flat = new_table.reshape(-1)
        old_table = pick(flat[:, None] == mig_dst[None, :], mig_src, flat).reshape(new_table.shape)
        count, table = attend_tables(old_table, seq_lens, me, slots)
        k_moved, v_moved = moved_pages(k_pool, v_pool, mig_src, me)
        rows = []
        h = None
        for layer in range(LAYERS):
            if layer == 0:
                q_all, kv, h = run_qkv(layer, embeds, weights, True)
            else:
                q_all, kv = run_qkv(layer, h, weights, False)
            part_o, part_l = run_attend(layer, count, table, q_all, k_pool, v_pool)
            h = run_out(layer, h, q_all, kv, part_o, part_l, w_out)
            h, kv_all = run_mlp(layer, h, kv, w_up, w_down)
            rows.append(by_token(kv_all))
        rows = jnp.stack(rows)
        k_out, v_out = run_pools(pool_tables(new_table, seq_lens, mig_src, mig_dst, me, slots), k_pool, v_pool, k_moved, v_moved, rows[:, 0], rows[:, 1])
        y = lax.dynamic_slice_in_dim(h.reshape(2, 32, D), (me % 2) * 16, 16, axis=1)
        return y, k_out, v_out

    return jax.shard_map(device_fn, mesh=mesh, in_specs=(tok_spec, P(), P(), P(), P(), P(), P(), pool_spec, pool_spec, P('rep', None), P('rep'), P('rep'), P('rep')), out_specs=(tok_spec, pool_spec, pool_spec), check_vma=False)
```

time: 1240 us -> 404 us (0.33)
  matrix products: 483 us -> 0 us
  Pallas kernels: 0 us -> 281 us
  local copies, waits for them, and re-layouts: 285 us -> 25.8 us
  waiting for transfers between devices: 203 us -> 64.8 us
  blocking collectives: 118 us -> 0 us
  other arithmetic: 111 us -> 16.2 us
    dot_general x32 -> x0, matrix products: 483 us -> none  [the longest x4 151 us: decode_layer(): jnp.dot(act_vals, w_down[layer_idx], preferred_element_type=jnp.float32)]
    pallas_call x0 -> x9, Pallas kernels: none -> 281 us  [the longest x2 91.1 us: run_out(): pl.pallas_call(functools.partial(out_kernel, layer), name=f'out{layer}',...]
    scatter x13 -> x0, local copies, waits for them, and re-layouts: 134 us -> none  [the longest x2 40 us: migrate(): k_pool.at[dst_local].set(k_pages, mode='drop').at[src_local]]
    psum x1, waiting for transfers between devices: 181 us -> 64.7 us  [moved_pages(): return lax.psum((k_pages, v_pages), 'kv')]
    all_gather x8 -> x0, blocking collectives: 88.5 us -> none  [the longest x4 49.1 us: decode_layer(): queries_all = lax.all_gather(queries, 'kv', axis=0, tiled=True)]
    scatter-add x12 -> x0, other arithmetic: 49 us -> none  [the longest x4 27.2 us: local_partials(): jax.ops.segment_sum(slot_out * rescale[..., None], seg_ids, num_segments=...]
    slice x12 -> x1, local copies, waits for them, and re-layouts: 45.3 us -> 0.18 us  [attend_tables(): some = owned[:, 0] | owned[:, 1]]
    unnamed x104 -> x25, local copies, waits for them, and re-layouts: 34 us -> 0.78 us
  transfers between devices with their start and end apart: 4 -> 1, of which waited for: 2 -> 1; matrix products, arithmetic and copies ran while one was open for 23% -> 2% of each run, Pallas kernels for 0% -> 63%
where the time goes in v1:
time: 404 us; the launch traced here: 403 us
  Pallas kernels  281 us (70%)
  waiting for transfers between devices  64.8 us (16%)
  local copies, waits for them, and re-layouts  25.8 us (6%)
  other arithmetic  16.2 us (4%)
  between operations  15.1 us (4%)
    pallas_call x2, Pallas kernels, run_out(): pl.pallas_call(functools.partial(out_kernel, layer), name=f'out{layer}',...  91.1 us
    pallas_call x2, Pallas kernels, run_mlp(): pl.pallas_call(functools.partial(mlp_kernel, layer), name=f'mlp{layer}',...  81.4 us
    psum x1, waiting for transfers between devices, moved_pages(): return lax.psum((k_pages, v_pages), 'kv')  64.7 us
    pallas_call x2, Pallas kernels, run_qkv(): pl.pallas_call(functools.partial(qkv_kernel, layer, first), name=f'qkv{la...  44.9 us
    pallas_call x2, Pallas kernels, run_attend(): pl.pallas_call(functools.partial(attend_kernel, layer), name=f'attend{lay...  38.2 us
    pallas_call x1, Pallas kernels, run_pools(): pl.pallas_call(pools_kernel, name='pools', out_shape=[shape, shape], in_s...  25.6 us
    select_n x1, other arithmetic, moved_pages(): v_pages = jnp.take(v_pool, local, axis=0, mode='fill', fill_value=0)  11.6 us
    gather x1, local copies, waits for them, and re-layouts, moved_pages(): v_pages = jnp.take(v_pool, local, axis=0, mode='fill', fill_value=0)  10 us
  transfers between devices with their start and end apart: 1, of which 1 were waited for; matrix products, arithmetic and copies ran while one was open for 2% of the time, Pallas kernels for 63%

profile of v1, /device:TPU:0, one launch (start us, length us, event | category | flops | bytes accessed | tf_op | source)
XLA Modules:
  0.0 403.2 jit_solution(8812740564054538240)
XLA Ops:
  7.2 0.7 compare_and_fusion.2
  7.9 10.0 %gather_fusion.1 = bf16[64,2,32,8,128]{4,3,2,1,0:T(8,128)(2,1)} fusion(bf16[96,2,32,8,128]{4,3,2,1,0:T(8,128)(2,1)} %v_pool.1, s32[1024]{0:T(1024)S(1)} %pad_clamp_fusion), kind=kCustom, calls=%fused_computation.1.clone | custom fusion | bytes 16777472 | tf_op jit(solution)/shard_map/jit(_take)/gather | solution.py:628
  17.9 10.0 %gather_fusion = bf16[64,2,32,8,128]{4,3,2,1,0:T(8,128)(2,1)} fusion(bf16[96,2,32,8,128]{4,3,2,1,0:T(8,128)(2,1)} %k_pool.1, s32[1024]{0:T(1024)S(1)} %pad_clamp_fusion), kind=kCustom, calls=%fused_computation.clone | custom fusion | bytes 16777472 | tf_op jit(solution)/shard_map/jit(_take)/gather | solution.py:627
  27.9 11.6 %broadcast_select_fusion = (bf16[64,2,32,8,128]{4,3,2,1,0:T(8,128)(2,1)}, bf16[64,2,32,8,128]{4,3,2,1,0:T(8,128)(2,1)}) fusion(bf16[64,2,32,8,128]{4,3,2,1,0:T(8,128)(2,1)} %gather_fusion.1, pred[64]{0:T(512)(128)(4,1)S(1)} %get-tuple-element.51, bf16[64,2,32,8,128]{4,3,2,1,0:T(8,128)(2,1)} %gather_fusion), kind=kLoop, calls=%fused_computation.2 | loop fusion | flops 8388608 | bytes 33554496 | tf_op jit(solution)/shard_map/jit(_take)/select_n | solution.py:628
  39.5 0.6 copy-done.5
  41.1 0.2 select_reduce_fusion.1
  41.3 1.2 multiply_subtract_fusion.1
  43.4 0.8 select_reduce_fusion.table
  44.2 23.8 %qkv0.1 = (bf16[2,8,64,512]{3,2,1,0:T(8,128)(2,1)}, bf16[64,1024]{1,0:T(8,128)(2,1)}, bf16[64,4096]{1,0:T(8,128)(2,1)}) custom-call(bf16[2,16,4096]{2,1,0:T(8,128)(2,1)} %refs_0_.1, bf16[2,4096,4096]{2,1,0:T(8,128)(2,1)} %refs_1_.3, bf16[2,4096,1024]{2,1,0:T(8,128)(2,1)} %refs_2_.3, bf16[2,4096,1024]{2,1,0:T(8,128)(2,1)} %refs_3_.3), custom_call_target="tpu_custom_call" | custom-call | flops 12884901888 | bytes 25165824 | tf_op jit(solution)/shard_map/qkv0/pallas_call | solution.py:128
  68.0 19.1 %attend0.1 = (f32[2,2,64,16,128]{4,3,2,1,0:T(8,128)}, f32[2,2,64,16,128]{4,3,2,1,0:T(8,128)}) custom-call(s32[1]{0:T(128)} %bitcast.count, s32[5,64]{1,0:T(8,128)} %select_reduce_fusion.table, bf16[2,8,64,512]{3,2,1,0:T(8,128)(2,1)} %get-tuple-element.20.q_all, bf16[96,2,256,128]{3,2,1,0:T(8,128)(2,1)} %bitcast.38, bf16[96,2,256,128]{3,2,1,0:T(8,128)(2,1)} %bitcast.40), custom_call_target="tpu_custom_call" | custom-call | flops 20000000000 | bytes 16777216 | tf_op jit(solution)/shard_map/attend0/pallas_call | solution.py:217
  87.0 45.4 %out0.1.h = bf16[64,4096]{1,0:T(8,128)(2,1)} custom-call(bf16[64,4096]{1,0:T(8,128)(2,1)} %get-tuple-element.19.h, bf16[2,8,64,512]{3,2,1,0:T(8,128)(2,1)} %get-tuple-element.20.q_all, bf16[64,1024]{1,0:T(8,128)(2,1)} %get-tuple-element.21.kv, f32[2,2,64,16,128]{4,3,2,1,0:T(8,128)} %get-tuple-element.22.part_o, ...), custom_call_target="tpu_custom_call" | custom-call | flops 99999997952 | bytes 20971520 | tf_op jit(solution)/shard_map/out0/pallas_call | solution.py:359
  132.5 40.5 %mlp0.1 = (bf16[64,4096]{1,0:T(8,128)(2,1)}, bf16[4,64,1024]{2,1,0:T(8,128)(2,1)}) custom-call(bf16[64,4096]{1,0:T(8,128)(2,1)} %out0.1.h, bf16[64,1024]{1,0:T(8,128)(2,1)} %get-tuple-element.21.kv, bf16[2,4096,14336]{2,1,0:T(8,128)(2,1)} %w_up.3, bf16[2,14336,4096]{2,1,0:T(8,128)(2,1)} %w_down.3), custom_call_target="tpu_custom_call" | custom-call | flops 60129542144 | bytes 117440512 | tf_op jit(solution)/shard_map/mlp0/pallas_call | solution.py:473
  173.0 21.1 %qkv1.1 = (bf16[2,8,64,512]{3,2,1,0:T(8,128)(2,1)}, bf16[64,1024]{1,0:T(8,128)(2,1)}) custom-call(bf16[64,4096]{1,0:T(8,128)(2,1)} %get-tuple-element.24.refs_0_.h, bf16[2,4096,4096]{2,1,0:T(8,128)(2,1)} %refs_1_.3, bf16[2,4096,1024]{2,1,0:T(8,128)(2,1)} %refs_2_.3, bf16[2,4096,1024]{2,1,0:T(8,128)(2,1)} %refs_3_.3), custom_call_target="tpu_custom_call" | custom-call | flops 12884901888 | bytes 25165824 | tf_op jit(solution)/shard_map/qkv1/pallas_call | solution.py:128
  194.1 19.2 %attend1.1 = (f32[2,2,64,16,128]{4,3,2,1,0:T(8,128)}, f32[2,2,64,16,128]{4,3,2,1,0:T(8,128)}) custom-call(s32[1]{0:T(128)} %bitcast.count, s32[5,64]{1,0:T(8,128)} %select_reduce_fusion.table, bf16[2,8,64,512]{3,2,1,0:T(8,128)(2,1)} %get-tuple-element.25.q_all, bf16[96,2,256,128]{3,2,1,0:T(8,128)(2,1)} %bitcast.39, bf16[96,2,256,128]{3,2,1,0:T(8,128)(2,1)} %bitcast.41), custom_call_target="tpu_custom_call" | custom-call | flops 20000000000 | bytes 16777216 | tf_op jit(solution)/shard_map/attend1/pallas_call | solution.py:217
  213.3 45.6 %out1.1.h = bf16[64,4096]{1,0:T(8,128)(2,1)} custom-call(bf16[64,4096]{1,0:T(8,128)(2,1)} %get-tuple-element.24.refs_0_.h, bf16[2,8,64,512]{3,2,1,0:T(8,128)(2,1)} %get-tuple-element.25.q_all, bf16[64,1024]{1,0:T(8,128)(2,1)} %get-tuple-element.26.kv, f32[2,2,64,16,128]{4,3,2,1,0:T(8,128)} %get-tuple-element.27.part_o, ...), custom_call_target="tpu_custom_call" | custom-call | flops 99999997952 | bytes 20971520 | tf_op jit(solution)/shard_map/out1/pallas_call | solution.py:359
  258.9 0.4 reshape.257
  259.3 0.2 copy.26
  259.6 41.0 %mlp1.1 = (bf16[64,4096]{1,0:T(8,128)(2,1)}, bf16[4,64,1024]{2,1,0:T(8,128)(2,1)}) custom-call(bf16[64,4096]{1,0:T(8,128)(2,1)} %out1.1.h, bf16[64,1024]{1,0:T(8,128)(2,1)} %get-tuple-element.26.kv, bf16[2,4096,14336]{2,1,0:T(8,128)(2,1)} %w_up.3, bf16[2,14336,4096]{2,1,0:T(8,128)(2,1)} %w_down.3), custom_call_target="tpu_custom_call" | custom-call | flops 60129542144 | bytes 117440512 | tf_op jit(solution)/shard_map/mlp1/pallas_call | solution.py:473
  300.6 1.4 reshape.258
  302.6 0.6 stack.13.table
  303.2 1.1 fusion.2
  304.3 1.7 constant_dynamic-slice_fusion
  305.9 64.7 %all-reduce.3.cloned.1.call-done = (bf16[64,2,32,8,128]{4,3,2,1,0:T(8,128)(2,1)}, bf16[64,2,32,8,128]{4,3,2,1,0:T(8,128)(2,1)}) async-done(((bf16[64,2,32,8,128]{4,3,2,1,0:T(8,128)(2,1)}, bf16[64,2,32,8,128]{4,3,2,1,0:T(8,128)(2,1)}), (bf16[64,2,32,8,128]{4,3,2,1,0:T(8,128)(2,1)}, bf16[64,2,32,8,128]{4,3,2,1,0:T(8,128)(2,1)})) %all-reduce.3.cloned.1.call-update) | async-done | bytes 16777232 | tf_op jit(solution)/shard_map/psum | solution.py:629
  370.7 25.6 %pools.1 = (bf16[96,2,32,8,128]{4,3,2,1,0:T(8,128)(2,1)}, bf16[96,2,32,8,128]{4,3,2,1,0:T(8,128)(2,1)}) custom-call(s32[6,96]{1,0:T(8,128)} %stack.13.table, bf16[96,2,32,8,128]{4,3,2,1,0:T(8,128)(2,1)} %k_pool.1, bf16[96,2,32,8,128]{4,3,2,1,0:T(8,128)(2,1)} %v_pool.1, bf16[64,2,32,8,128]{4,3,2,1,0:T(8,128)(2,1)} %get-tuple-element.49.k_moved, ...), custom_call_target="tpu_custom_call" | custom-call | flops 20000000000 | bytes 52428800 | tf_op jit(solution)/shard_map/pools/pallas_call | solution.py:568
  (49 shorter events, 1.7 us)
Async XLA Ops:
  7.2 363.5 %all-reduce.3.cloned.1.call-start = ((), (), s32[]{:S(2)}) async-start(), calls=%async_computation | async-start | bytes 33554432 | tf_op jit(solution)/shard_map/psum | solution.py:629
  39.5 0.7 copy-start.5
  39.5 0.9 copy-start.1
  39.5 0.9 copy-start.3
  39.5 1.8 copy-start.11
  213.3 45.7 %copy-start = (bf16[4,64,1024]{2,1,0:T(8,128)(2,1)S(1)}, bf16[4,64,1024]{2,1,0:T(8,128)(2,1)}, u32[]{:S(2)}) copy-start(bf16[4,64,1024]{2,1,0:T(8,128)(2,1)} %get-tuple-element.30) | copy-start | bytes 1572868
  259.5 42.7 %copy-start.6 = (s32[64,2]{0,1:T(2,128)S(1)}, s32[64,2]{0,1:T(2,128)}, u32[]{:S(2)}) copy-start(s32[64,2]{0,1:T(2,128)} %param.24) | copy-start | bytes 1540
  259.5 42.7 %copy-start.7 = (s32[64]{0:T(128)S(1)}, s32[64]{0:T(128)}, u32[]{:S(2)}) copy-start(s32[64]{0:T(128)} %get-tuple-element.54) | copy-start | bytes 772
  259.5 42.7 %copy-start.8 = (s32[64]{0:T(128)S(1)}, s32[64]{0:T(128)}, u32[]{:S(2)}) copy-start(s32[64]{0:T(128)} %get-tuple-element.76) | copy-start | bytes 772
  259.5 42.7 %copy-start.2 = (s32[64]{0:T(128)S(1)}, s32[64]{0:T(128)}, u32[]{:S(2)}) copy-start(s32[64]{0:T(128)} %param.26) | copy-start | bytes 772
  259.6 42.7 %copy-start.4 = (s32[64]{0:T(128)S(1)}, s32[64]{0:T(128)}, u32[]{:S(2)}) copy-start(s32[64]{0:T(128)} %param.27) | copy-start | bytes 772
  259.6 42.8 %copy-start.9 = (s32[64]{0:T(128)S(1)}, s32[64]{0:T(128)}, u32[]{:S(2)}) copy-start(s32[64]{0:T(128)} %get-tuple-element.53) | copy-start | bytes 772
  259.6 42.8 %copy-start.10 = (s32[64]{0:T(128)S(1)}, s32[64]{0:T(128)}, u32[]{:S(2)}) copy-start(s32[64]{0:T(128)} %get-tuple-element.75) | copy-start | bytes 772
Sparse Core Ops, SparseCore 0:
  39.6 331.0 all-reduce.2

commit v2 on v1

v2 whole, which is shorter than its diff:
```python
import functools

import jax
import jax.numpy as jnp
from jax import lax
from jax.experimental import pallas as pl
from jax.experimental.pallas import tpu as pltpu
from jax.sharding import PartitionSpec as P

BF16 = jnp.bfloat16
F32 = jnp.float32
MESH = pl.DeviceIdType.MESH
NEG = -3.0e38
VMEM_LIMIT = 60 * 1024 * 1024

D = 4096
HEADS = 32
KV_HEADS = 8
HEAD = 128
FF = 14336
PAGE = 32
LAYERS = 2
SEQS = 64
MIG = 64
TOK = 64
HALF_HEADS = HEADS // 2
ROWS = TOK * HALF_HEADS
TN = 512
SCALE = HEAD ** -0.5
LOG2E = 1.4426950408889634
SLOTS = 96
UNROLL = 4
FAST_PAGES = 32
BOX = jax.ShapeDtypeStruct((3 * MIG, 2, PAGE * KV_HEADS, HEAD), BF16)


def flat_pool(pool):
    return pool.reshape(pool.shape[0], LAYERS, PAGE * KV_HEADS, HEAD)


def dot(a, b):
    return jnp.dot(a, b, preferred_element_type=F32)


def places():
    me = lax.axis_index('kv')
    core = lax.rem(me, 2)
    chip = me // 2
    partner = me + 1 - 2 * core
    across = lax.rem(me + 2, 4)
    diag = lax.rem(partner + 2, 4)
    return me, chip, core, partner, across, diag


def meet(peers):
    barrier = pltpu.get_barrier_semaphore()
    for peer in peers:
        pl.semaphore_signal(barrier, inc=1, device_id={'kv': peer}, device_id_type=MESH)
    pl.semaphore_wait(barrier, len(peers))


def send(src, dst, send_sem, recv_sem, peer):
    return pltpu.make_async_remote_copy(src_ref=src, dst_ref=dst, send_sem=send_sem, recv_sem=recv_sem, device_id={'kv': peer}, device_id_type=MESH)


VMEM = pl.BlockSpec(memory_space=pltpu.VMEM)
SMEM = pl.BlockSpec(memory_space=pltpu.SMEM)
ANY = pl.BlockSpec(memory_space=pl.ANY)
DMA = pltpu.SemaphoreType.DMA


WINDOW = 3


def qkv_kernel(layer, first, *refs):
    if first:
        emb, wq, wk, wv, q_all, kv, h, wbuf, wsem, psend, precv, xsend, xrecv, fsend, frecv, hsend, hrecv = refs
    else:
        h, wq, wk, wv, q_all, kv, wbuf, wsem, psend, precv, xsend, xrecv, fsend, frecv = refs
    me, chip, core, partner, across, diag = places()

    def fetch(j):
        if j < 4:
            src = wq.at[layer, :, pl.ds(pl.multiple_of(core * 2048 + j * TN, TN), TN)]
        else:
            src = (wk, wv)[j - 4].at[layer, :, pl.ds(pl.multiple_of(core * TN, TN), TN)]
        return pltpu.make_async_copy(src, wbuf.at[j], wsem.at[j])

    for j in range(WINDOW):
        fetch(j).start()
    meet((partner, across))
    if first:
        copies = []
        for t in range(2):
            rows = pl.ds(pl.multiple_of(t * 32 + core * 16, 16), 16)
            h[rows, :] = emb[t]
            copies.append(send(emb.at[t], h.at[rows, :], hsend.at[t], hrecv.at[t], partner))
        for copy in copies:
            copy.start()
        for copy in copies:
            copy.wait()

    def to_partner(j):
        ref = q_all.at[chip, core * 4 + j]
        return send(ref, ref, psend.at[j], precv.at[j], partner)

    def to_across(j):
        ref = q_all.at[chip, core * 4 + j]
        return send(ref, ref, xsend.at[j], xrecv.at[j], across)

    def forward(j):
        ref = q_all.at[1 - chip, core * 4 + j]
        return send(ref, ref, fsend.at[j], frecv.at[j], partner)

    def tile(j, carry):
        pltpu.make_async_copy(wq.at[layer, :, pl.ds(0, TN)], wbuf.at[j], wsem.at[j]).wait()
        q_all[chip, core * 4 + j] = dot(h[...], wbuf[j]).astype(BF16)
        for i in range(4):
            if i + WINDOW < 6:
                pl.when(j == i)(lambda i=i: fetch(i + WINDOW).start())

        @pl.when(j > 0)
        def _():
            to_across(j - 1).start()
            to_partner(j - 1).start()
        return carry

    lax.fori_loop(0, 4, tile, 0)
    for j in range(4, 6):
        fetch(j).wait()
        kv[:, (j - 4) * TN:(j - 3) * TN] = dot(h[...], wbuf[j]).astype(BF16)
        if j == 4:
            to_across(3).start()
            to_partner(3).start()
    for j in range(4):
        to_across(j).wait_recv()
        forward(j).start()
    for j in range(4):
        to_across(j).wait_send()
        to_partner(j).wait()
        forward(j).wait()


def run_qkv(layer, h, weights, first):
    wq, wk, wv = weights[:3]
    out_shape = [jax.ShapeDtypeStruct((2, 8, TOK, TN), BF16), jax.ShapeDtypeStruct((TOK, 2 * TN), BF16)]
    if first:
        out_shape.append(jax.ShapeDtypeStruct((TOK, D), BF16))
    scratch = [pltpu.VMEM((6, D, TN), BF16), DMA((6,))] + [DMA((4,))] * 6
    if first:
        scratch += [DMA((2,))] * 2
    return pl.pallas_call(
        functools.partial(qkv_kernel, layer, first),
        name=f'qkv{layer}',
        out_shape=out_shape,
        in_specs=[VMEM, ANY, ANY, ANY],
        out_specs=[VMEM] * len(out_shape),
        scratch_shapes=scratch,
        cost_estimate=pl.CostEstimate(flops=2 * TOK * D * 6 * TN * 8, bytes_accessed=D * 6 * TN * 2, transcendentals=0),
        compiler_params=pltpu.CompilerParams(collective_id=layer, has_side_effects=True, vmem_limit_bytes=VMEM_LIMIT),
    )(h, wq, wk, wv)


def plan_kernel(new_table, seq_lens, mig_src, mig_dst, meta, items, slots, moved, rows, source, place_of, counts):
    me = lax.axis_index('kv')
    base = me * SLOTS

    def home(slot):
        return sum((slot >= i * SLOTS).astype(jnp.int32) for i in range(1, 4))

    def clear(i, carry):
        source[i] = -1
        place_of[i] = -1
        return carry

    lax.fori_loop(0, 4 * SLOTS, clear, 0, unroll=16)
    for i in range(16):
        counts[i] = 0

    def keep(i, carry):
        slots[i] = 0
        return carry

    lax.fori_loop(0, SLOTS, keep, 0, unroll=16)

    def entry(e, carry):
        n, even, odd = carry
        s, d = mig_src[e], mig_dst[e]
        hs, hd = home(s), home(d)
        pair = hs * 4 + hd
        rank = counts[pair]
        counts[pair] = rank + 1
        channel = (hs ^ hd) - 1
        place = channel * MIG + rank
        source[d] = s
        place_of[d] = place
        misfit = ((channel == 1) | (rank >= FAST_PAGES)).astype(jnp.int32)
        even = even | misfit | (hs & 1)
        odd = odd | misfit | (1 - (hs & 1))

        @pl.when(hs == me)
        def _():
            slots[s - base] = 1

        @pl.when(hd == me)
        def _():
            slots[d - base] = 2
        moved[0, n] = d - base
        moved[1, n] = place
        return n + (hd == me).astype(jnp.int32), even, odd

    zero = jnp.int32(0)
    n_moved, even, odd = lax.fori_loop(0, MIG, entry, (zero, zero, zero), unroll=4)

    def sequence(b, carry):
        n, m = carry
        length = seq_lens[b]
        local, own, place = [], [], []
        for j in range(2):
            slot = new_table[j, b]
            src = source[slot]
            old = jnp.where(src >= 0, src, slot) - base
            mine = (old >= 0) & (old < SLOTS)
            local.append(old)
            own.append(mine)
            place.append(jnp.where(mine, place_of[slot], -1))
        items[0, n] = b
        items[1, n] = jnp.where(own[0], local[0], local[1])
        items[2, n] = jnp.where(own[1], local[1], local[0])
        items[3, n] = jnp.where(own[0], jnp.minimum(length, PAGE), 0)
        items[4, n] = jnp.where(own[1], jnp.maximum(length - PAGE, 0), 0)
        items[5, n] = place[0]
        items[6, n] = place[1]
        for t in range(2):
            pos = length + t
            second = pos >= PAGE
            here = jnp.where(second, new_table[1, b], new_table[0, b]) - base
            rows[0, m] = here
            rows[1, m] = jnp.where(second, pos - PAGE, pos)
            rows[2, m] = (b // 32) * TOK + t * 32 + b % 32
            m = m + ((here >= 0) & (here < SLOTS)).astype(jnp.int32)
        return n + (own[0] | own[1]).astype(jnp.int32), m

    n_items, n_rows = lax.fori_loop(0, SEQS, sequence, (zero, zero), unroll=4)

    @pl.when(n_items > 0)
    def _():
        for i in range(UNROLL - 1):
            for f in range(5):
                items[f, n_items + i] = items[f, n_items - 1]
            for f in range(5, 7):
                items[f, n_items + i] = -1
    meta[0] = n_items
    meta[1] = jnp.where(even == 0, 0, jnp.where(odd == 0, 1, 2))
    meta[2] = n_moved
    meta[3] = n_rows


def run_plan(new_table, seq_lens, mig_src, mig_dst):
    shapes = [(4,), (7, SEQS + UNROLL), (SLOTS,), (2, MIG + 1), (3, 2 * SEQS + 1)]
    return pl.pallas_call(
        plan_kernel,
        name='plan',
        out_shape=[jax.ShapeDtypeStruct(shape, jnp.int32) for shape in shapes],
        in_specs=[SMEM] * 4,
        out_specs=[SMEM] * len(shapes),
        scratch_shapes=[pltpu.SMEM((4 * SLOTS,), jnp.int32), pltpu.SMEM((4 * SLOTS,), jnp.int32), pltpu.SMEM((16,), jnp.int32)],
    )(new_table.T, seq_lens, mig_src, mig_dst)


NBUF = 3
STEPS = SEQS // UNROLL
SLOTS_STEP = SLOTS // STEPS


def attend_kernel(layer, meta, table, slots, q_all, k_pool, v_pool, part_o, part_l, outbox, pool_out, q_rows, kbuf, vbuf, ring, zeros, sems, out_sems, ring_in, ring_out):
    groups = (meta[0] + UNROLL - 1) // UNROLL
    pool = (k_pool, v_pool)[layer]

    def copies(g, start):
        slot = lax.rem(g, NBUF)
        for u in range(UNROLL):
            for j in range(2):
                page = table[1 + j, g * UNROLL + u]
                for ref, buf in ((k_pool, kbuf), (v_pool, vbuf)):
                    copy = pltpu.make_async_copy(ref.at[page, layer], buf.at[slot, u, j], sems.at[slot])
                    copy.start() if start else copy.wait()

    def packs(g, start):
        slot = lax.rem(g, NBUF)
        for u in range(UNROLL):
            for j in range(2):
                place = table[5 + j, g * UNROLL + u]

                @pl.when(place >= 0)
                def _():
                    for p, buf in enumerate((kbuf, vbuf)):
                        copy = pltpu.make_async_copy(buf.at[slot, u, j], outbox.at[place, p], out_sems.at[slot])
                        copy.start() if start else copy.wait()

    def keep(s, phase):
        place = lax.rem(s, NBUF)
        for i in range(SLOTS_STEP):
            slot = s * SLOTS_STEP + i
            state = slots[slot]


            def load():
                return pltpu.make_async_copy(pool.at[slot], ring.at[place, i], ring_in.at[place, i])

            def store():
                return pltpu.make_async_copy(ring.at[place, i], pool_out.at[slot], ring_out.at[place, i])

            if phase == 'load':
                pl.when(state == 0)(lambda: load().start())
            elif phase == 'store':
                @pl.when(state == 0)
                def _():
                    load().wait()
                    store().start()

                @pl.when(state == 1)
                def _():
                    pltpu.make_async_copy(zeros, pool_out.at[slot], ring_out.at[place, i]).start()
            else:
                pl.when(state < 2)(lambda: store().wait())

    for g in range(NBUF - 1):
        @pl.when(g < groups)
        def _():
            copies(g, True)
        keep(g, 'load')
    zeros[...] = jnp.zeros_like(zeros)
    part_o[...] = jnp.zeros_like(part_o)
    part_l[...] = jnp.full_like(part_l, NEG)

    for chip in range(2):
        for tile in range(8):
            for i in range(4):
                rows = q_all[chip, tile, :, i * HEAD:(i + 1) * HEAD].astype(F32)
                q_rows[pl.ds(chip * TOK * HEADS + tile * 4 + i, TOK, stride=HEADS), :] = rows

    row = lax.broadcasted_iota(jnp.int32, (2 * HEADS, 256), 0)
    col = lax.broadcasted_iota(jnp.int32, (2 * HEADS, 256), 1)
    pos = jnp.where((row % HEADS) // 4 == col % KV_HEADS, col // KV_HEADS, PAGE)

    def attend(g):
        slot = lax.rem(g, NBUF)
        outs = []
        for u in range(UNROLL):
            item = g * UNROLL + u
            seq = table[0, item]
            base = (seq // 32) * TOK * HEADS + (seq % 32) * HEADS
            q0 = q_rows[pl.ds(pl.multiple_of(base, HEADS), HEADS), :]
            q1 = q_rows[pl.ds(pl.multiple_of(base + 32 * HEADS, HEADS), HEADS), :]
            q = jnp.concatenate([q0, q1], axis=0).astype(BF16)
            scores = []
            for j in range(2):
                s = lax.dot_general(q, kbuf[slot, u, j], (((1,), (1,)), ((), ())), preferred_element_type=F32)
                scores.append(jnp.where(pos < table[3 + j, item], s, NEG))
            top = jnp.max(jnp.maximum(scores[0], scores[1]), axis=1, keepdims=True)
            probs = [jnp.exp2((s - top) * (SCALE * LOG2E)) for s in scores]
            total = jnp.sum(probs[0] + probs[1], axis=1, keepdims=True)
            out = sum(dot(p.astype(BF16), vbuf[slot, u, j]) for j, p in enumerate(probs))
            live = top > NEG
            lse = jnp.where(live, top * SCALE + jnp.log(total), NEG)
            outs.append((seq, jnp.where(live, out / total, 0.0), jnp.broadcast_to(lse, (2 * HEADS, HEAD))))
        for seq, out, lse in outs:
            for t in range(2):
                for half in range(2):
                    rows = slice(t * HEADS + half * HALF_HEADS, t * HEADS + (half + 1) * HALF_HEADS)
                    part_o[seq // 32, half, t * 32 + seq % 32] = out[rows]
                    part_l[seq // 32, half, t * 32 + seq % 32] = lse[rows]

    def step(g, carry):
        keep(g, 'store')

        @pl.when(g < groups)
        def _():
            copies(g, False)
            packs(g, True)

        @pl.when(g > 0)
        def _():
            keep(g - 1, 'drain')

        @pl.when((g > 0) & (g <= groups))
        def _():
            packs(g - 1, False)

        @pl.when(g + NBUF - 1 < STEPS)
        def _():
            keep(g + NBUF - 1, 'load')

        @pl.when(g + NBUF - 1 < groups)
        def _():
            copies(g + NBUF - 1, True)

        @pl.when(g < groups)
        def _():
            attend(g)
        return carry

    lax.fori_loop(0, STEPS, step, 0)
    keep(STEPS - 1, 'drain')

    @pl.when(groups == STEPS)
    def _():
        packs(groups - 1, False)


def run_attend(layer, meta, table, slots, q_all, k_flat, v_flat):
    shape = jax.ShapeDtypeStruct((2, 2, TOK, HALF_HEADS, HEAD), F32)
    page = (UNROLL, 2, PAGE * KV_HEADS, HEAD)
    return pl.pallas_call(
        functools.partial(attend_kernel, layer),
        name=f'attend{layer}',
        out_shape=[shape, shape, BOX, jax.ShapeDtypeStruct(k_flat.shape, BF16)],
        in_specs=[SMEM, SMEM, SMEM, VMEM, ANY, ANY],
        out_specs=[VMEM, VMEM, ANY, ANY],
        scratch_shapes=[
            pltpu.VMEM((2 * TOK * HEADS, HEAD), F32),
            pltpu.VMEM((NBUF,) + page, BF16),
            pltpu.VMEM((NBUF,) + page, BF16),
            pltpu.VMEM((NBUF, SLOTS_STEP) + k_flat.shape[1:], BF16),
            pltpu.VMEM(k_flat.shape[1:], BF16),
            DMA((NBUF,)),
            DMA((NBUF,)),
            DMA((NBUF, SLOTS_STEP)),
            DMA((NBUF, SLOTS_STEP)),
        ],
        cost_estimate=pl.CostEstimate(flops=2 * 10 ** 10, bytes_accessed=16 * 2 ** 20, transcendentals=0),
        compiler_params=pltpu.CompilerParams(vmem_limit_bytes=VMEM_LIMIT),
    )(meta, table, slots, q_all, k_flat, v_flat)


def merge(parts):
    top = functools.reduce(jnp.maximum, [l for _, l in parts])
    weights = [jnp.exp(l - top) for _, l in parts]
    total = functools.reduce(jnp.add, weights)
    out = functools.reduce(jnp.add, [w * o for w, (o, _) in zip(weights, parts)]) / total
    return out, top + jnp.log(total)


EARLY = 6
MODES = tuple(
    ([((core,), 2, 0, EARLY)], [((core,), 2, EARLY, FAST_PAGES), ((core,), 0, 0, FAST_PAGES)]) for core in range(2)
) + (([], [((0, 1), channel, 0, MIG) for channel in range(3)]),)
CHUNK = 2


class Boxes:
    def __init__(self, moves, outbox, inbox, send_sems, recv_sems):
        me, chip, self.core, partner, across, diag = places()
        self.peers = (partner, across, diag)
        self.moves, self.outbox, self.inbox, self.send_sems, self.recv_sems = moves, outbox, inbox, send_sems, recv_sems

    def each(self, sending, act):
        for cores, channel, first, end in self.moves:
            def run(cores=cores, channel=channel, first=first, end=end):
                def one(i, carry):
                    rows = pl.ds(channel * MIG + i * CHUNK, CHUNK)
                    act(send(self.outbox.at[rows], self.inbox.at[rows], self.send_sems.at[channel, i], self.recv_sems.at[channel, i], self.peers[channel]))
                    return carry

                lax.fori_loop(first // CHUNK, end // CHUNK, one, 0)

            if len(cores) == 2:
                run()
            else:
                cross = 0 if channel == 1 else 1
                at = cores[0] if sending else (cores[0] + cross) % 2
                pl.when(self.core == at)(run)

    def start(self):
        self.each(True, lambda copy: copy.start())

    def wait(self):
        self.each(True, lambda copy: copy.wait_send())
        self.each(False, lambda copy: copy.wait_recv())


def out_kernel(layer, mode, h, q_all, kv, part_o, part_l, wo, outbox, out, inbox, wbuf, wsem, got_o, got_l, mine_o, mine_l, give_o, give_l, far_o, far_l,
               q_rows, k_rows, v_rows, attn, psend, precv, dsend, drecv, xsend, xrecv, ssem, rsem, bsend, brecv):
    boxes = Boxes(MODES[mode][0], outbox, inbox, bsend, brecv)
    me, chip, core, partner, across, diag = places()

    def fetch(j):
        src = wo.at[layer, pl.ds(pl.multiple_of(core * 2048, 2048), 2048), pl.ds(j * TN, TN)]
        return pltpu.make_async_copy(src, wbuf.at[j], wsem.at[j])

    for j in range(8):
        fetch(j).start()
    meet((partner, across, diag))

    near = []
    for which in range(2):
        owner = 1 - chip if which == 0 else chip
        pair = [
            send(part_o.at[owner, 1 - core], got_o.at[which], dsend.at[which, 0], drecv.at[which, 0], partner),
            send(part_l.at[owner, 1 - core], got_l.at[which], dsend.at[which, 1], drecv.at[which, 1], partner),
        ]
        for copy in pair:
            copy.start()
        near.append(pair)

    lane = lax.broadcasted_iota(jnp.int32, (8, HEAD), 1)

    for copy in near[0]:
        copy.wait_recv()

    def chip_merge(i, compact):
        o, l = merge([(part_o[1 - chip, core, i], part_l[1 - chip, core, i]), (got_o[0, i], got_l[0, i])])
        give_o[i] = o
        compact = jnp.where(lane == 2 * i, l[:8], compact)
        return jnp.where(lane == 2 * i + 1, l[8:], compact)

    compact = lax.fori_loop(0, TOK, chip_merge, jnp.zeros((8, HEAD), F32), unroll=8)
    give_l[...] = compact
    far = [
        send(give_l, far_l, xsend.at[0], xrecv.at[0], across),
        send(give_o, far_o, xsend.at[1], xrecv.at[1], across),
    ]
    for copy in far:
        copy.start()

    for head in range(HALF_HEADS):
        tile = core * 4 + head // 4
        rows = pl.ds(head, TOK, stride=HALF_HEADS)
        q_rows[rows, :] = q_all[chip, tile, :, (head % 4) * HEAD:(head % 4 + 1) * HEAD].astype(F32)
        k_rows[rows, :] = kv[:, (head // 4) * HEAD:(head // 4 + 1) * HEAD].astype(F32)
        v_rows[rows, :] = kv[:, TN + (head // 4) * HEAD:TN + (head // 4 + 1) * HEAD].astype(F32)
    for copy in near[1]:
        copy.wait_recv()

    half = ROWS // 2

    def score(q, k):
        s = jnp.sum(q * k, axis=1, keepdims=True) * SCALE
        return jnp.broadcast_to(s, q.shape)

    def own(i, carry):
        a = pl.ds(pl.multiple_of(i * HALF_HEADS, HALF_HEADS), HALF_HEADS)
        b = pl.ds(pl.multiple_of(half + i * HALF_HEADS, HALF_HEADS), HALF_HEADS)
        k0, v0, k1, v1 = k_rows[a, :], v_rows[a, :], k_rows[b, :], v_rows[b, :]
        q0, q1 = q_rows[a, :], q_rows[b, :]
        j = i + TOK // 2
        o, l = merge([(part_o[chip, core, i], part_l[chip, core, i]), (got_o[1, i], got_l[1, i]), (v0, score(q0, k0))])
        mine_o[i] = o
        mine_l[i] = l
        o, l = merge([(part_o[chip, core, j], part_l[chip, core, j]), (got_o[1, j], got_l[1, j]), (v0, score(q1, k0)), (v1, score(q1, k1))])
        mine_o[j] = o
        mine_l[j] = l
        return carry

    lax.fori_loop(0, TOK // 2, own, 0, unroll=4)

    for copy in far:
        copy.wait_recv()
    boxes.start()
    spread = far_l[...]

    def last_merge(i, carry):
        l = jnp.concatenate([
            jnp.broadcast_to(jnp.sum(jnp.where(lane == 2 * i + k, spread, 0.0), axis=1, keepdims=True), (8, HEAD)) for k in range(2)
        ], axis=0)
        o, _ = merge([(mine_o[i], mine_l[i]), (far_o[i], l)])
        q_rows[pl.ds(pl.multiple_of(i * HALF_HEADS, HALF_HEADS), HALF_HEADS), :] = o
        return carry

    lax.fori_loop(0, TOK, last_merge, 0, unroll=8)
    for head in range(HALF_HEADS):
        attn[:, head * HEAD:(head + 1) * HEAD] = q_rows[pl.ds(head, TOK, stride=HALF_HEADS), :].astype(BF16)

    def reduce(j):
        return send(psend.at[j], precv.at[j], ssem.at[j], rsem.at[j], partner)

    def project(j, carry):
        pltpu.make_async_copy(wo.at[layer, pl.ds(0, 2048), pl.ds(0, TN)], wbuf.at[j], wsem.at[j]).wait()
        psend[j] = dot(attn[...], wbuf[j])

        @pl.when(j > 0)
        def _():
            reduce(j - 1).start()
        return carry

    lax.fori_loop(0, 8, project, 0)
    reduce(7).start()
    for j in range(8):
        reduce(j).wait_recv()
        cols = slice(j * TN, (j + 1) * TN)
        out[:, cols] = (h[:, cols].astype(F32) + (psend[j] + precv[j])).astype(BF16)
    for j in range(8):
        reduce(j).wait_send()
    for pair in near:
        for copy in pair:
            copy.wait_send()
    for copy in far:
        copy.wait_send()
    boxes.wait()


def run_out(layer, mode, h, q_all, kv, part_o, part_l, w_out, outbox):
    token = (TOK, HALF_HEADS, HEAD)
    return pl.pallas_call(
        functools.partial(out_kernel, layer, mode),
        name=f'out{layer}_{mode}',
        out_shape=[jax.ShapeDtypeStruct((TOK, D), BF16), BOX],
        in_specs=[VMEM] * 5 + [ANY, ANY],
        out_specs=[VMEM, ANY],
        scratch_shapes=[
            pltpu.VMEM((8, 2048, TN), BF16),
            DMA((8,)),
            pltpu.VMEM((2,) + token, F32),
            pltpu.VMEM((2,) + token, F32),
            pltpu.VMEM(token, F32),
            pltpu.VMEM(token, F32),
            pltpu.VMEM(token, F32),
            pltpu.VMEM((8, HEAD), F32),
            pltpu.VMEM(token, F32),
            pltpu.VMEM((8, HEAD), F32),
            pltpu.VMEM((ROWS, HEAD), F32),
            pltpu.VMEM((ROWS, HEAD), F32),
            pltpu.VMEM((ROWS, HEAD), F32),
            pltpu.VMEM((TOK, 2048), BF16),
            pltpu.VMEM((8, TOK, TN), F32),
            pltpu.VMEM((8, TOK, TN), F32),
            DMA((2, 2)),
            DMA((2, 2)),
            DMA((2,)),
            DMA((2,)),
            DMA((8,)),
            DMA((8,)),
            DMA((3, MIG // CHUNK)),
            DMA((3, MIG // CHUNK)),
        ],
        cost_estimate=pl.CostEstimate(flops=10 ** 11, bytes_accessed=20 * 2 ** 20, transcendentals=0),
        compiler_params=pltpu.CompilerParams(collective_id=2 + layer * 3 + mode, has_side_effects=True, vmem_limit_bytes=VMEM_LIMIT),
    )(h, q_all, kv, part_o, part_l, w_out, outbox)


NU = 4
ND = 4
UP_TILES = FF // 2 // TN
KROWS = FF // 4
DOWN_TILES = 2 * (D // TN)


def mlp_kernel(layer, mode, h, kv, w_up, w_down, outbox, inbox_in, out, kv_all, inbox, ubuf, dbuf, act, psend, precv, usem, dsem, ssem, rsem, ksend, krecv, bsend, brecv):
    me, chip, core, partner, across, diag = places()
    boxes = Boxes(MODES[mode][1], outbox, inbox, bsend, brecv)

    def fetch_up(s):
        src = w_up.at[layer, :, pl.ds(pl.multiple_of(core * (FF // 2) + s * TN, TN), TN)]
        slot = lax.rem(s, NU)
        return pltpu.make_async_copy(src, ubuf.at[slot], usem.at[slot])

    def fetch_down(s):
        src = w_down.at[layer, pl.ds(pl.multiple_of(core * (FF // 2) + lax.rem(s, 2) * KROWS, KROWS), KROWS), pl.ds(pl.multiple_of((s // 2) * TN, TN), TN)]
        slot = lax.rem(s, ND)
        return pltpu.make_async_copy(src, dbuf.at[slot], dsem.at[slot])

    for s in range(NU):
        fetch_up(jnp.int32(s)).start()
    meet((partner, across, diag))
    kv_all[me] = kv[...]
    rows = [send(kv, kv_all.at[me], ksend.at[i], krecv.at[i], peer) for i, peer in enumerate((partner, across))]
    rows.append(send(kv_all.at[across], kv_all.at[across], ksend.at[2], krecv.at[2], partner))
    for copy in rows[:2]:
        copy.start()
    boxes.start()

    def up(s, carry):
        fetch_up(s).wait()
        u = dot(h[...], ubuf[lax.rem(s, NU)]).astype(BF16)
        a = jax.nn.gelu(u.astype(F32), approximate=True).astype(BF16)
        act[s // 7, :, pl.ds(pl.multiple_of(lax.rem(s, 7) * TN, TN), TN)] = a

        @pl.when(s + NU < UP_TILES)
        def _():
            fetch_up(s + NU).start()

        @pl.when(s + NU >= UP_TILES)
        def _():
            fetch_down(s + NU - UP_TILES).start()
        return carry

    lax.fori_loop(0, UP_TILES, up, 0)
    rows[1].wait_recv()
    rows[2].start()

    def reduce(j):
        return send(psend.at[j], precv.at[j], ssem.at[j], rsem.at[j], partner)

    def down(j, carry):
        total = None
        for k in range(2):
            s = 2 * j + k
            fetch_down(s).wait()
            part = dot(act[k], dbuf[lax.rem(s, ND)])
            total = part if total is None else total + part

            @pl.when(s + ND < DOWN_TILES)
            def _():
                fetch_down(s + ND).start()
        psend[j] = total

        @pl.when(j > 0)
        def _():
            reduce(j - 1).start()
        return carry

    lax.fori_loop(0, 8, down, 0)
    reduce(7).start()
    for j in range(8):
        reduce(j).wait_recv()
        cols = slice(j * TN, (j + 1) * TN)
        out[:, cols] = (h[:, cols].astype(F32) + (psend[j] + precv[j])).astype(BF16)
    for j in range(8):
        reduce(j).wait_send()
    rows[0].wait()
    rows[1].wait_send()
    rows[2].wait()
    boxes.wait()


def run_mlp(layer, mode, h, kv, w_up, w_down, outbox, inbox):
    return pl.pallas_call(
        functools.partial(mlp_kernel, layer, mode),
        name=f'mlp{layer}_{mode}',
        out_shape=[jax.ShapeDtypeStruct((TOK, D), BF16), jax.ShapeDtypeStruct((4, TOK, 2 * TN), BF16), BOX],
        in_specs=[VMEM, VMEM, ANY, ANY, ANY, ANY],
        out_specs=[VMEM, VMEM, ANY],
        input_output_aliases={5: 2},
        scratch_shapes=[
            pltpu.VMEM((NU, D, TN), BF16),
            pltpu.VMEM((ND, KROWS, TN), BF16),
            pltpu.VMEM((2, TOK, KROWS), BF16),
            pltpu.VMEM((8, TOK, TN), F32),
            pltpu.VMEM((8, TOK, TN), F32),
            DMA((NU,)),
            DMA((ND,)),
            DMA((8,)),
            DMA((8,)),
            DMA((3,)),
            DMA((3,)),
            DMA((3, MIG // CHUNK)),
            DMA((3, MIG // CHUNK)),
        ],
        cost_estimate=pl.CostEstimate(flops=2 * TOK * D * FF * 8, bytes_accessed=D * FF * 2, transcendentals=0),
        compiler_params=pltpu.CompilerParams(collective_id=8 + layer * 3 + mode, has_side_effects=True, vmem_limit_bytes=VMEM_LIMIT),
    )(h, kv, w_up, w_down, outbox, inbox)


RING = 16
AHEAD = RING // 2


def finish_kernel(meta, moved, rows, inbox0, inbox1, k_rows, v_rows, k_in, v_in, k_out, v_out, buf, in_sem, out_sem, row_sem):
    del k_in, v_in
    inboxes = (inbox0, inbox1)
    outs = (k_out, v_out)
    count = meta[2]

    def load(i):
        slot = lax.rem(i, RING)
        return [pltpu.make_async_copy(inboxes[l].at[moved[1, i], p], buf.at[slot, p, l], in_sem.at[slot, p, l]) for p in range(2) for l in range(LAYERS)]

    def store(i):
        slot = lax.rem(i, RING)
        return [pltpu.make_async_copy(buf.at[slot, p], outs[p].at[moved[0, i]], out_sem.at[slot, p]) for p in range(2)]

    def begin(group):
        for copy in group:
            copy.start()

    def end(group):
        for copy in group:
            copy.wait()

    def loop(first, last, body):
        lax.fori_loop(first, last, lambda i, carry: (body(i), carry)[1], 0)

    loop(0, jnp.minimum(count, AHEAD), lambda i: begin(load(i)))

    def page(i):
        end(load(i))
        begin(store(i))

        @pl.when(i + AHEAD < count)
        def _():
            @pl.when(i >= AHEAD)
            def _():
                end(store(i - AHEAD))
            begin(load(i + AHEAD))

    loop(0, count, page)
    loop(jnp.maximum(count - RING, 0), count, lambda i: end(store(i)))

    def row(i):
        at = pl.ds(pl.multiple_of(rows[1, i] * KV_HEADS, KV_HEADS), KV_HEADS)
        return [pltpu.make_async_copy(src.at[l, rows[2, i]], outs[p].at[rows[0, i], l, at, :], row_sem.at[p, l]) for p, src in enumerate((k_rows, v_rows)) for l in range(LAYERS)]

    loop(0, meta[3], lambda i: begin(row(i)))
    loop(0, meta[3], lambda i: end(row(i)))


def run_finish(meta, moved, rows, inboxes, k_rows, v_rows, k_part, v_part):
    shape = jax.ShapeDtypeStruct(k_part.shape, BF16)
    return pl.pallas_call(
        finish_kernel,
        name='finish',
        out_shape=[shape, shape],
        in_specs=[SMEM, SMEM, SMEM, ANY, ANY, VMEM, VMEM, ANY, ANY],
        out_specs=[ANY, ANY],
        scratch_shapes=[
            pltpu.VMEM((RING, 2) + k_part.shape[1:], BF16),
            DMA((RING, 2, LAYERS)),
            DMA((RING, 2)),
            DMA((2, LAYERS)),
        ],
        input_output_aliases={7: 0, 8: 1},
        cost_estimate=pl.CostEstimate(flops=10 ** 10, bytes_accessed=16 * 2 ** 20, transcendentals=0),
        compiler_params=pltpu.CompilerParams(vmem_limit_bytes=VMEM_LIMIT),
    )(meta, moved, rows, *inboxes, k_rows, v_rows, k_part, v_part)


def by_token(kv_all):
    x = kv_all.reshape(2, 2, TOK, 2, 4, HEAD)
    return x.transpose(3, 0, 2, 1, 4, 5).reshape(2, 2 * TOK, KV_HEADS, HEAD)


def solution(mesh):
    pool_spec = P(('rep', 'kv'))
    tok_spec = P(None, ('rep', 'kv'), None)

    def device_fn(embeds, w_query, w_key, w_value, w_out, w_up, w_down, k_pool, v_pool, new_table, seq_lens, mig_src, mig_dst):
        me = lax.axis_index('kv')
        weights = (w_query, w_key, w_value)
        k_flat, v_flat = flat_pool(k_pool), flat_pool(v_pool)
        meta, items, slots, moved, where = run_plan(new_table, seq_lens, mig_src, mig_dst)
        rows, inboxes, pools = [], [], []
        h = None
        for layer in range(LAYERS):
            if layer == 0:
                q_all, kv, h = run_qkv(layer, embeds, weights, True)
            else:
                q_all, kv = run_qkv(layer, h, weights, False)
            part_o, part_l, outbox, pool = run_attend(layer, meta, items, slots, q_all, k_flat, v_flat)

            def rest(mode, h, q_all, kv, part_o, part_l, outbox, w_out, w_up, w_down, layer=layer):
                h, inbox = run_out(layer, mode, h, q_all, kv, part_o, part_l, w_out, outbox)
                return run_mlp(layer, mode, h, kv, w_up, w_down, outbox, inbox)

            forms = [functools.partial(rest, mode) for mode in range(len(MODES))]
            h, kv_all, inbox = lax.switch(meta[1], forms, h, q_all, kv, part_o, part_l, outbox, w_out, w_up, w_down)
            inboxes.append(inbox)
            rows.append(by_token(kv_all))
            pools.append(pool)
        rows = jnp.stack(rows)
        k_out, v_out = run_finish(meta, moved, where, inboxes, rows[:, 0], rows[:, 1], *pools)
        k_out, v_out = k_out.reshape(k_pool.shape), v_out.reshape(v_pool.shape)
        y = lax.dynamic_slice_in_dim(h.reshape(2, 32, D), (me % 2) * 16, 16, axis=1)
        return y, k_out, v_out

    return jax.shard_map(device_fn, mesh=mesh, in_specs=(tok_spec, P(), P(), P(), P(), P(), P(), pool_spec, pool_spec, P('rep', None), P('rep'), P('rep'), P('rep')), out_specs=(tok_spec, pool_spec, pool_spec), check_vma=False)
```

time: 404 us -> 264 us (0.65)
  waiting for transfers between devices: 64.8 us -> 0 us
  Pallas kernels: 281 us -> 256 us
  local copies, waits for them, and re-layouts: 25.8 us -> 3.49 us
  other arithmetic: 16.2 us -> 1.08 us
  between operations: 15.1 us -> 1.39 us
    psum x1 -> x0, waiting for transfers between devices: 64.7 us -> none  [moved_pages(): return lax.psum((k_pages, v_pages), 'kv')]
    gather x2 -> x0, local copies, waits for them, and re-layouts: 20 us -> none  [the longest x1 10 us: moved_pages(): v_pages = jnp.take(v_pool, local, axis=0, mode='fill', fill_value=0)]
    pallas_call x2, Pallas kernels: 44.9 us -> 29.3 us  [run_qkv(): pl.pallas_call(functools.partial(qkv_kernel, layer, first), name=f'qkv{la...]
    select_n x5 -> x0, other arithmetic: 11.8 us -> none  [the longest x1 11.6 us: moved_pages(): v_pages = jnp.take(v_pool, local, axis=0, mode='fill', fill_value=0)]
    pallas_call x2, Pallas kernels: 38.2 us -> 30.3 us  [run_attend(): pl.pallas_call(functools.partial(attend_kernel, layer), name=f'attend{lay...]
    pallas_call x5 -> x6, Pallas kernels: 198 us -> 196 us  [the longest x2 92.6 us: run_mlp(): pl.pallas_call(functools.partial(mlp_kernel, layer, mode), name=f'mlp{lay...]
  transfers between devices with their start and end apart: 1 -> 0, of which waited for: 1 -> 0; matrix products, arithmetic and copies ran while one was open for 2% -> 0% of each run, Pallas kernels for 63% -> 0%
where the time goes in v2:
time: 264 us; the launch traced here: 263 us
  Pallas kernels  256 us (97%)
  local copies, waits for them, and re-layouts  3.49 us (1%)
    pallas_call x2, Pallas kernels, run_mlp(): pl.pallas_call(functools.partial(mlp_kernel, layer, mode), name=f'mlp{lay...  92.6 us
    pallas_call x2, Pallas kernels, run_out(): pl.pallas_call(functools.partial(out_kernel, layer, mode), name=f'out{lay...  87.8 us
    pallas_call x2, Pallas kernels, run_attend(): pl.pallas_call(functools.partial(attend_kernel, layer), name=f'attend{lay...  30.3 us
    pallas_call x2, Pallas kernels, run_qkv(): pl.pallas_call(functools.partial(qkv_kernel, layer, first), name=f'qkv{la...  29.3 us
    pallas_call x1, Pallas kernels, run_finish(): pl.pallas_call(finish_kernel, name='finish', out_shape=[shape, shape], in...  10.2 us
    pallas_call x1, Pallas kernels, run_plan(): pl.pallas_call(plan_kernel, name='plan', out_shape=[jax.ShapeDtypeStruct(...  5.63 us

profile of v2, /device:TPU:0, one launch (start us, length us, event | category | flops | bytes accessed | tf_op | source)
XLA Modules:
  0.0 262.8 jit_solution(9348044154768783252)
XLA Ops:
  0.6 5.6 %plan.1 = (s32[4]{0:T(128)}, s32[7,68]{1,0:T(8,128)}, s32[96]{0:T(128)}, s32[2,65]{1,0:T(2,128)}, s32[3,129]{1,0:T(4,128)}) custom-call(s32[2,64]{1,0:T(2,128)} %bitcast.22, s32[64]{0:T(128)} %seq_lens.1, s32[64]{0:T(128)} %mig_src.1, s32[64]{0:T(128)} %mig_dst.1), custom_call_target="tpu_custom_call" | custom-call | tf_op jit(solution)/shard_map/plan/pallas_call | solution.py:261
  6.3 16.3 %qkv0.1 = (bf16[2,8,64,512]{3,2,1,0:T(8,128)(2,1)S(1)}, bf16[64,1024]{1,0:T(8,128)(2,1)S(1)}, bf16[64,4096]{1,0:T(8,128)(2,1)S(1)}) custom-call(bf16[2,16,4096]{2,1,0:T(8,128)(2,1)} %refs_0_.1, bf16[2,4096,4096]{2,1,0:T(8,128)(2,1)} %refs_1_.3, bf16[2,4096,1024]{2,1,0:T(8,128)(2,1)} %refs_2_.3, bf16[2,4096,1024]{2,1,0:T(8,128)(2,1)} %refs_3_.3), custom_call_target="tpu_custom_call" | custom-call | flops 12884901888 | bytes 25165824 | tf_op jit(solution)/shard_map/qkv0/pallas_call | solution.py:152
  22.5 0.0 copy-start.2
  22.6 15.2 %attend0.1 = (f32[2,2,64,16,128]{4,3,2,1,0:T(8,128)}, f32[2,2,64,16,128]{4,3,2,1,0:T(8,128)}, bf16[192,2,256,128]{3,2,1,0:T(8,128)(2,1)}, bf16[96,2,256,128]{3,2,1,0:T(8,128)(2,1)}) custom-call(s32[4]{0:T(128)} %get-tuple-element.217.meta, s32[7,68]{1,0:T(8,128)} %get-tuple-element.221.table, s32[96]{0:T(128)} %get-tuple-element.222.slots, ...), custom_call_target="tpu_custom_call" | custom-call | flops 20000000000 | bytes 16777216 | tf_op jit(solution)/shard_map/attend0/pallas_call | solution.py:415
  37.7 0.0 copy-done.2
  37.8 0.6 slice.10
  39.0 90.5 %conditional.2 = ((bf16[64,4096]{1,0:T(8,128)(2,1)S(1)}, bf16[4,64,1024]{2,1,0:T(8,128)(2,1)}, bf16[192,2,256,128]{3,2,1,0:T(8,128)(2,1)})) conditional(s32[]{:T(128)} %bitcast.1, (bf16[64,4096]{1,0:T(8,128)(2,1)S(1)}, bf16[2,8,64,512]{3,2,1,0:T(8,128)(2,1)S(1)}, bf16[64,1024]{1,0:T(8,128)(2,1)S(1)}, ...), branch_computations={%region_0.0_spmd, %region_1.0_spmd, %region_2.0_spmd} | conditional | flops 160129548288 | bytes 138412032 | solution.py:856
  39.0 43.8 %out0_1.1 = (bf16[64,4096]{1,0:T(8,128)(2,1)}, bf16[192,2,256,128]{3,2,1,0:T(8,128)(2,1)}) custom-call(bf16[64,4096]{1,0:T(8,128)(2,1)S(1)} %get-tuple-element.133.h, bf16[2,8,64,512]{3,2,1,0:T(8,128)(2,1)S(1)} %get-tuple-element.134.q_all, bf16[64,1024]{1,0:T(8,128)(2,1)S(1)} %get-tuple-element.135.kv, f32[2,2,64,16,128]{4,3,2,1,0:T(8,128)} %get-tuple-element.136.part_o, ...), custom_call_target="tpu_custom_call" | custom-call | flops 99999997952 | bytes 20971520 | tf_op jit(solution)/shard_map/cond/branch_1_fun/out0_1/pallas_call | solution.py:605
  82.8 46.2 %mlp0_1.1 = (bf16[64,4096]{1,0:T(8,128)(2,1)S(1)}, bf16[4,64,1024]{2,1,0:T(8,128)(2,1)}, bf16[192,2,256,128]{3,2,1,0:T(8,128)(2,1)}) custom-call(bf16[64,4096]{1,0:T(8,128)(2,1)} %get-tuple-element.140.h, bf16[64,1024]{1,0:T(8,128)(2,1)S(1)} %get-tuple-element.135.kv, ...), custom_call_target="tpu_custom_call", output_to_operand_aliasing={{2}: (5, {})} | custom-call | flops 60129542144 | bytes 117440512 | tf_op jit(solution)/shard_map/cond/branch_1_fun/mlp0_1/pallas_call | solution.py:728
  129.5 13.1 %qkv1.1 = (bf16[2,8,64,512]{3,2,1,0:T(8,128)(2,1)S(1)}, bf16[64,1024]{1,0:T(8,128)(2,1)S(1)}) custom-call(bf16[64,4096]{1,0:T(8,128)(2,1)S(1)} %get-tuple-element.226.refs_0_, bf16[2,4096,4096]{2,1,0:T(8,128)(2,1)} %refs_1_.3, bf16[2,4096,1024]{2,1,0:T(8,128)(2,1)} %refs_2_.3, bf16[2,4096,1024]{2,1,0:T(8,128)(2,1)} %refs_3_.3), custom_call_target="tpu_custom_call" | custom-call | flops 12884901888 | bytes 25165824 | tf_op jit(solution)/shard_map/qkv1/pallas_call | solution.py:152
  142.6 15.1 %attend1.1 = (f32[2,2,64,16,128]{4,3,2,1,0:T(8,128)}, f32[2,2,64,16,128]{4,3,2,1,0:T(8,128)}, bf16[192,2,256,128]{3,2,1,0:T(8,128)(2,1)}, bf16[96,2,256,128]{3,2,1,0:T(8,128)(2,1)}) custom-call(s32[4]{0:T(128)} %get-tuple-element.217.meta, s32[7,68]{1,0:T(8,128)} %get-tuple-element.221.table, s32[96]{0:T(128)} %get-tuple-element.222.slots, ...), custom_call_target="tpu_custom_call" | custom-call | flops 20000000000 | bytes 16777216 | tf_op jit(solution)/shard_map/attend1/pallas_call | solution.py:415
  157.7 0.0 copy-start
  157.7 90.9 %conditional.3 = ((bf16[64,4096]{1,0:T(8,128)(2,1)}, bf16[4,64,1024]{2,1,0:T(8,128)(2,1)}, bf16[192,2,256,128]{3,2,1,0:T(8,128)(2,1)})) conditional(s32[]{:T(128)} %bitcast.1, (bf16[64,4096]{1,0:T(8,128)(2,1)S(1)}, bf16[2,8,64,512]{3,2,1,0:T(8,128)(2,1)S(1)}, bf16[64,1024]{1,0:T(8,128)(2,1)S(1)}, f32[2,2,64,16,128]{4,3,2,1,0:T(8,128)}, ...), branch_computations={%region_3.0_spmd, %region_4.0_spmd, %region_5.0_spmd} | conditional | flops 160129548288 | bytes 138412032 | solution.py:856
  157.7 44.0 %out1_1.1 = (bf16[64,4096]{1,0:T(8,128)(2,1)}, bf16[192,2,256,128]{3,2,1,0:T(8,128)(2,1)}) custom-call(bf16[64,4096]{1,0:T(8,128)(2,1)S(1)} %get-tuple-element.166.h, bf16[2,8,64,512]{3,2,1,0:T(8,128)(2,1)S(1)} %get-tuple-element.167.q_all, bf16[64,1024]{1,0:T(8,128)(2,1)S(1)} %get-tuple-element.168.kv, f32[2,2,64,16,128]{4,3,2,1,0:T(8,128)} %get-tuple-element.169.part_o, ...), custom_call_target="tpu_custom_call" | custom-call | flops 99999997952 | bytes 20971520 | tf_op jit(solution)/shard_map/cond/branch_1_fun/out1_1/pallas_call | solution.py:605
  201.7 46.4 %mlp1_1.1 = (bf16[64,4096]{1,0:T(8,128)(2,1)}, bf16[4,64,1024]{2,1,0:T(8,128)(2,1)}, bf16[192,2,256,128]{3,2,1,0:T(8,128)(2,1)}) custom-call(bf16[64,4096]{1,0:T(8,128)(2,1)} %get-tuple-element.173.h, bf16[64,1024]{1,0:T(8,128)(2,1)S(1)} %get-tuple-element.168.kv, bf16[2,4096,14336]{2,1,0:T(8,128)(2,1)} %get-tuple-element.174.w_up, ...), custom_call_target="tpu_custom_call", output_to_operand_aliasing={{2}: (5, {})} | custom-call | flops 60129542144 | bytes 117440512 | tf_op jit(solution)/shard_map/cond/branch_1_fun/mlp1_1/pallas_call | solution.py:728
  248.6 1.4 reshape.38
  250.0 0.2 copy.25
  250.2 0.0 copy-done
  250.2 0.4 reshape.37
  250.6 0.2 copy.24
  250.8 1.1 fusion.2
  251.9 10.2 %finish.1 = (bf16[96,2,256,128]{3,2,1,0:T(8,128)(2,1)}, bf16[96,2,256,128]{3,2,1,0:T(8,128)(2,1)}) custom-call(s32[4]{0:T(128)} %get-tuple-element.217.meta, s32[2,65]{1,0:T(2,128)} %get-tuple-element.233.moved, s32[3,129]{1,0:T(4,128)} %get-tuple-element.234.rows, ...), custom_call_target="tpu_custom_call", output_to_operand_aliasing={{0}: (7, {}), {1}: (8, {})} | custom-call | flops 10000000000 | bytes 16777216 | tf_op jit(solution)/shard_map/finish/pallas_call | solution.py:810
  262.1 0.0 copy-done.1
  262.1 0.7 constant_dynamic-slice_fusion
  (1 shorter events, 0.0 us)
Async XLA Ops:
  22.5 15.2 %copy-start.2 = (s32[4]{0:T(128)S(1)}, s32[4]{0:T(128)}, u32[]{:S(2)}) copy-start(s32[4]{0:T(128)} %get-tuple-element.217.meta) | copy-start | bytes 52
  157.7 92.6 %copy-start = (bf16[4,64,1024]{2,1,0:T(8,128)(2,1)S(1)}, bf16[4,64,1024]{2,1,0:T(8,128)(2,1)}, u32[]{:S(2)}) copy-start(bf16[4,64,1024]{2,1,0:T(8,128)(2,1)} %get-tuple-element.237) | copy-start | bytes 1572868
  251.9 10.2 %copy-start.1 = (bf16[64,4096]{1,0:T(8,128)(2,1)S(1)}, bf16[64,4096]{1,0:T(8,128)(2,1)}, u32[]{:S(2)}) copy-start(bf16[64,4096]{1,0:T(8,128)(2,1)} %get-tuple-element.254) | copy-start | bytes 1572868

commit v3 on v2

--- a/solution.py
+++ b/solution.py
@@ -198,13 +198,8 @@
         even = even | misfit | (hs & 1)
         odd = odd | misfit | (1 - (hs & 1))
 
-        @pl.when(hs == me)
-        def _():
-            slots[s - base] = 1
-
-        @pl.when(hd == me)
-        def _():
-            slots[d - base] = 2
+        slots[jnp.where(hs == me, s - base, SLOTS)] = 1
+        slots[jnp.where(hd == me, d - base, SLOTS)] = 2
         moved[0, n] = d - base
         moved[1, n] = place
         return n + (hd == me).astype(jnp.int32), even, odd
@@ -257,7 +252,7 @@
 
 
 def run_plan(new_table, seq_lens, mig_src, mig_dst):
-    shapes = [(4,), (7, SEQS + UNROLL), (SLOTS,), (2, MIG + 1), (3, 2 * SEQS + 1)]
+    shapes = [(4,), (7, SEQS + UNROLL), (SLOTS + 1,), (2, MIG + 1), (3, 2 * SEQS + 1)]
     return pl.pallas_call(
         plan_kernel,
         name='plan',
@@ -273,7 +268,11 @@
 SLOTS_STEP = SLOTS // STEPS
 
 
-def attend_kernel(layer, meta, table, slots, q_all, k_pool, v_pool, part_o, part_l, outbox, pool_out, q_rows, kbuf, vbuf, ring, zeros, sems, out_sems, ring_in, ring_out):
+def attend_kernel(layer, meta, table, slots, q_all, k_pool, v_pool, *refs):
+    if layer == 0:
+        part_o, part_l, outbox, pool_out, q_rows, kbuf, vbuf, ring, zeros, sems, out_sems, ring_in, ring_out = refs
+    else:
+        moved, inbox, _, part_o, part_l, outbox, pool_out, k_out, q_rows, kbuf, vbuf, ring, zeros, sems, out_sems, ring_in, ring_out, pages, page_in, page_out = refs
     groups = (meta[0] + UNROLL - 1) // UNROLL
     pool = (k_pool, v_pool)[layer]
 
@@ -325,11 +324,25 @@
             else:
                 pl.when(state < 2)(lambda: store().wait())
 
+    def settle(phase):
+        def one(i, carry):
+            for p, dst in enumerate((k_out, pool_out)):
+                if phase < 2:
+                    copy = pltpu.make_async_copy(inbox.at[moved[1, i], p], pages.at[i, p], page_in)
+                else:
+                    copy = pltpu.make_async_copy(pages.at[i, p], dst.at[moved[0, i], 0], page_out)
+                copy.wait() if phase % 2 else copy.start()
+            return carry
+
+        lax.fori_loop(0, meta[2], one, 0)
+
     for g in range(NBUF - 1):
         @pl.when(g < groups)
         def _():
             copies(g, True)
         keep(g, 'load')
+    if layer == 1:
+        settle(0)
     zeros[...] = jnp.zeros_like(zeros)
     part_o[...] = jnp.zeros_like(part_o)
     part_l[...] = jnp.full_like(part_l, NEG)
@@ -374,6 +387,11 @@
 
     def step(g, carry):
         keep(g, 'store')
+        if layer == 1:
+            @pl.when(g == STEPS // 2)
+            def _():
+                settle(1)
+                settle(2)
 
         @pl.when(g < groups)
         def _():
@@ -403,21 +421,24 @@
 
     lax.fori_loop(0, STEPS, step, 0)
     keep(STEPS - 1, 'drain')
+    if layer == 1:
+        settle(3)
 
     @pl.when(groups == STEPS)
     def _():
         packs(groups - 1, False)
 
 
-def run_attend(layer, meta, table, slots, q_all, k_flat, v_flat):
+def run_attend(layer, meta, table, slots, q_all, k_flat, v_flat, extra=()):
     shape = jax.ShapeDtypeStruct((2, 2, TOK, HALF_HEADS, HEAD), F32)
     page = (UNROLL, 2, PAGE * KV_HEADS, HEAD)
     return pl.pallas_call(
         functools.partial(attend_kernel, layer),
         name=f'attend{layer}',
-        out_shape=[shape, shape, BOX, jax.ShapeDtypeStruct(k_flat.shape, BF16)],
-        in_specs=[SMEM, SMEM, SMEM, VMEM, ANY, ANY],
-        out_specs=[VMEM, VMEM, ANY, ANY],
+        out_shape=[shape, shape, BOX] + [jax.ShapeDtypeStruct(k_flat.shape, BF16)] * (layer + 1),
+        in_specs=[SMEM, SMEM, SMEM, VMEM, ANY, ANY] + [SMEM, ANY, ANY] * layer,
+        out_specs=[VMEM, VMEM, ANY, ANY] + [ANY] * layer,
+        input_output_aliases={8: 4} if layer else {},
         scratch_shapes=[
             pltpu.VMEM((2 * TOK * HEADS, HEAD), F32),
             pltpu.VMEM((NBUF,) + page, BF16),
@@ -428,10 +449,10 @@
             DMA((NBUF,)),
             DMA((NBUF, SLOTS_STEP)),
             DMA((NBUF, SLOTS_STEP)),
-        ],
+        ] + [pltpu.VMEM((MIG, 2, PAGE * KV_HEADS, HEAD), BF16), DMA, DMA] * layer,
         cost_estimate=pl.CostEstimate(flops=2 * 10 ** 10, bytes_accessed=16 * 2 ** 20, transcendentals=0),
         compiler_params=pltpu.CompilerParams(vmem_limit_bytes=VMEM_LIMIT),
-    )(meta, table, slots, q_all, k_flat, v_flat)
+    )(meta, table, slots, q_all, k_flat, v_flat, *extra)
 
 
 def merge(parts):
@@ -442,10 +463,7 @@
     return out, top + jnp.log(total)
 
 
-EARLY = 6
-MODES = tuple(
-    ([((core,), 2, 0, EARLY)], [((core,), 2, EARLY, FAST_PAGES), ((core,), 0, 0, FAST_PAGES)]) for core in range(2)
-) + (([], [((0, 1), channel, 0, MIG) for channel in range(3)]),)
+MODES = ([((0,), 2, FAST_PAGES), ((0,), 0, FAST_PAGES)], [((1,), 2, FAST_PAGES), ((1,), 0, FAST_PAGES)], [((0, 1), i, MIG) for i in range(3)])
 CHUNK = 2
 
 
@@ -456,14 +474,14 @@
         self.moves, self.outbox, self.inbox, self.send_sems, self.recv_sems = moves, outbox, inbox, send_sems, recv_sems
 
     def each(self, sending, act):
-        for cores, channel, first, end in self.moves:
-            def run(cores=cores, channel=channel, first=first, end=end):
+        for cores, channel, pages in self.moves:
+            def run(channel=channel, pages=pages):
                 def one(i, carry):
                     rows = pl.ds(channel * MIG + i * CHUNK, CHUNK)
                     act(send(self.outbox.at[rows], self.inbox.at[rows], self.send_sems.at[channel, i], self.recv_sems.at[channel, i], self.peers[channel]))
                     return carry
 
-                lax.fori_loop(first // CHUNK, end // CHUNK, one, 0)
+                lax.fori_loop(0, pages // CHUNK, one, 0)
 
             if len(cores) == 2:
                 run()
@@ -480,49 +498,86 @@
         self.each(False, lambda copy: copy.wait_recv())
 
 
-def out_kernel(layer, mode, h, q_all, kv, part_o, part_l, wo, outbox, out, inbox, wbuf, wsem, got_o, got_l, mine_o, mine_l, give_o, give_l, far_o, far_l,
-               q_rows, k_rows, v_rows, attn, psend, precv, dsend, drecv, xsend, xrecv, ssem, rsem, bsend, brecv):
-    boxes = Boxes(MODES[mode][0], outbox, inbox, bsend, brecv)
+RING_W = 20
+TK = 2048
+UP_TILES = FF // 2 // TN
+TD = FF // 8
+OUT_END = D // TN
+UP_END = OUT_END + 2 * UP_TILES
+ALL_TILES = UP_END + 4 * (D // TN)
+PART = TOK // 2
+
+
+def rest_kernel(layer, mode, h_in, q_all, kv, part_o, part_l, wo, w_up, w_down, outbox, out, kv_all, inbox, ring, ring_sem, own_o, own_l, own_sem,
+                got_o, got_l, mine_o, mine_l, give_o, give_l, far_o, far_l, q_rows, k_rows, v_rows, attn, act, h, psend, precv,
+                dsend, drecv, xsend, xrecv, ssem, rsem, ksend, krecv, bsend, brecv):
     me, chip, core, partner, across, diag = places()
-
-    def fetch(j):
-        src = wo.at[layer, pl.ds(pl.multiple_of(core * 2048, 2048), 2048), pl.ds(j * TN, TN)]
-        return pltpu.make_async_copy(src, wbuf.at[j], wsem.at[j])
-
-    for j in range(8):
-        fetch(j).start()
+    boxes = Boxes(MODES[mode], outbox, inbox, bsend, brecv)
+
+    def tile_copy(t, kind):
+        slot = lax.rem(t, RING_W)
+        if kind == 0:
+            src = wo.at[layer, pl.ds(pl.multiple_of(core * TK, TK), TK), pl.ds(pl.multiple_of(t * TN, TN), TN)]
+        elif kind == 1:
+            i = t - OUT_END
+            src = w_up.at[layer, pl.ds(pl.multiple_of(lax.rem(i, 2) * TK, TK), TK), pl.ds(pl.multiple_of(core * (FF // 2) + (i // 2) * TN, TN), TN)]
+        else:
+            i = t - UP_END
+            src = w_down.at[layer, pl.ds(pl.multiple_of(core * (FF // 2) + lax.rem(i, 4) * TD, TD), TD), pl.ds(pl.multiple_of((i // 4) * TN, TN), TN)]
+        dst = ring.at[slot, pl.ds(0, TD)] if kind == 2 else ring.at[slot]
+        return pltpu.make_async_copy(src, dst, ring_sem.at[slot])
+
+    def fetch(t):
+        pl.when(t < OUT_END)(lambda: tile_copy(t, 0).start())
+        pl.when((t >= OUT_END) & (t < UP_END))(lambda: tile_copy(t, 1).start())
+        pl.when((t >= UP_END) & (t < ALL_TILES))(lambda: tile_copy(t, 2).start())
+
+    own, near = [], []
+    for which, (owner, first, size) in enumerate(((1 - chip, 0, PART), (1 - chip, PART, PART), (chip, 0, TOK))):
+        at = pl.ds(which * PART, size)
+        rows = pl.ds(first, size)
+        for i, (src, dst) in enumerate(((part_o, own_o), (part_l, own_l))):
+            copy = pltpu.make_async_copy(src.at[owner, core, rows], dst.at[at], own_sem.at[which, i])
+            copy.start()
+            own.append(copy)
+        near.append([
+            send(part_o.at[owner, 1 - core, rows], got_o.at[at], dsend.at[which, 0], drecv.at[which, 0], partner),
+            send(part_l.at[owner, 1 - core, rows], got_l.at[at], dsend.at[which, 1], drecv.at[which, 1], partner),
+        ])
     meet((partner, across, diag))
-
-    near = []
-    for which in range(2):
-        owner = 1 - chip if which == 0 else chip
+    for pair in near:
+        for copy in pair:
+            copy.start()
+    lax.fori_loop(0, RING_W, lambda t, carry: (fetch(t), carry)[1], 0)
+
+    lane = lax.broadcasted_iota(jnp.int32, (8, HEAD), 1)
+    far = []
+    for part in range(2):
+        for copy in own[2 * part:2 * part + 2]:
+            copy.wait()
+        for copy in near[part]:
+            copy.wait_recv()
+
+        def chip_merge(i, compact, part=part):
+            j = part * PART + i
+            o, l = merge([(own_o[j], own_l[j]), (got_o[j], got_l[j])])
+            give_o[j] = o
+            compact = jnp.where(lane == 2 * i, l[:8], compact)
+            return jnp.where(lane == 2 * i + 1, l[8:], compact)
+
+        give_l[part] = lax.fori_loop(0, PART, chip_merge, jnp.zeros((8, HEAD), F32), unroll=8)
+        rows = pl.ds(part * PART, PART)
         pair = [
-            send(part_o.at[owner, 1 - core], got_o.at[which], dsend.at[which, 0], drecv.at[which, 0], partner),
-            send(part_l.at[owner, 1 - core], got_l.at[which], dsend.at[which, 1], drecv.at[which, 1], partner),
+            send(give_l.at[part], far_l.at[part], xsend.at[part, 0], xrecv.at[part, 0], across),
+            send(give_o.at[rows], far_o.at[rows], xsend.at[part, 1], xrecv.at[part, 1], across),
         ]
         for copy in pair:
             copy.start()
-        near.append(pair)
-
-    lane = lax.broadcasted_iota(jnp.int32, (8, HEAD), 1)
-
-    for copy in near[0]:
-        copy.wait_recv()
-
-    def chip_merge(i, compact):
-        o, l = merge([(part_o[1 - chip, core, i], part_l[1 - chip, core, i]), (got_o[0, i], got_l[0, i])])
-        give_o[i] = o
-        compact = jnp.where(lane == 2 * i, l[:8], compact)
-        return jnp.where(lane == 2 * i + 1, l[8:], compact)
-
-    compact = lax.fori_loop(0, TOK, chip_merge, jnp.zeros((8, HEAD), F32), unroll=8)
-    give_l[...] = compact
-    far = [
-        send(give_l, far_l, xsend.at[0], xrecv.at[0], across),
-        send(give_o, far_o, xsend.at[1], xrecv.at[1], across),
-    ]
-    for copy in far:
-        copy.start()
+        far.append(pair)
+
+    kv_all[me] = kv[...]
+    new_rows = [send(kv, kv_all.at[me], ksend.at[i], krecv.at[i], peer) for i, peer in enumerate((partner, across))]
+    new_rows.append(send(kv_all.at[across], kv_all.at[across], ksend.at[2], krecv.at[2], partner))
 
     for head in range(HALF_HEADS):
         tile = core * 4 + head // 4
@@ -530,7 +585,9 @@
         q_rows[rows, :] = q_all[chip, tile, :, (head % 4) * HEAD:(head % 4 + 1) * HEAD].astype(F32)
         k_rows[rows, :] = kv[:, (head // 4) * HEAD:(head // 4 + 1) * HEAD].astype(F32)
         v_rows[rows, :] = kv[:, TN + (head // 4) * HEAD:TN + (head // 4 + 1) * HEAD].astype(F32)
-    for copy in near[1]:
+    for copy in own[4:]:
+        copy.wait()
+    for copy in near[2]:
         copy.wait_recv()
 
     half = ROWS // 2
@@ -539,236 +596,174 @@
         s = jnp.sum(q * k, axis=1, keepdims=True) * SCALE
         return jnp.broadcast_to(s, q.shape)
 
-    def own(i, carry):
+    def own_merge(i, carry):
         a = pl.ds(pl.multiple_of(i * HALF_HEADS, HALF_HEADS), HALF_HEADS)
         b = pl.ds(pl.multiple_of(half + i * HALF_HEADS, HALF_HEADS), HALF_HEADS)
         k0, v0, k1, v1 = k_rows[a, :], v_rows[a, :], k_rows[b, :], v_rows[b, :]
         q0, q1 = q_rows[a, :], q_rows[b, :]
-        j = i + TOK // 2
-        o, l = merge([(part_o[chip, core, i], part_l[chip, core, i]), (got_o[1, i], got_l[1, i]), (v0, score(q0, k0))])
+        j = i + PART
+        m, n = TOK + i, TOK + j
+        o, l = merge([(own_o[m], own_l[m]), (got_o[m], got_l[m]), (v0, score(q0, k0))])
         mine_o[i] = o
         mine_l[i] = l
-        o, l = merge([(part_o[chip, core, j], part_l[chip, core, j]), (got_o[1, j], got_l[1, j]), (v0, score(q1, k0)), (v1, score(q1, k1))])
+        o, l = merge([(own_o[n], own_l[n]), (got_o[n], got_l[n]), (v0, score(q1, k0)), (v1, score(q1, k1))])
         mine_o[j] = o
         mine_l[j] = l
         return carry
 
-    lax.fori_loop(0, TOK // 2, own, 0, unroll=4)
-
-    for copy in far:
-        copy.wait_recv()
-    boxes.start()
-    spread = far_l[...]
-
-    def last_merge(i, carry):
-        l = jnp.concatenate([
-            jnp.broadcast_to(jnp.sum(jnp.where(lane == 2 * i + k, spread, 0.0), axis=1, keepdims=True), (8, HEAD)) for k in range(2)
-        ], axis=0)
-        o, _ = merge([(mine_o[i], mine_l[i]), (far_o[i], l)])
-        q_rows[pl.ds(pl.multiple_of(i * HALF_HEADS, HALF_HEADS), HALF_HEADS), :] = o
-        return carry
-
-    lax.fori_loop(0, TOK, last_merge, 0, unroll=8)
+    lax.fori_loop(0, PART, own_merge, 0, unroll=4)
+
+    for part in range(2):
+        for copy in far[part]:
+            copy.wait_recv()
+        if part == 1:
+            for copy in new_rows[:2]:
+                copy.start()
+            boxes.start()
+        spread = far_l[part]
+
+        def last_merge(i, carry, part=part, spread=spread):
+            l = jnp.concatenate([
+                jnp.broadcast_to(jnp.sum(jnp.where(lane == 2 * i + k, spread, 0.0), axis=1, keepdims=True), (8, HEAD)) for k in range(2)
+            ], axis=0)
+            j = part * PART + i
+            o, _ = merge([(mine_o[j], mine_l[j]), (far_o[j], l)])
+            q_rows[pl.ds(pl.multiple_of(j * HALF_HEADS, HALF_HEADS), HALF_HEADS), :] = o
+            return carry
+
+        lax.fori_loop(0, PART, last_merge, 0, unroll=8)
     for head in range(HALF_HEADS):
         attn[:, head * HEAD:(head + 1) * HEAD] = q_rows[pl.ds(head, TOK, stride=HALF_HEADS), :].astype(BF16)
 
     def reduce(j):
         return send(psend.at[j], precv.at[j], ssem.at[j], rsem.at[j], partner)
 
+    def finish_sum(first, res, target):
+        reduce(first + 7).start()
+        for j in range(8):
+            reduce(first + j).wait_recv()
+            cols = slice(j * TN, (j + 1) * TN)
+            target[:, cols] = (res[:, cols].astype(F32) + (psend[first + j] + precv[first + j])).astype(BF16)
+
     def project(j, carry):
-        pltpu.make_async_copy(wo.at[layer, pl.ds(0, 2048), pl.ds(0, TN)], wbuf.at[j], wsem.at[j]).wait()
-        psend[j] = dot(attn[...], wbuf[j])
+        tile_copy(j, 0).wait()
+        psend[j] = dot(attn[...], ring[lax.rem(j, RING_W)])
+        fetch(j + RING_W)
 
         @pl.when(j > 0)
         def _():
             reduce(j - 1).start()
         return carry
 
-    lax.fori_loop(0, 8, project, 0)
-    reduce(7).start()
-    for j in range(8):
-        reduce(j).wait_recv()
-        cols = slice(j * TN, (j + 1) * TN)
-        out[:, cols] = (h[:, cols].astype(F32) + (psend[j] + precv[j])).astype(BF16)
-    for j in range(8):
+    lax.fori_loop(0, OUT_END, project, 0)
+    finish_sum(0, h_in, h)
+
+    def up(s, carry):
+        u = None
+        for k in range(2):
+            t = OUT_END + 2 * s + k
+            tile_copy(t, 1).wait()
+            part = dot(h[:, k * TK:(k + 1) * TK], ring[lax.rem(t, RING_W)])
+            u = part if u is None else u + part
+            fetch(t + RING_W)
+        a = jax.nn.gelu(u.astype(BF16).astype(F32), approximate=True).astype(BF16)
+        act[:, pl.ds(pl.multiple_of(s * TN, TN), TN)] = a
+        return carry
+
+    lax.fori_loop(0, UP_TILES, up, 0)
+    new_rows[1].wait_recv()
+    new_rows[2].start()
+
+    def down(j, carry):
+        total = None
+        for k in range(4):
+            t = UP_END + 4 * j + k
+            tile_copy(t, 2).wait()
+            part = dot(act[:, k * TD:(k + 1) * TD], ring[lax.rem(t, RING_W), :TD])
+            total = part if total is None else total + part
+            fetch(t + RING_W)
+        psend[8 + j] = total
+
+        @pl.when(j > 0)
+        def _():
+            reduce(8 + j - 1).start()
+        return carry
+
+    lax.fori_loop(0, D // TN, down, 0)
+    finish_sum(8, h, out)
+    for j in range(16):
         reduce(j).wait_send()
-    for pair in near:
+    for pair in near + far:
         for copy in pair:
             copy.wait_send()
-    for copy in far:
-        copy.wait_send()
+    new_rows[0].wait()
+    new_rows[1].wait_send()
+    new_rows[2].wait()
     boxes.wait()
 
 
-def run_out(layer, mode, h, q_all, kv, part_o, part_l, w_out, outbox):
-    token = (TOK, HALF_HEADS, HEAD)
+def run_rest(layer, mode, h, q_all, kv, part_o, part_l, outbox, w_out, w_up, w_down):
+    token = (HALF_HEADS, HEAD)
     return pl.pallas_call(
-        functools.partial(out_kernel, layer, mode),
-        name=f'out{layer}_{mode}',
-        out_shape=[jax.ShapeDtypeStruct((TOK, D), BF16), BOX],
-        in_specs=[VMEM] * 5 + [ANY, ANY],
-        out_specs=[VMEM, ANY],
+        functools.partial(rest_kernel, layer, mode),
+        name=f'rest{layer}_{mode}',
+        out_shape=[jax.ShapeDtypeStruct((TOK, D), BF16), jax.ShapeDtypeStruct((4, TOK, 2 * TN), BF16), BOX],
+        in_specs=[VMEM] * 3 + [ANY] * 6,
+        out_specs=[VMEM, VMEM, ANY],
         scratch_shapes=[
-            pltpu.VMEM((8, 2048, TN), BF16),
-            DMA((8,)),
-            pltpu.VMEM((2,) + token, F32),
-            pltpu.VMEM((2,) + token, F32),
-            pltpu.VMEM(token, F32),
-            pltpu.VMEM(token, F32),
-            pltpu.VMEM(token, F32),
-            pltpu.VMEM((8, HEAD), F32),
-            pltpu.VMEM(token, F32),
-            pltpu.VMEM((8, HEAD), F32),
+            pltpu.VMEM((RING_W, TK, TN), BF16),
+            DMA((RING_W,)),
+            pltpu.VMEM((2 * TOK,) + token, F32),
+            pltpu.VMEM((2 * TOK,) + token, F32),
+            DMA((3, 2)),
+            pltpu.VMEM((2 * TOK,) + token, F32),
+            pltpu.VMEM((2 * TOK,) + token, F32),
+            pltpu.VMEM((TOK,) + token, F32),
+            pltpu.VMEM((TOK,) + token, F32),
+            pltpu.VMEM((TOK,) + token, F32),
+            pltpu.VMEM((2, 8, HEAD), F32),
+            pltpu.VMEM((TOK,) + token, F32),
+            pltpu.VMEM((2, 8, HEAD), F32),
             pltpu.VMEM((ROWS, HEAD), F32),
             pltpu.VMEM((ROWS, HEAD), F32),
             pltpu.VMEM((ROWS, HEAD), F32),
             pltpu.VMEM((TOK, 2048), BF16),
-            pltpu.VMEM((8, TOK, TN), F32),
-            pltpu.VMEM((8, TOK, TN), F32),
+            pltpu.VMEM((TOK, FF // 2), BF16),
+            pltpu.VMEM((TOK, D), BF16),
+            pltpu.VMEM((16, TOK, TN), F32),
+            pltpu.VMEM((16, TOK, TN), F32),
+            DMA((3, 2)),
+            DMA((3, 2)),
             DMA((2, 2)),
             DMA((2, 2)),
-            DMA((2,)),
-            DMA((2,)),
-            DMA((8,)),
-            DMA((8,)),
-            DMA((3, MIG // CHUNK)),
-            DMA((3, MIG // CHUNK)),
-        ],
-        cost_estimate=pl.CostEstimate(flops=10 ** 11, bytes_accessed=20 * 2 ** 20, transcendentals=0),
-        compiler_params=pltpu.CompilerParams(collective_id=2 + layer * 3 + mode, has_side_effects=True, vmem_limit_bytes=VMEM_LIMIT),
-    )(h, q_all, kv, part_o, part_l, w_out, outbox)
-
-
-NU = 4
-ND = 4
-UP_TILES = FF // 2 // TN
-KROWS = FF // 4
-DOWN_TILES = 2 * (D // TN)
-
-
-def mlp_kernel(layer, mode, h, kv, w_up, w_down, outbox, inbox_in, out, kv_all, inbox, ubuf, dbuf, act, psend, precv, usem, dsem, ssem, rsem, ksend, krecv, bsend, brecv):
-    me, chip, core, partner, across, diag = places()
-    boxes = Boxes(MODES[mode][1], outbox, inbox, bsend, brecv)
-
-    def fetch_up(s):
-        src = w_up.at[layer, :, pl.ds(pl.multiple_of(core * (FF // 2) + s * TN, TN), TN)]
-        slot = lax.rem(s, NU)
-        return pltpu.make_async_copy(src, ubuf.at[slot], usem.at[slot])
-
-    def fetch_down(s):
-        src = w_down.at[layer, pl.ds(pl.multiple_of(core * (FF // 2) + lax.rem(s, 2) * KROWS, KROWS), KROWS), pl.ds(pl.multiple_of((s // 2) * TN, TN), TN)]
-        slot = lax.rem(s, ND)
-        return pltpu.make_async_copy(src, dbuf.at[slot], dsem.at[slot])
-
-    for s in range(NU):
-        fetch_up(jnp.int32(s)).start()
-    meet((partner, across, diag))
-    kv_all[me] = kv[...]
-    rows = [send(kv, kv_all.at[me], ksend.at[i], krecv.at[i], peer) for i, peer in enumerate((partner, across))]
-    rows.append(send(kv_all.at[across], kv_all.at[across], ksend.at[2], krecv.at[2], partner))
-    for copy in rows[:2]:
-        copy.start()
-    boxes.start()
-
-    def up(s, carry):
-        fetch_up(s).wait()
-        u = dot(h[...], ubuf[lax.rem(s, NU)]).astype(BF16)
-        a = jax.nn.gelu(u.astype(F32), approximate=True).astype(BF16)
-        act[s // 7, :, pl.ds(pl.multiple_of(lax.rem(s, 7) * TN, TN), TN)] = a
-
-        @pl.when(s + NU < UP_TILES)
-        def _():
-            fetch_up(s + NU).start()
-
-        @pl.when(s + NU >= UP_TILES)
-        def _():
-            fetch_down(s + NU - UP_TILES).start()
-        return carry
-
-    lax.fori_loop(0, UP_TILES, up, 0)
-    rows[1].wait_recv()
-    rows[2].start()
-
-    def reduce(j):
-        return send(psend.at[j], precv.at[j], ssem.at[j], rsem.at[j], partner)
-
-    def down(j, carry):
-        total = None
-        for k in range(2):
-            s = 2 * j + k
-            fetch_down(s).wait()
-            part = dot(act[k], dbuf[lax.rem(s, ND)])
-            total = part if total is None else total + part
-
-            @pl.when(s + ND < DOWN_TILES)
-            def _():
-                fetch_down(s + ND).start()
-        psend[j] = total
-
-        @pl.when(j > 0)
-        def _():
-            reduce(j - 1).start()
-        return carry
-
-    lax.fori_loop(0, 8, down, 0)
-    reduce(7).start()
-    for j in range(8):
-        reduce(j).wait_recv()
-        cols = slice(j * TN, (j + 1) * TN)
-        out[:, cols] = (h[:, cols].astype(F32) + (psend[j] + precv[j])).astype(BF16)
-    for j in range(8):
-        reduce(j).wait_send()
-    rows[0].wait()
-    rows[1].wait_send()
-    rows[2].wait()
-    boxes.wait()
-
-
-def run_mlp(layer, mode, h, kv, w_up, w_down, outbox, inbox):
-    return pl.pallas_call(
-        functools.partial(mlp_kernel, layer, mode),
-        name=f'mlp{layer}_{mode}',
-        out_shape=[jax.ShapeDtypeStruct((TOK, D), BF16), jax.ShapeDtypeStruct((4, TOK, 2 * TN), BF16), BOX],
-        in_specs=[VMEM, VMEM, ANY, ANY, ANY, ANY],
-        out_specs=[VMEM, VMEM, ANY],
-        input_output_aliases={5: 2},
-        scratch_shapes=[
-            pltpu.VMEM((NU, D, TN), BF16),
-            pltpu.VMEM((ND, KROWS, TN), BF16),
-            pltpu.VMEM((2, TOK, KROWS), BF16),
-            pltpu.VMEM((8, TOK, TN), F32),
-            pltpu.VMEM((8, TOK, TN), F32),
-            DMA((NU,)),
-            DMA((ND,)),
-            DMA((8,)),
-            DMA((8,)),
+            DMA((16,)),
+            DMA((16,)),
             DMA((3,)),
             DMA((3,)),
             DMA((3, MIG // CHUNK)),
             DMA((3, MIG // CHUNK)),
         ],
         cost_estimate=pl.CostEstimate(flops=2 * TOK * D * FF * 8, bytes_accessed=D * FF * 2, transcendentals=0),
-        compiler_params=pltpu.CompilerParams(collective_id=8 + layer * 3 + mode, has_side_effects=True, vmem_limit_bytes=VMEM_LIMIT),
-    )(h, kv, w_up, w_down, outbox, inbox)
-
-
-RING = 16
+        compiler_params=pltpu.CompilerParams(collective_id=2 + layer * 3 + mode, has_side_effects=True, vmem_limit_bytes=67043328),
+    )(h, q_all, kv, part_o, part_l, w_out, w_up, w_down, outbox)
+
+
+RING = 32
 AHEAD = RING // 2
 
 
-def finish_kernel(meta, moved, rows, inbox0, inbox1, k_rows, v_rows, k_in, v_in, k_out, v_out, buf, in_sem, out_sem, row_sem):
+def finish_kernel(meta, moved, rows, inbox, k_rows, v_rows, k_in, v_in, k_out, v_out, buf, in_sem, out_sem, row_sem):
     del k_in, v_in
-    inboxes = (inbox0, inbox1)
     outs = (k_out, v_out)
     count = meta[2]
 
     def load(i):
         slot = lax.rem(i, RING)
-        return [pltpu.make_async_copy(inboxes[l].at[moved[1, i], p], buf.at[slot, p, l], in_sem.at[slot, p, l]) for p in range(2) for l in range(LAYERS)]
+        return [pltpu.make_async_copy(inbox.at[moved[1, i], p], buf.at[slot, p], in_sem.at[slot, p]) for p in range(2)]
 
     def store(i):
         slot = lax.rem(i, RING)
-        return [pltpu.make_async_copy(buf.at[slot, p], outs[p].at[moved[0, i]], out_sem.at[slot, p]) for p in range(2)]
+        return [pltpu.make_async_copy(buf.at[slot, p], outs[p].at[moved[0, i], 1], out_sem.at[slot, p]) for p in range(2)]
 
     def begin(group):
         for copy in group:
@@ -805,24 +800,24 @@
     loop(0, meta[3], lambda i: end(row(i)))
 
 
-def run_finish(meta, moved, rows, inboxes, k_rows, v_rows, k_part, v_part):
+def run_finish(meta, moved, rows, inbox, k_rows, v_rows, k_part, v_part):
     shape = jax.ShapeDtypeStruct(k_part.shape, BF16)
     return pl.pallas_call(
         finish_kernel,
         name='finish',
         out_shape=[shape, shape],
-        in_specs=[SMEM, SMEM, SMEM, ANY, ANY, VMEM, VMEM, ANY, ANY],
+        in_specs=[SMEM, SMEM, SMEM, ANY, VMEM, VMEM, ANY, ANY],
         out_specs=[ANY, ANY],
         scratch_shapes=[
-            pltpu.VMEM((RING, 2) + k_part.shape[1:], BF16),
-            DMA((RING, 2, LAYERS)),
+            pltpu.VMEM((RING, 2) + k_part.shape[2:], BF16),
+            DMA((RING, 2)),
             DMA((RING, 2)),
             DMA((2, LAYERS)),
         ],
-        input_output_aliases={7: 0, 8: 1},
+        input_output_aliases={6: 0, 7: 1},
         cost_estimate=pl.CostEstimate(flops=10 ** 10, bytes_accessed=16 * 2 ** 20, transcendentals=0),
         compiler_params=pltpu.CompilerParams(vmem_limit_bytes=VMEM_LIMIT),
-    )(meta, moved, rows, *inboxes, k_rows, v_rows, k_part, v_part)
+    )(meta, moved, rows, inbox, k_rows, v_rows, k_part, v_part)
 
 
 def by_token(kv_all):
@@ -839,26 +834,21 @@
         weights = (w_query, w_key, w_value)
         k_flat, v_flat = flat_pool(k_pool), flat_pool(v_pool)
         meta, items, slots, moved, where = run_plan(new_table, seq_lens, mig_src, mig_dst)
-        rows, inboxes, pools = [], [], []
+        rows = []
         h = None
         for layer in range(LAYERS):
             if layer == 0:
                 q_all, kv, h = run_qkv(layer, embeds, weights, True)
             else:
                 q_all, kv = run_qkv(layer, h, weights, False)
-            part_o, part_l, outbox, pool = run_attend(layer, meta, items, slots, q_all, k_flat, v_flat)
-
-            def rest(mode, h, q_all, kv, part_o, part_l, outbox, w_out, w_up, w_down, layer=layer):
-                h, inbox = run_out(layer, mode, h, q_all, kv, part_o, part_l, w_out, outbox)
-                return run_mlp(layer, mode, h, kv, w_up, w_down, outbox, inbox)
-
-            forms = [functools.partial(rest, mode) for mode in range(len(MODES))]
+            extra = (moved, inbox, pools[0]) if layer else ()
+            part_o, part_l, outbox, *pools = run_attend(layer, meta, items, slots, q_all, k_flat, v_flat, extra)
+
+            forms = [functools.partial(run_rest, layer, mode) for mode in range(len(MODES))]
             h, kv_all, inbox = lax.switch(meta[1], forms, h, q_all, kv, part_o, part_l, outbox, w_out, w_up, w_down)
-            inboxes.append(inbox)
             rows.append(by_token(kv_all))
-            pools.append(pool)
         rows = jnp.stack(rows)
-        k_out, v_out = run_finish(meta, moved, where, inboxes, rows[:, 0], rows[:, 1], *pools)
+        k_out, v_out = run_finish(meta, moved, where, inbox, rows[:, 0], rows[:, 1], pools[1], pools[0])
         k_out, v_out = k_out.reshape(k_pool.shape), v_out.reshape(v_pool.shape)
         y = lax.dynamic_slice_in_dim(h.reshape(2, 32, D), (me % 2) * 16, 16, axis=1)
         return y, k_out, v_out

time: 264 us -> 249 us (0.943)
  the two profiles are of different devices: /device:TPU:0 before, /device:TPU:6 now
where the time goes in v3:
time: 249 us
  Pallas kernels  241 us (97%)
  local copies, waits for them, and re-layouts  4.55 us (2%)
    pallas_call x2, Pallas kernels, run_rest(): pl.pallas_call(functools.partial(rest_kernel, layer, mode), name=f'rest{l...  165 us
    pallas_call x2, Pallas kernels, run_attend(): pl.pallas_call(functools.partial(attend_kernel, layer), name=f'attend{lay...  32.9 us
    pallas_call x2, Pallas kernels, run_qkv(): pl.pallas_call(functools.partial(qkv_kernel, layer, first), name=f'qkv{la...  29.3 us
    pallas_call x1, Pallas kernels, run_finish(): pl.pallas_call(finish_kernel, name='finish', out_shape=[shape, shape], in...  7.44 us
    pallas_call x1, Pallas kernels, run_plan(): pl.pallas_call(plan_kernel, name='plan', out_shape=[jax.ShapeDtypeStruct(...  5.69 us

profile of v3, /device:TPU:6, one launch (start us, length us, event | category | flops | bytes accessed | tf_op | source)
XLA Modules:
  0.0 248.8 jit_solution(10211488342099156543)
XLA Ops:
  0.6 5.7 %plan.1 = (s32[4]{0:T(128)}, s32[7,68]{1,0:T(8,128)}, s32[97]{0:T(128)}, s32[2,65]{1,0:T(2,128)}, s32[3,129]{1,0:T(4,128)}) custom-call(s32[2,64]{1,0:T(2,128)} %bitcast.22, s32[64]{0:T(128)} %seq_lens.1, s32[64]{0:T(128)} %mig_src.1, s32[64]{0:T(128)} %mig_dst.1), custom_call_target="tpu_custom_call" | custom-call | tf_op jit(solution)/shard_map/plan/pallas_call | solution.py:256
  6.3 15.1 %qkv0.1 = (bf16[2,8,64,512]{3,2,1,0:T(8,128)(2,1)}, bf16[64,1024]{1,0:T(8,128)(2,1)}, bf16[64,4096]{1,0:T(8,128)(2,1)}) custom-call(bf16[2,16,4096]{2,1,0:T(8,128)(2,1)} %refs_0_.1, bf16[2,4096,4096]{2,1,0:T(8,128)(2,1)} %refs_1_.3, bf16[2,4096,1024]{2,1,0:T(8,128)(2,1)} %refs_2_.3, bf16[2,4096,1024]{2,1,0:T(8,128)(2,1)} %refs_3_.3), custom_call_target="tpu_custom_call" | custom-call | flops 12884901888 | bytes 25165824 | tf_op jit(solution)/shard_map/qkv0/pallas_call | solution.py:152
  21.4 0.0 copy-start.1
  21.5 15.7 %attend0.1 = (f32[2,2,64,16,128]{4,3,2,1,0:T(8,128)}, f32[2,2,64,16,128]{4,3,2,1,0:T(8,128)}, bf16[192,2,256,128]{3,2,1,0:T(8,128)(2,1)}, bf16[96,2,256,128]{3,2,1,0:T(8,128)(2,1)}) custom-call(s32[4]{0:T(128)} %get-tuple-element.206.meta, s32[7,68]{1,0:T(8,128)} %get-tuple-element.210.table, s32[97]{0:T(128)} %get-tuple-element.211.slots, ...), custom_call_target="tpu_custom_call" | custom-call | flops 20000000000 | bytes 16777216 | tf_op jit(solution)/shard_map/attend0/pallas_call | solution.py:435
  37.2 0.0 copy-done.1
  37.2 0.6 slice.10
  38.5 83.5 %conditional.2 = ((bf16[64,4096]{1,0:T(8,128)(2,1)}, bf16[4,64,1024]{2,1,0:T(8,128)(2,1)}, bf16[192,2,256,128]{3,2,1,0:T(8,128)(2,1)})) conditional(s32[]{:T(128)} %bitcast.1, (bf16[64,4096]{1,0:T(8,128)(2,1)}, bf16[2,8,64,512]{3,2,1,0:T(8,128)(2,1)}, bf16[64,1024]{1,0:T(8,128)(2,1)}, f32[2,2,64,16,128]{4,3,2,1,0:T(8,128)}, ...), branch_computations={%region_0.0_spmd, %region_1.0_spmd, %region_2.0_spmd} | conditional | flops 60129542144 | bytes 117440520 | solution.py:848
  38.5 83.1 %rest0_1.1 = (bf16[64,4096]{1,0:T(8,128)(2,1)}, bf16[4,64,1024]{2,1,0:T(8,128)(2,1)}, bf16[192,2,256,128]{3,2,1,0:T(8,128)(2,1)}) custom-call(bf16[64,4096]{1,0:T(8,128)(2,1)} %get-tuple-element.131.h_in, bf16[2,8,64,512]{3,2,1,0:T(8,128)(2,1)} %get-tuple-element.132.q_all, bf16[64,1024]{1,0:T(8,128)(2,1)} %get-tuple-element.133.kv, ...), custom_call_target="tpu_custom_call" | custom-call | flops 60129542144 | bytes 117440512 | tf_op jit(solution)/shard_map/cond/branch_1_fun/rest0_1/pallas_call | solution.py:707
  122.0 14.2 %qkv1.1 = (bf16[2,8,64,512]{3,2,1,0:T(8,128)(2,1)}, bf16[64,1024]{1,0:T(8,128)(2,1)}) custom-call(bf16[64,4096]{1,0:T(8,128)(2,1)} %get-tuple-element.215.refs_0_, bf16[2,4096,4096]{2,1,0:T(8,128)(2,1)} %refs_1_.3, bf16[2,4096,1024]{2,1,0:T(8,128)(2,1)} %refs_2_.3, bf16[2,4096,1024]{2,1,0:T(8,128)(2,1)} %refs_3_.3), custom_call_target="tpu_custom_call" | custom-call | flops 12884901888 | bytes 25165824 | tf_op jit(solution)/shard_map/qkv1/pallas_call | solution.py:152
  136.2 17.2 %attend1.1 = (f32[2,2,64,16,128]{4,3,2,1,0:T(8,128)}, f32[2,2,64,16,128]{4,3,2,1,0:T(8,128)}, bf16[192,2,256,128]{3,2,1,0:T(8,128)(2,1)}, bf16[96,2,256,128]{3,2,1,0:T(8,128)(2,1)}, bf16[96,2,256,128]{3,2,1,0:T(8,128)(2,1)}) custom-call(s32[4]{0:T(128)} %get-tuple-element.206.meta, ...), custom_call_target="tpu_custom_call", output_to_operand_aliasing={{4}: (8, {})} | custom-call | flops 20000000000 | bytes 16777216 | tf_op jit(solution)/shard_map/attend1/pallas_call | solution.py:435
  153.5 82.9 %conditional.3 = ((bf16[64,4096]{1,0:T(8,128)(2,1)}, bf16[4,64,1024]{2,1,0:T(8,128)(2,1)}, bf16[192,2,256,128]{3,2,1,0:T(8,128)(2,1)})) conditional(s32[]{:T(128)} %bitcast.1, (bf16[64,4096]{1,0:T(8,128)(2,1)}, bf16[2,8,64,512]{3,2,1,0:T(8,128)(2,1)}, bf16[64,1024]{1,0:T(8,128)(2,1)}, f32[2,2,64,16,128]{4,3,2,1,0:T(8,128)}, ...), branch_computations={%region_3.0_spmd, %region_4.0_spmd, %region_5.0_spmd} | conditional | flops 60129542144 | bytes 117440520 | solution.py:848
  153.5 82.3 %rest1_1.1 = (bf16[64,4096]{1,0:T(8,128)(2,1)}, bf16[4,64,1024]{2,1,0:T(8,128)(2,1)}, bf16[192,2,256,128]{3,2,1,0:T(8,128)(2,1)}) custom-call(bf16[64,4096]{1,0:T(8,128)(2,1)} %get-tuple-element.158.h_in, bf16[2,8,64,512]{3,2,1,0:T(8,128)(2,1)} %get-tuple-element.159.q_all, bf16[64,1024]{1,0:T(8,128)(2,1)} %get-tuple-element.160.kv, ...), custom_call_target="tpu_custom_call" | custom-call | flops 60129542144 | bytes 117440512 | tf_op jit(solution)/shard_map/cond/branch_1_fun/rest1_1/pallas_call | solution.py:707
  236.4 1.4 reshape.38
  237.8 0.2 copy.20
  238.0 1.4 reshape.37
  239.4 0.2 copy.19
  239.6 1.1 fusion.2
  240.6 0.0 copy-start
  240.6 7.4 %finish.1 = (bf16[96,2,256,128]{3,2,1,0:T(8,128)(2,1)}, bf16[96,2,256,128]{3,2,1,0:T(8,128)(2,1)}) custom-call(s32[4]{0:T(128)} %get-tuple-element.206.meta, s32[2,65]{1,0:T(2,128)} %get-tuple-element.218.refs_0_.moved, s32[3,129]{1,0:T(4,128)} %get-tuple-element.225.rows, ...), custom_call_target="tpu_custom_call", output_to_operand_aliasing={{0}: (6, {}), {1}: (7, {})} | custom-call | flops 10000000000 | bytes 16777216 | tf_op jit(solution)/shard_map/finish/pallas_call | solution.py:805
  248.1 0.0 copy-done
  248.1 0.7 constant_dynamic-slice_fusion
Async XLA Ops:
  21.4 15.7 %copy-start.1 = (s32[4]{0:T(128)S(1)}, s32[4]{0:T(128)}, u32[]{:S(2)}) copy-start(s32[4]{0:T(128)} %get-tuple-element.206.meta) | copy-start | bytes 52
  240.6 7.5 %copy-start = (bf16[64,4096]{1,0:T(8,128)(2,1)S(1)}, bf16[64,4096]{1,0:T(8,128)(2,1)}, u32[]{:S(2)}) copy-start(bf16[64,4096]{1,0:T(8,128)(2,1)} %get-tuple-element.244) | copy-start | bytes 1572868

commit v4 on v3

--- a/solution.py
+++ b/solution.py
@@ -161,7 +161,7 @@
     )(h, wq, wk, wv)
 
 
-def plan_kernel(new_table, seq_lens, mig_src, mig_dst, meta, items, slots, moved, rows, source, place_of, counts):
+def plan_kernel(new_table, seq_lens, mig_src, mig_dst, meta, items, slots, gone, moved, rows, source, place_of, counts):
     me = lax.axis_index('kv')
     base = me * SLOTS
 
@@ -184,7 +184,7 @@
     lax.fori_loop(0, SLOTS, keep, 0, unroll=16)
 
     def entry(e, carry):
-        n, even, odd = carry
+        n, m, even, odd = carry
         s, d = mig_src[e], mig_dst[e]
         hs, hd = home(s), home(d)
         pair = hs * 4 + hd
@@ -199,13 +199,14 @@
         odd = odd | misfit | (1 - (hs & 1))
 
         slots[jnp.where(hs == me, s - base, SLOTS)] = 1
-        slots[jnp.where(hd == me, d - base, SLOTS)] = 2
+        slots[jnp.where(hd == me, d - base, SLOTS)] = 1
+        gone[m] = s - base
         moved[0, n] = d - base
         moved[1, n] = place
-        return n + (hd == me).astype(jnp.int32), even, odd
+        return n + (hd == me).astype(jnp.int32), m + (hs == me).astype(jnp.int32), even, odd
 
     zero = jnp.int32(0)
-    n_moved, even, odd = lax.fori_loop(0, MIG, entry, (zero, zero, zero), unroll=4)
+    n_moved, n_gone, even, odd = lax.fori_loop(0, MIG, entry, (zero, zero, zero, zero), unroll=8)
 
     def sequence(b, carry):
         n, m = carry
@@ -220,8 +221,8 @@
             own.append(mine)
             place.append(jnp.where(mine, place_of[slot], -1))
         items[0, n] = b
-        items[1, n] = jnp.where(own[0], local[0], local[1])
-        items[2, n] = jnp.where(own[1], local[1], local[0])
+        items[1, n] = jnp.where(own[0], local[0], -1)
+        items[2, n] = jnp.where(own[1], local[1], -1)
         items[3, n] = jnp.where(own[0], jnp.minimum(length, PAGE), 0)
         items[4, n] = jnp.where(own[1], jnp.maximum(length - PAGE, 0), 0)
         items[5, n] = place[0]
@@ -236,7 +237,7 @@
             m = m + ((here >= 0) & (here < SLOTS)).astype(jnp.int32)
         return n + (own[0] | own[1]).astype(jnp.int32), m
 
-    n_items, n_rows = lax.fori_loop(0, SEQS, sequence, (zero, zero), unroll=4)
+    n_items, n_rows = lax.fori_loop(0, SEQS, sequence, (zero, zero), unroll=8)
 
     @pl.when(n_items > 0)
     def _():
@@ -249,10 +250,11 @@
     meta[1] = jnp.where(even == 0, 0, jnp.where(odd == 0, 1, 2))
     meta[2] = n_moved
     meta[3] = n_rows
+    meta[4] = n_gone
 
 
 def run_plan(new_table, seq_lens, mig_src, mig_dst):
-    shapes = [(4,), (7, SEQS + UNROLL), (SLOTS + 1,), (2, MIG + 1), (3, 2 * SEQS + 1)]
+    shapes = [(5,), (7, SEQS + UNROLL), (SLOTS + 1,), (MIG + 1,), (2, MIG + 1), (3, 2 * SEQS + 1)]
     return pl.pallas_call(
         plan_kernel,
         name='plan',
@@ -263,27 +265,33 @@
     )(new_table.T, seq_lens, mig_src, mig_dst)
 
 
-NBUF = 3
+NBUF = 6
+AFTER = 2
+DIST = NBUF - AFTER
 STEPS = SEQS // UNROLL
 SLOTS_STEP = SLOTS // STEPS
 
 
 def attend_kernel(layer, meta, table, slots, q_all, k_pool, v_pool, *refs):
     if layer == 0:
-        part_o, part_l, outbox, pool_out, q_rows, kbuf, vbuf, ring, zeros, sems, out_sems, ring_in, ring_out = refs
+        part_o, part_l, outbox, pool_out, *refs = refs
     else:
-        moved, inbox, _, part_o, part_l, outbox, pool_out, k_out, q_rows, kbuf, vbuf, ring, zeros, sems, out_sems, ring_in, ring_out, pages, page_in, page_out = refs
+        moved, inbox, spare, _, part_o, part_l, outbox, pool_out, k_out, *refs, pages, page_in, page_out = refs
+    q_rows, kbuf, vbuf, ring, sems, out_sems, ring_in, ring_out = refs
+    pool = (k_pool, v_pool)[layer]
     groups = (meta[0] + UNROLL - 1) // UNROLL
-    pool = (k_pool, v_pool)[layer]
 
     def copies(g, start):
         slot = lax.rem(g, NBUF)
         for u in range(UNROLL):
             for j in range(2):
                 page = table[1 + j, g * UNROLL + u]
-                for ref, buf in ((k_pool, kbuf), (v_pool, vbuf)):
-                    copy = pltpu.make_async_copy(ref.at[page, layer], buf.at[slot, u, j], sems.at[slot])
-                    copy.start() if start else copy.wait()
+
+                @pl.when(page >= 0)
+                def _():
+                    for ref, buf in ((k_pool, kbuf), (v_pool, vbuf)):
+                        copy = pltpu.make_async_copy(ref.at[page, layer], buf.at[slot, u, j], sems.at[slot])
+                        copy.start() if start else copy.wait()
 
     def packs(g, start):
         slot = lax.rem(g, NBUF)
@@ -301,49 +309,43 @@
         place = lax.rem(s, NBUF)
         for i in range(SLOTS_STEP):
             slot = s * SLOTS_STEP + i
-            state = slots[slot]
-
-
-            def load():
-                return pltpu.make_async_copy(pool.at[slot], ring.at[place, i], ring_in.at[place, i])
-
-            def store():
-                return pltpu.make_async_copy(ring.at[place, i], pool_out.at[slot], ring_out.at[place, i])
-
-            if phase == 'load':
-                pl.when(state == 0)(lambda: load().start())
-            elif phase == 'store':
-                @pl.when(state == 0)
-                def _():
-                    load().wait()
-                    store().start()
-
-                @pl.when(state == 1)
-                def _():
-                    pltpu.make_async_copy(zeros, pool_out.at[slot], ring_out.at[place, i]).start()
-            else:
-                pl.when(state < 2)(lambda: store().wait())
+
+            @pl.when(slots[slot] == 0)
+            def _():
+                if phase < 2:
+                    load = pltpu.make_async_copy(pool.at[slot], ring.at[place, i], ring_in.at[place, i])
+                    load.wait() if phase else load.start()
+                if phase > 0:
+                    store = pltpu.make_async_copy(ring.at[place, i], pool_out.at[slot], ring_out.at[place, i])
+                    store.start() if phase == 1 else store.wait()
 
     def settle(phase):
         def one(i, carry):
-            for p, dst in enumerate((k_out, pool_out)):
-                if phase < 2:
-                    copy = pltpu.make_async_copy(inbox.at[moved[1, i], p], pages.at[i, p], page_in)
-                else:
-                    copy = pltpu.make_async_copy(pages.at[i, p], dst.at[moved[0, i], 0], page_out)
-                copy.wait() if phase % 2 else copy.start()
+            def move(box):
+                for p, dst in enumerate((k_out, pool_out)):
+                    if phase < 2:
+                        copy = pltpu.make_async_copy(box.at[moved[1, i], p], pages.at[i, p], page_in)
+                    else:
+                        copy = pltpu.make_async_copy(pages.at[i, p], dst.at[moved[0, i], 0], page_out)
+                    copy.wait() if phase % 2 else copy.start()
+
+            if phase:
+                move(inbox)
+            else:
+                pl.when(meta[1] < 2)(lambda: move(inbox))
+                pl.when(meta[1] == 2)(lambda: move(spare))
             return carry
 
         lax.fori_loop(0, meta[2], one, 0)
 
-    for g in range(NBUF - 1):
-        @pl.when(g < groups)
-        def _():
-            copies(g, True)
-        keep(g, 'load')
     if layer == 1:
         settle(0)
-    zeros[...] = jnp.zeros_like(zeros)
+    vbuf[...] = jnp.zeros_like(vbuf)
+    for g in range(DIST):
+        @pl.when(g < groups)
+        def _():
+            copies(g, True)
+        keep(g, 0)
     part_o[...] = jnp.zeros_like(part_o)
     part_l[...] = jnp.full_like(part_l, NEG)
 
@@ -386,7 +388,7 @@
                     part_l[seq // 32, half, t * 32 + seq % 32] = lse[rows]
 
     def step(g, carry):
-        keep(g, 'store')
+        keep(g, 1)
         if layer == 1:
             @pl.when(g == STEPS // 2)
             def _():
@@ -398,21 +400,21 @@
             copies(g, False)
             packs(g, True)
 
-        @pl.when(g > 0)
-        def _():
-            keep(g - 1, 'drain')
-
-        @pl.when((g > 0) & (g <= groups))
-        def _():
-            packs(g - 1, False)
-
-        @pl.when(g + NBUF - 1 < STEPS)
-        def _():
-            keep(g + NBUF - 1, 'load')
-
-        @pl.when(g + NBUF - 1 < groups)
-        def _():
-            copies(g + NBUF - 1, True)
+        @pl.when(g >= AFTER)
+        def _():
+            keep(g - AFTER, 2)
+
+        @pl.when((g >= AFTER) & (g - AFTER < groups))
+        def _():
+            packs(g - AFTER, False)
+
+        @pl.when(g + DIST < STEPS)
+        def _():
+            keep(g + DIST, 0)
+
+        @pl.when(g + DIST < groups)
+        def _():
+            copies(g + DIST, True)
 
         @pl.when(g < groups)
         def _():
@@ -420,13 +422,14 @@
         return carry
 
     lax.fori_loop(0, STEPS, step, 0)
-    keep(STEPS - 1, 'drain')
+    for g in range(STEPS - AFTER, STEPS):
+        keep(g, 2)
+
+        @pl.when(g < groups)
+        def _():
+            packs(g, False)
     if layer == 1:
         settle(3)
-
-    @pl.when(groups == STEPS)
-    def _():
-        packs(groups - 1, False)
 
 
 def run_attend(layer, meta, table, slots, q_all, k_flat, v_flat, extra=()):
@@ -436,15 +439,14 @@
         functools.partial(attend_kernel, layer),
         name=f'attend{layer}',
         out_shape=[shape, shape, BOX] + [jax.ShapeDtypeStruct(k_flat.shape, BF16)] * (layer + 1),
-        in_specs=[SMEM, SMEM, SMEM, VMEM, ANY, ANY] + [SMEM, ANY, ANY] * layer,
+        in_specs=[SMEM, SMEM, SMEM, VMEM, ANY, ANY] + [SMEM, ANY, ANY, ANY] * layer,
         out_specs=[VMEM, VMEM, ANY, ANY] + [ANY] * layer,
-        input_output_aliases={8: 4} if layer else {},
+        input_output_aliases={9: 4} if layer else {},
         scratch_shapes=[
             pltpu.VMEM((2 * TOK * HEADS, HEAD), F32),
             pltpu.VMEM((NBUF,) + page, BF16),
             pltpu.VMEM((NBUF,) + page, BF16),
             pltpu.VMEM((NBUF, SLOTS_STEP) + k_flat.shape[1:], BF16),
-            pltpu.VMEM(k_flat.shape[1:], BF16),
             DMA((NBUF,)),
             DMA((NBUF,)),
             DMA((NBUF, SLOTS_STEP)),
@@ -463,7 +465,8 @@
     return out, top + jnp.log(total)
 
 
-MODES = ([((0,), 2, FAST_PAGES), ((0,), 0, FAST_PAGES)], [((1,), 2, FAST_PAGES), ((1,), 0, FAST_PAGES)], [((0, 1), i, MIG) for i in range(3)])
+LANES = ([((0,), 2, FAST_PAGES), ((0,), 0, FAST_PAGES)], [((1,), 2, FAST_PAGES), ((1,), 0, FAST_PAGES)])
+EVERYTHING = [((0, 1), i, MIG) for i in range(3)]
 CHUNK = 2
 
 
@@ -498,21 +501,29 @@
         self.each(False, lambda copy: copy.wait_recv())
 
 
-RING_W = 20
+RING_W = 18
 TK = 2048
 UP_TILES = FF // 2 // TN
 TD = FF // 8
 OUT_END = D // TN
 UP_END = OUT_END + 2 * UP_TILES
-ALL_TILES = UP_END + 4 * (D // TN)
+DOWN_END = UP_END + 4 * (D // TN)
+QKV_END = DOWN_END + 12
 PART = TOK // 2
 
 
-def rest_kernel(layer, mode, h_in, q_all, kv, part_o, part_l, wo, w_up, w_down, outbox, out, kv_all, inbox, ring, ring_sem, own_o, own_l, own_sem,
-                got_o, got_l, mine_o, mine_l, give_o, give_l, far_o, far_l, q_rows, k_rows, v_rows, attn, act, h, psend, precv,
-                dsend, drecv, xsend, xrecv, ssem, rsem, ksend, krecv, bsend, brecv):
+def rest_kernel(layer, lane_core, h_in, q_all, kv, part_o, part_l, wo, w_up, w_down, outbox, *refs):
+    last = layer == LAYERS - 1
+    if last:
+        out, kv_all, inbox, *refs = refs
+    else:
+        wq, wk, wv, out, kv_all, inbox, q_next, kv_next, *refs = refs
+        *refs, qp_send, qp_recv, qx_send, qx_recv, qf_send, qf_recv = refs
+    (ring, ring_sem, own_o, own_l, own_sem, got_o, got_l, mine_o, mine_l, give_o, give_l, far_o, far_l, q_rows, k_rows, v_rows, attn, act, h,
+     psend, precv, dsend, drecv, xsend, xrecv, ssem, rsem, ksend, krecv, bsend, brecv) = refs
     me, chip, core, partner, across, diag = places()
-    boxes = Boxes(MODES[mode], outbox, inbox, bsend, brecv)
+    boxes = Boxes(LANES[lane_core], outbox, inbox, bsend, brecv)
+    end = DOWN_END if last else QKV_END
 
     def tile_copy(t, kind):
         slot = lax.rem(t, RING_W)
@@ -521,6 +532,13 @@
         elif kind == 1:
             i = t - OUT_END
             src = w_up.at[layer, pl.ds(pl.multiple_of(lax.rem(i, 2) * TK, TK), TK), pl.ds(pl.multiple_of(core * (FF // 2) + (i // 2) * TN, TN), TN)]
+        elif kind >= 3:
+            i = t - DOWN_END
+            rows = pl.ds(pl.multiple_of(lax.rem(i, 2) * TK, TK), TK)
+            if kind == 3:
+                src = wq.at[layer + 1, rows, pl.ds(pl.multiple_of(core * 2048 + (i // 2) * TN, TN), TN)]
+            else:
+                src = (wk, wv)[kind - 4].at[layer + 1, rows, pl.ds(pl.multiple_of(core * TN, TN), TN)]
         else:
             i = t - UP_END
             src = w_down.at[layer, pl.ds(pl.multiple_of(core * (FF // 2) + lax.rem(i, 4) * TD, TD), TD), pl.ds(pl.multiple_of((i // 4) * TN, TN), TN)]
@@ -530,7 +548,11 @@
     def fetch(t):
         pl.when(t < OUT_END)(lambda: tile_copy(t, 0).start())
         pl.when((t >= OUT_END) & (t < UP_END))(lambda: tile_copy(t, 1).start())
-        pl.when((t >= UP_END) & (t < ALL_TILES))(lambda: tile_copy(t, 2).start())
+        pl.when((t >= UP_END) & (t < DOWN_END))(lambda: tile_copy(t, 2).start())
+        if not last:
+            pl.when((t >= DOWN_END) & (t < DOWN_END + 8))(lambda: tile_copy(t, 3).start())
+            pl.when((t >= DOWN_END + 8) & (t < DOWN_END + 10))(lambda: tile_copy(t, 4).start())
+            pl.when((t >= DOWN_END + 10) & (t < QKV_END))(lambda: tile_copy(t, 5).start())
 
     own, near = [], []
     for which, (owner, first, size) in enumerate(((1 - chip, 0, PART), (1 - chip, PART, PART), (chip, 0, TOK))):
@@ -691,6 +713,54 @@
 
     lax.fori_loop(0, D // TN, down, 0)
     finish_sum(8, h, out)
+
+    if not last:
+        def to_partner(j):
+            ref = q_next.at[chip, core * 4 + j]
+            return send(ref, ref, qp_send.at[j], qp_recv.at[j], partner)
+
+        def to_across(j):
+            ref = q_next.at[chip, core * 4 + j]
+            return send(ref, ref, qx_send.at[j], qx_recv.at[j], across)
+
+        def forward(j):
+            ref = q_next.at[1 - chip, core * 4 + j]
+            return send(ref, ref, qf_send.at[j], qf_recv.at[j], partner)
+
+        def project_next(j, kind):
+            total = None
+            for k in range(2):
+                t = DOWN_END + 2 * j + k
+                tile_copy(t, kind).wait()
+                part = dot(out[:, k * TK:(k + 1) * TK], ring[lax.rem(t, RING_W)])
+                total = part if total is None else total + part
+            return total.astype(BF16)
+
+        def query(j, carry):
+            q_next[chip, core * 4 + j] = project_next(j, 3)
+
+            @pl.when(j > 0)
+            def _():
+                to_across(j - 1).start()
+                to_partner(j - 1).start()
+            return carry
+
+        lax.fori_loop(0, 4, query, 0)
+        to_across(3).start()
+        to_partner(3).start()
+
+        def key_value(j, carry):
+            kv_next[:, pl.ds(pl.multiple_of(j * TN, TN), TN)] = project_next(j + 4, 4)
+            return carry
+
+        lax.fori_loop(0, 2, key_value, 0)
+        for j in range(4):
+            to_across(j).wait_recv()
+            forward(j).start()
+        for j in range(4):
+            to_across(j).wait_send()
+            to_partner(j).wait()
+            forward(j).wait()
     for j in range(16):
         reduce(j).wait_send()
     for pair in near + far:
@@ -702,14 +772,15 @@
     boxes.wait()
 
 
-def run_rest(layer, mode, h, q_all, kv, part_o, part_l, outbox, w_out, w_up, w_down):
+def run_rest(layer, lane_core, h, q_all, kv, part_o, part_l, outbox, w_out, w_up, w_down, *weights):
+    more = [jax.ShapeDtypeStruct((2, 8, TOK, TN), BF16), jax.ShapeDtypeStruct((TOK, 2 * TN), BF16)] if weights else []
     token = (HALF_HEADS, HEAD)
     return pl.pallas_call(
-        functools.partial(rest_kernel, layer, mode),
-        name=f'rest{layer}_{mode}',
-        out_shape=[jax.ShapeDtypeStruct((TOK, D), BF16), jax.ShapeDtypeStruct((4, TOK, 2 * TN), BF16), BOX],
-        in_specs=[VMEM] * 3 + [ANY] * 6,
-        out_specs=[VMEM, VMEM, ANY],
+        functools.partial(rest_kernel, layer, lane_core),
+        name=f'rest{layer}_{lane_core}',
+        out_shape=[jax.ShapeDtypeStruct((TOK, D), BF16), jax.ShapeDtypeStruct((4, TOK, 2 * TN), BF16), BOX] + more,
+        in_specs=[VMEM] * 3 + [ANY] * (6 + len(weights)),
+        out_specs=[VMEM, VMEM, ANY] + [VMEM] * len(more),
         scratch_shapes=[
             pltpu.VMEM((RING_W, TK, TN), BF16),
             DMA((RING_W,)),
@@ -742,24 +813,54 @@
             DMA((3,)),
             DMA((3, MIG // CHUNK)),
             DMA((3, MIG // CHUNK)),
-        ],
+        ] + [DMA((4,))] * (6 if weights else 0),
         cost_estimate=pl.CostEstimate(flops=2 * TOK * D * FF * 8, bytes_accessed=D * FF * 2, transcendentals=0),
-        compiler_params=pltpu.CompilerParams(collective_id=2 + layer * 3 + mode, has_side_effects=True, vmem_limit_bytes=67043328),
-    )(h, q_all, kv, part_o, part_l, w_out, w_up, w_down, outbox)
+        compiler_params=pltpu.CompilerParams(collective_id=2 + layer * 2 + lane_core, has_side_effects=True, vmem_limit_bytes=67043328),
+    )(h, q_all, kv, part_o, part_l, w_out, w_up, w_down, outbox, *weights)
+
+
+def move_kernel(outbox, inbox, send_sems, recv_sems):
+    me, chip, core, partner, across, diag = places()
+    meet((partner, across, diag))
+    boxes = Boxes(EVERYTHING, outbox, inbox, send_sems, recv_sems)
+    boxes.start()
+    boxes.wait()
+
+
+def run_move(layer, outbox):
+    return pl.pallas_call(
+        move_kernel,
+        name=f'move{layer}',
+        out_shape=BOX,
+        in_specs=[ANY],
+        out_specs=ANY,
+        scratch_shapes=[DMA((3, MIG // CHUNK)), DMA((3, MIG // CHUNK))],
+        compiler_params=pltpu.CompilerParams(collective_id=6 + layer, has_side_effects=True),
+    )(outbox)
+
+
+def run_blank(layer):
+    return pl.pallas_call(lambda box: None, name=f'blank{layer}', out_shape=BOX, out_specs=ANY)()
 
 
 RING = 32
 AHEAD = RING // 2
 
 
-def finish_kernel(meta, moved, rows, inbox, k_rows, v_rows, k_in, v_in, k_out, v_out, buf, in_sem, out_sem, row_sem):
+def finish_kernel(meta, moved, gone, rows, inbox, spare, kv0, kv1, k_in, v_in, k_out, v_out, wide, row_buf, zeros, buf, in_sem, out_sem, zero_sem, row_sem):
     del k_in, v_in
     outs = (k_out, v_out)
     count = meta[2]
 
-    def load(i):
+    def loop(first, last, body):
+        lax.fori_loop(first, last, lambda i, carry: (body(i), carry)[1], 0)
+
+    def clear(i):
+        return [pltpu.make_async_copy(zeros, out.at[gone[i]], zero_sem) for out in outs]
+
+    def load(i, box):
         slot = lax.rem(i, RING)
-        return [pltpu.make_async_copy(inbox.at[moved[1, i], p], buf.at[slot, p], in_sem.at[slot, p]) for p in range(2)]
+        return [pltpu.make_async_copy(box.at[moved[1, i], p], buf.at[slot, p], in_sem.at[slot, p]) for p in range(2)]
 
     def store(i):
         slot = lax.rem(i, RING)
@@ -773,13 +874,24 @@
         for copy in group:
             copy.wait()
 
-    def loop(first, last, body):
-        lax.fori_loop(first, last, lambda i, carry: (body(i), carry)[1], 0)
-
-    loop(0, jnp.minimum(count, AHEAD), lambda i: begin(load(i)))
+    def begin_load(i):
+        pl.when(meta[1] < 2)(lambda: begin(load(i, inbox)))
+        pl.when(meta[1] == 2)(lambda: begin(load(i, spare)))
+
+    loop(0, jnp.minimum(count, AHEAD), begin_load)
+    zeros[...] = jnp.zeros_like(zeros)
+    loop(0, meta[4], lambda i: begin(clear(i)))
+
+    for l, kv in enumerate((kv0, kv1)):
+        for p in range(2):
+            for dev in range(4):
+                for i in range(4):
+                    at = pl.ds((dev // 2) * TOK * KV_HEADS + (dev % 2) * 4 + i, TOK, stride=KV_HEADS)
+                    wide[at, :] = kv[dev, :, (p * 4 + i) * HEAD:(p * 4 + i + 1) * HEAD].astype(F32)
+            row_buf[p, l] = wide[...].astype(BF16)
 
     def page(i):
-        end(load(i))
+        end(load(i, inbox))
         begin(store(i))
 
         @pl.when(i + AHEAD < count)
@@ -787,42 +899,43 @@
             @pl.when(i >= AHEAD)
             def _():
                 end(store(i - AHEAD))
-            begin(load(i + AHEAD))
+            begin_load(i + AHEAD)
 
     loop(0, count, page)
     loop(jnp.maximum(count - RING, 0), count, lambda i: end(store(i)))
 
     def row(i):
         at = pl.ds(pl.multiple_of(rows[1, i] * KV_HEADS, KV_HEADS), KV_HEADS)
-        return [pltpu.make_async_copy(src.at[l, rows[2, i]], outs[p].at[rows[0, i], l, at, :], row_sem.at[p, l]) for p, src in enumerate((k_rows, v_rows)) for l in range(LAYERS)]
+        src = pl.ds(pl.multiple_of(rows[2, i] * KV_HEADS, KV_HEADS), KV_HEADS)
+        return [pltpu.make_async_copy(row_buf.at[p, l, src, :], outs[p].at[rows[0, i], l, at, :], row_sem.at[p, l]) for p in range(2) for l in range(LAYERS)]
 
     loop(0, meta[3], lambda i: begin(row(i)))
     loop(0, meta[3], lambda i: end(row(i)))
-
-
-def run_finish(meta, moved, rows, inbox, k_rows, v_rows, k_part, v_part):
+    loop(0, meta[4], lambda i: end(clear(i)))
+
+
+def run_finish(meta, moved, gone, rows, boxes, kvs, k_part, v_part):
     shape = jax.ShapeDtypeStruct(k_part.shape, BF16)
     return pl.pallas_call(
         finish_kernel,
         name='finish',
         out_shape=[shape, shape],
-        in_specs=[SMEM, SMEM, SMEM, ANY, VMEM, VMEM, ANY, ANY],
+        in_specs=[SMEM] * 4 + [ANY, ANY, VMEM, VMEM, ANY, ANY],
         out_specs=[ANY, ANY],
         scratch_shapes=[
+            pltpu.VMEM((2 * TOK * KV_HEADS, HEAD), F32),
+            pltpu.VMEM((2, LAYERS, 2 * TOK * KV_HEADS, HEAD), BF16),
+            pltpu.VMEM(k_part.shape[1:], BF16),
             pltpu.VMEM((RING, 2) + k_part.shape[2:], BF16),
             DMA((RING, 2)),
             DMA((RING, 2)),
+            DMA,
             DMA((2, LAYERS)),
         ],
-        input_output_aliases={6: 0, 7: 1},
+        input_output_aliases={8: 0, 9: 1},
         cost_estimate=pl.CostEstimate(flops=10 ** 10, bytes_accessed=16 * 2 ** 20, transcendentals=0),
         compiler_params=pltpu.CompilerParams(vmem_limit_bytes=VMEM_LIMIT),
-    )(meta, moved, rows, inbox, k_rows, v_rows, k_part, v_part)
-
-
-def by_token(kv_all):
-    x = kv_all.reshape(2, 2, TOK, 2, 4, HEAD)
-    return x.transpose(3, 0, 2, 1, 4, 5).reshape(2, 2 * TOK, KV_HEADS, HEAD)
+    )(meta, moved, gone, rows, *boxes, *kvs, k_part, v_part)
 
 
 def solution(mesh):
@@ -833,22 +946,21 @@
         me = lax.axis_index('kv')
         weights = (w_query, w_key, w_value)
         k_flat, v_flat = flat_pool(k_pool), flat_pool(v_pool)
-        meta, items, slots, moved, where = run_plan(new_table, seq_lens, mig_src, mig_dst)
-        rows = []
-        h = None
+        meta, items, slots, gone, moved, where = run_plan(new_table, seq_lens, mig_src, mig_dst)
+        lane_core = jnp.minimum(meta[1], 1)
+        q_all, kv, h = run_qkv(0, embeds, weights, True)
+        kvs, boxes, pools = [], (), ()
         for layer in range(LAYERS):
-            if layer == 0:
-                q_all, kv, h = run_qkv(layer, embeds, weights, True)
-            else:
-                q_all, kv = run_qkv(layer, h, weights, False)
-            extra = (moved, inbox, pools[0]) if layer else ()
+            extra = (moved, *boxes, *pools) if layer else ()
             part_o, part_l, outbox, *pools = run_attend(layer, meta, items, slots, q_all, k_flat, v_flat, extra)
-
-            forms = [functools.partial(run_rest, layer, mode) for mode in range(len(MODES))]
-            h, kv_all, inbox = lax.switch(meta[1], forms, h, q_all, kv, part_o, part_l, outbox, w_out, w_up, w_down)
-            rows.append(by_token(kv_all))
-        rows = jnp.stack(rows)
-        k_out, v_out = run_finish(meta, moved, where, inbox, rows[:, 0], rows[:, 1], pools[1], pools[0])
+            forms = [functools.partial(run_rest, layer, core) for core in range(2)]
+            more = weights if layer == 0 else ()
+            h, kv_all, inbox, *more = lax.switch(lane_core, forms, h, q_all, kv, part_o, part_l, outbox, w_out, w_up, w_down, *more)
+            kvs.append(kv_all)
+            if more:
+                q_all, kv = more
+            boxes = inbox, lax.cond(meta[1] == 2, functools.partial(run_move, layer), lambda box: run_blank(layer), outbox)
+        k_out, v_out = run_finish(meta, moved, gone, where, boxes, kvs, pools[1], pools[0])
         k_out, v_out = k_out.reshape(k_pool.shape), v_out.reshape(v_pool.shape)
         y = lax.dynamic_slice_in_dim(h.reshape(2, 32, D), (me % 2) * 16, 16, axis=1)
         return y, k_out, v_out

time: 249 us -> 242 us (0.972)
  the two profiles are of different devices: /device:TPU:6 before, /device:TPU:5 now
where the time goes in v4:
time: 242 us; the launch traced here: 240 us
  Pallas kernels  233 us (96%)
  local copies, waits for them, and re-layouts  4.08 us (2%)
    pallas_call x2, Pallas kernels, run_rest(): pl.pallas_call(functools.partial(rest_kernel, layer, lane_core), name=f'r...  177 us
    pallas_call x2, Pallas kernels, run_attend(): pl.pallas_call(functools.partial(attend_kernel, layer), name=f'attend{lay...  27.7 us
    pallas_call x1, Pallas kernels, run_qkv(): pl.pallas_call(functools.partial(qkv_kernel, layer, first), name=f'qkv{la...  16.2 us
    pallas_call x1, Pallas kernels, run_finish(): pl.pallas_call(finish_kernel, name='finish', out_shape=[shape, shape], in...  6.95 us
    pallas_call x1, Pallas kernels, run_plan(): pl.pallas_call(plan_kernel, name='plan', out_shape=[jax.ShapeDtypeStruct(...  5.7 us

profile of v4, /device:TPU:5, one launch (start us, length us, event | category | flops | bytes accessed | tf_op | source)
XLA Modules:
  0.0 239.6 jit_solution(16692102033313289550)
XLA Ops:
  0.6 5.7 %plan.1 = (s32[5]{0:T(128)}, s32[7,68]{1,0:T(8,128)}, s32[97]{0:T(128)}, s32[65]{0:T(128)}, s32[2,65]{1,0:T(2,128)}, /*index=5*/s32[3,129]{1,0:T(4,128)}) custom-call(s32[2,64]{1,0:T(2,128)} %bitcast.15, s32[64]{0:T(128)} %seq_lens.1, s32[64]{0:T(128)} %mig_src.1, s32[64]{0:T(128)} %mig_dst.1), custom_call_target="tpu_custom_call" | custom-call | tf_op jit(solution)/shard_map/plan/pallas_call | solution.py:258
  6.4 1.2 slice.2
  8.9 16.2 %qkv0.1 = (bf16[2,8,64,512]{3,2,1,0:T(8,128)(2,1)}, bf16[64,1024]{1,0:T(8,128)(2,1)}, bf16[64,4096]{1,0:T(8,128)(2,1)}) custom-call(bf16[2,16,4096]{2,1,0:T(8,128)(2,1)} %refs_0_.1, bf16[2,4096,4096]{2,1,0:T(8,128)(2,1)} %refs_1_.1, bf16[2,4096,1024]{2,1,0:T(8,128)(2,1)} %refs_2_.1, bf16[2,4096,1024]{2,1,0:T(8,128)(2,1)} %refs_3_.1), custom_call_target="tpu_custom_call" | custom-call | flops 12884901888 | bytes 25165824 | tf_op jit(solution)/shard_map/qkv0/pallas_call | solution.py:152
  25.0 13.0 %attend0.1 = (f32[2,2,64,16,128]{4,3,2,1,0:T(8,128)}, f32[2,2,64,16,128]{4,3,2,1,0:T(8,128)}, bf16[192,2,256,128]{3,2,1,0:T(8,128)(2,1)}, bf16[96,2,256,128]{3,2,1,0:T(8,128)(2,1)}) custom-call(s32[5]{0:T(128)} %get-tuple-element.176.meta, s32[7,68]{1,0:T(8,128)} %get-tuple-element.180.table, s32[97]{0:T(128)} %get-tuple-element.181.slots, ...), custom_call_target="tpu_custom_call" | custom-call | flops 20000000000 | bytes 16777216 | tf_op jit(solution)/shard_map/attend0/pallas_call | solution.py:438
  38.0 94.0 %conditional.4 = ((bf16[64,4096]{1,0:T(8,128)(2,1)}, bf16[4,64,1024]{2,1,0:T(8,128)(2,1)}, bf16[192,2,256,128]{3,2,1,0:T(8,128)(2,1)}, bf16[2,8,64,512]{3,2,1,0:T(8,128)(2,1)}, bf16[64,1024]{1,0:T(8,128)(2,1)})) conditional(s32[]{:T(128)} %bitcast.1, (bf16[64,4096]{1,0:T(8,128)(2,1)}, bf16[2,8,64,512]{3,2,1,0:T(8,128)(2,1)}, ...), branch_computations={%region_0.0_spmd, %region_1.0_spmd} | conditional | flops 60129542144 | bytes 117440520 | solution.py:958
  38.0 93.7 %rest0_0.1 = (bf16[64,4096]{1,0:T(8,128)(2,1)}, bf16[4,64,1024]{2,1,0:T(8,128)(2,1)}, bf16[192,2,256,128]{3,2,1,0:T(8,128)(2,1)}, bf16[2,8,64,512]{3,2,1,0:T(8,128)(2,1)}, bf16[64,1024]{1,0:T(8,128)(2,1)}) custom-call(bf16[64,4096]{1,0:T(8,128)(2,1)} %get-tuple-element.103.h_in, bf16[2,8,64,512]{3,2,1,0:T(8,128)(2,1)} %get-tuple-element.104.q_all, ...), custom_call_target="tpu_custom_call" | custom-call | flops 60129542144 | bytes 117440512 | tf_op jit(solution)/shard_map/cond/branch_0_fun/rest0_0/pallas_call | solution.py:778
  132.0 14.7 %attend1.1 = (f32[2,2,64,16,128]{4,3,2,1,0:T(8,128)}, f32[2,2,64,16,128]{4,3,2,1,0:T(8,128)}, bf16[192,2,256,128]{3,2,1,0:T(8,128)(2,1)}, bf16[96,2,256,128]{3,2,1,0:T(8,128)(2,1)}, bf16[96,2,256,128]{3,2,1,0:T(8,128)(2,1)}) custom-call(s32[5]{0:T(128)} %get-tuple-element.176.meta, ...), custom_call_target="tpu_custom_call", output_to_operand_aliasing={{4}: (9, {})} | custom-call | flops 20000000000 | bytes 16777216 | tf_op jit(solution)/shard_map/attend1/pallas_call | solution.py:438
  146.7 82.9 %conditional.6 = ((bf16[64,4096]{1,0:T(8,128)(2,1)}, bf16[4,64,1024]{2,1,0:T(8,128)(2,1)}, bf16[192,2,256,128]{3,2,1,0:T(8,128)(2,1)})) conditional(s32[]{:T(128)} %bitcast.1, (bf16[64,4096]{1,0:T(8,128)(2,1)}, bf16[2,8,64,512]{3,2,1,0:T(8,128)(2,1)}, bf16[64,1024]{1,0:T(8,128)(2,1)}, f32[2,2,64,16,128]{4,3,2,1,0:T(8,128)}, ...), branch_computations={%region_4.0_spmd, %region_5.0_spmd} | conditional | flops 60129542144 | bytes 117440520 | solution.py:958
  146.7 82.8 %rest1_0.1 = (bf16[64,4096]{1,0:T(8,128)(2,1)}, bf16[4,64,1024]{2,1,0:T(8,128)(2,1)}, bf16[192,2,256,128]{3,2,1,0:T(8,128)(2,1)}) custom-call(bf16[64,4096]{1,0:T(8,128)(2,1)} %get-tuple-element.127.h_in, bf16[2,8,64,512]{3,2,1,0:T(8,128)(2,1)} %get-tuple-element.128.q_all, bf16[64,1024]{1,0:T(8,128)(2,1)} %get-tuple-element.129.kv, ...), custom_call_target="tpu_custom_call" | custom-call | flops 60129542144 | bytes 117440512 | tf_op jit(solution)/shard_map/cond/branch_0_fun/rest1_0/pallas_call | solution.py:778
  229.6 1.7 constant_dynamic-slice_fusion
  231.3 0.0 copy-start
  231.3 0.0 copy-start.1
  231.3 1.0 copy-done
  232.3 0.2 copy-done.1
  232.5 6.9 %finish.1 = (bf16[96,2,256,128]{3,2,1,0:T(8,128)(2,1)}, bf16[96,2,256,128]{3,2,1,0:T(8,128)(2,1)}) custom-call(s32[5]{0:T(128)} %get-tuple-element.176.meta, s32[2,65]{1,0:T(2,128)} %get-tuple-element.188.refs_0_.moved, s32[65]{0:T(128)} %get-tuple-element.195.gone, s32[3,129]{1,0:T(4,128)} %get-tuple-element.196.rows, ...), custom_call_target="tpu_custom_call", output_to_operand_aliasing={{0}: (8, {}), {1}: (9, {})} | custom-call | flops 10000000000 | bytes 16777216 | tf_op jit(solution)/shard_map/finish/pallas_call | solution.py:919
  (4 shorter events, 0.0 us)
Async XLA Ops:
  231.3 1.0 copy-start
  231.3 1.2 copy-start.1

commit v5 on v4

--- a/solution.py
+++ b/solution.py
@@ -31,6 +31,8 @@
 SLOTS = 96
 UNROLL = 4
 FAST_PAGES = 32
+LATE = 23
+LATES = FAST_PAGES - LATE
 BOX = jax.ShapeDtypeStruct((3 * MIG, 2, PAGE * KV_HEADS, HEAD), BF16)
 
 
@@ -161,7 +163,7 @@
     )(h, wq, wk, wv)
 
 
-def plan_kernel(new_table, seq_lens, mig_src, mig_dst, meta, items, slots, gone, moved, rows, source, place_of, counts):
+def plan_kernel(new_table, seq_lens, mig_src, mig_dst, meta, items, slots, gone, moved, rows, lates, source, place_of, counts):
     me = lax.axis_index('kv')
     base = me * SLOTS
 
@@ -176,6 +178,8 @@
     lax.fori_loop(0, 4 * SLOTS, clear, 0, unroll=16)
     for i in range(16):
         counts[i] = 0
+    for i in range(LATES):
+        lates[i] = -1
 
     def keep(i, carry):
         slots[i] = 0
@@ -201,6 +205,8 @@
         slots[jnp.where(hs == me, s - base, SLOTS)] = 1
         slots[jnp.where(hd == me, d - base, SLOTS)] = 1
         gone[m] = s - base
+        is_late = (hs == me) & (channel == 2) & (rank >= LATE) & (rank < FAST_PAGES)
+        lates[jnp.where(is_late, rank - LATE, LATES)] = s - base
         moved[0, n] = d - base
         moved[1, n] = place
         return n + (hd == me).astype(jnp.int32), m + (hs == me).astype(jnp.int32), even, odd
@@ -254,7 +260,7 @@
 
 
 def run_plan(new_table, seq_lens, mig_src, mig_dst):
-    shapes = [(5,), (7, SEQS + UNROLL), (SLOTS + 1,), (MIG + 1,), (2, MIG + 1), (3, 2 * SEQS + 1)]
+    shapes = [(5,), (7, SEQS + UNROLL), (SLOTS + 1,), (MIG + 1,), (2, MIG + 1), (3, 2 * SEQS + 1), (LATES + 1,)]
     return pl.pallas_call(
         plan_kernel,
         name='plan',
@@ -274,10 +280,10 @@
 
 def attend_kernel(layer, meta, table, slots, q_all, k_pool, v_pool, *refs):
     if layer == 0:
-        part_o, part_l, outbox, pool_out, *refs = refs
+        lates, part_o, part_l, outbox, pool_out, late_box, *refs, late_buf, late_in, late_out = refs
     else:
         moved, inbox, spare, _, part_o, part_l, outbox, pool_out, k_out, *refs, pages, page_in, page_out = refs
-    q_rows, kbuf, vbuf, ring, sems, out_sems, ring_in, ring_out = refs
+    q_rows, kvbuf, ring, sems, out_sems, ring_in, ring_out = refs
     pool = (k_pool, v_pool)[layer]
     groups = (meta[0] + UNROLL - 1) // UNROLL
 
@@ -289,9 +295,11 @@
 
                 @pl.when(page >= 0)
                 def _():
-                    for ref, buf in ((k_pool, kbuf), (v_pool, vbuf)):
-                        copy = pltpu.make_async_copy(ref.at[page, layer], buf.at[slot, u, j], sems.at[slot])
-                        copy.start() if start else copy.wait()
+                    if start:
+                        for p, ref in enumerate((k_pool, v_pool)):
+                            pltpu.make_async_copy(ref.at[page, layer], kvbuf.at[slot, u, j, p], sems.at[slot]).start()
+                    else:
+                        pltpu.make_async_copy(outbox.at[0], kvbuf.at[slot, u, j], sems.at[slot]).wait()
 
     def packs(g, start):
         slot = lax.rem(g, NBUF)
@@ -301,9 +309,8 @@
 
                 @pl.when(place >= 0)
                 def _():
-                    for p, buf in enumerate((kbuf, vbuf)):
-                        copy = pltpu.make_async_copy(buf.at[slot, u, j], outbox.at[place, p], out_sems.at[slot])
-                        copy.start() if start else copy.wait()
+                    copy = pltpu.make_async_copy(kvbuf.at[slot, u, j], outbox.at[place], out_sems.at[slot])
+                    copy.start() if start else copy.wait()
 
     def keep(s, phase):
         place = lax.rem(s, NBUF)
@@ -321,6 +328,9 @@
 
     def settle(phase):
         def one(i, carry):
+            place = moved[1, i]
+            here = (place < 2 * MIG + LATE) | (meta[1] == 2)
+
             def move(box):
                 for p, dst in enumerate((k_out, pool_out)):
                     if phase < 2:
@@ -330,17 +340,34 @@
                     copy.wait() if phase % 2 else copy.start()
 
             if phase:
-                move(inbox)
+                pl.when(here)(lambda: move(inbox))
             else:
-                pl.when(meta[1] < 2)(lambda: move(inbox))
+                pl.when(here & (meta[1] < 2))(lambda: move(inbox))
                 pl.when(meta[1] == 2)(lambda: move(spare))
             return carry
 
         lax.fori_loop(0, meta[2], one, 0)
 
+    def late(phase):
+        def one(i, carry):
+            @pl.when(lates[i] >= 0)
+            def _():
+                for l in range(LAYERS):
+                    for p, ref in enumerate((k_pool, v_pool)):
+                        if phase < 2:
+                            copy = pltpu.make_async_copy(ref.at[lates[i], l], late_buf.at[l, i, p], late_in)
+                        else:
+                            copy = pltpu.make_async_copy(late_buf.at[l, i, p], late_box.at[l, i, p], late_out)
+                        copy.wait() if phase % 2 else copy.start()
+            return carry
+
+        lax.fori_loop(0, LATES, one, 0)
+
     if layer == 1:
         settle(0)
-    vbuf[...] = jnp.zeros_like(vbuf)
+    else:
+        late(0)
+    kvbuf[...] = jnp.zeros_like(kvbuf)
     for g in range(DIST):
         @pl.when(g < groups)
         def _():
@@ -371,12 +398,12 @@
             q = jnp.concatenate([q0, q1], axis=0).astype(BF16)
             scores = []
             for j in range(2):
-                s = lax.dot_general(q, kbuf[slot, u, j], (((1,), (1,)), ((), ())), preferred_element_type=F32)
+                s = lax.dot_general(q, kvbuf[slot, u, j, 0], (((1,), (1,)), ((), ())), preferred_element_type=F32)
                 scores.append(jnp.where(pos < table[3 + j, item], s, NEG))
             top = jnp.max(jnp.maximum(scores[0], scores[1]), axis=1, keepdims=True)
             probs = [jnp.exp2((s - top) * (SCALE * LOG2E)) for s in scores]
             total = jnp.sum(probs[0] + probs[1], axis=1, keepdims=True)
-            out = sum(dot(p.astype(BF16), vbuf[slot, u, j]) for j, p in enumerate(probs))
+            out = sum(dot(p.astype(BF16), kvbuf[slot, u, j, 1]) for j, p in enumerate(probs))
             live = top > NEG
             lse = jnp.where(live, top * SCALE + jnp.log(total), NEG)
             outs.append((seq, jnp.where(live, out / total, 0.0), jnp.broadcast_to(lse, (2 * HEADS, HEAD))))
@@ -389,11 +416,11 @@
 
     def step(g, carry):
         keep(g, 1)
-        if layer == 1:
-            @pl.when(g == STEPS // 2)
-            def _():
-                settle(1)
-                settle(2)
+
+        @pl.when(g == STEPS // 2)
+        def _():
+            for phase in (1, 2):
+                settle(phase) if layer == 1 else late(phase)
 
         @pl.when(g < groups)
         def _():
@@ -428,30 +455,33 @@
         @pl.when(g < groups)
         def _():
             packs(g, False)
-    if layer == 1:
-        settle(3)
-
-
-def run_attend(layer, meta, table, slots, q_all, k_flat, v_flat, extra=()):
+    settle(3) if layer == 1 else late(3)
+
+
+def run_attend(layer, meta, table, slots, q_all, k_flat, v_flat, *extra):
     shape = jax.ShapeDtypeStruct((2, 2, TOK, HALF_HEADS, HEAD), F32)
-    page = (UNROLL, 2, PAGE * KV_HEADS, HEAD)
+    page = (PAGE * KV_HEADS, HEAD)
+    late = (LAYERS, LATES, 2) + page
+    more = [jax.ShapeDtypeStruct(k_flat.shape if layer else late, BF16)]
     return pl.pallas_call(
         functools.partial(attend_kernel, layer),
         name=f'attend{layer}',
-        out_shape=[shape, shape, BOX] + [jax.ShapeDtypeStruct(k_flat.shape, BF16)] * (layer + 1),
-        in_specs=[SMEM, SMEM, SMEM, VMEM, ANY, ANY] + [SMEM, ANY, ANY, ANY] * layer,
-        out_specs=[VMEM, VMEM, ANY, ANY] + [ANY] * layer,
+        out_shape=[shape, shape, BOX, jax.ShapeDtypeStruct(k_flat.shape, BF16)] + more,
+        in_specs=[SMEM, SMEM, SMEM, VMEM, ANY, ANY, SMEM] + [ANY, ANY, ANY] * layer,
+        out_specs=[VMEM, VMEM, ANY, ANY, ANY],
         input_output_aliases={9: 4} if layer else {},
         scratch_shapes=[
             pltpu.VMEM((2 * TOK * HEADS, HEAD), F32),
-            pltpu.VMEM((NBUF,) + page, BF16),
-            pltpu.VMEM((NBUF,) + page, BF16),
+            pltpu.VMEM((NBUF, UNROLL, 2, 2) + page, BF16),
             pltpu.VMEM((NBUF, SLOTS_STEP) + k_flat.shape[1:], BF16),
             DMA((NBUF,)),
             DMA((NBUF,)),
             DMA((NBUF, SLOTS_STEP)),
             DMA((NBUF, SLOTS_STEP)),
-        ] + [pltpu.VMEM((MIG, 2, PAGE * KV_HEADS, HEAD), BF16), DMA, DMA] * layer,
+            pltpu.VMEM(((MIG, 2) + page) if layer else late, BF16),
+            DMA,
+            DMA,
+        ],
         cost_estimate=pl.CostEstimate(flops=2 * 10 ** 10, bytes_accessed=16 * 2 ** 20, transcendentals=0),
         compiler_params=pltpu.CompilerParams(vmem_limit_bytes=VMEM_LIMIT),
     )(meta, table, slots, q_all, k_flat, v_flat, *extra)
@@ -465,9 +495,9 @@
     return out, top + jnp.log(total)
 
 
-LANES = ([((0,), 2, FAST_PAGES), ((0,), 0, FAST_PAGES)], [((1,), 2, FAST_PAGES), ((1,), 0, FAST_PAGES)])
+LANES = ([((0,), 2, LATE), ((0,), 0, FAST_PAGES)], [((1,), 2, LATE), ((1,), 0, FAST_PAGES)])
 EVERYTHING = [((0, 1), i, MIG) for i in range(3)]
-CHUNK = 2
+CHUNK = 1
 
 
 class Boxes:
@@ -587,7 +617,7 @@
             compact = jnp.where(lane == 2 * i, l[:8], compact)
             return jnp.where(lane == 2 * i + 1, l[8:], compact)
 
-        give_l[part] = lax.fori_loop(0, PART, chip_merge, jnp.zeros((8, HEAD), F32), unroll=8)
+        give_l[part] = lax.fori_loop(0, PART, chip_merge, jnp.zeros((8, HEAD), F32), unroll=4)
         rows = pl.ds(part * PART, PART)
         pair = [
             send(give_l.at[part], far_l.at[part], xsend.at[part, 0], xrecv.at[part, 0], across),
@@ -633,7 +663,7 @@
         mine_l[j] = l
         return carry
 
-    lax.fori_loop(0, PART, own_merge, 0, unroll=4)
+    lax.fori_loop(0, PART, own_merge, 0, unroll=2)
 
     for part in range(2):
         for copy in far[part]:
@@ -653,7 +683,7 @@
             q_rows[pl.ds(pl.multiple_of(j * HALF_HEADS, HALF_HEADS), HALF_HEADS), :] = o
             return carry
 
-        lax.fori_loop(0, PART, last_merge, 0, unroll=8)
+        lax.fori_loop(0, PART, last_merge, 0, unroll=4)
     for head in range(HALF_HEADS):
         attn[:, head * HEAD:(head + 1) * HEAD] = q_rows[pl.ds(head, TOK, stride=HALF_HEADS), :].astype(BF16)
 
@@ -727,33 +757,30 @@
             ref = q_next.at[1 - chip, core * 4 + j]
             return send(ref, ref, qf_send.at[j], qf_recv.at[j], partner)
 
-        def project_next(j, kind):
+        def project_next(j, carry):
             total = None
             for k in range(2):
                 t = DOWN_END + 2 * j + k
-                tile_copy(t, kind).wait()
+                tile_copy(t, 4).wait()
                 part = dot(out[:, k * TK:(k + 1) * TK], ring[lax.rem(t, RING_W)])
                 total = part if total is None else total + part
-            return total.astype(BF16)
-
-        def query(j, carry):
-            q_next[chip, core * 4 + j] = project_next(j, 3)
-
-            @pl.when(j > 0)
+            tile = total.astype(BF16)
+
+            @pl.when(j < 4)
+            def _():
+                q_next[chip, core * 4 + j] = tile
+
+            @pl.when(j >= 4)
+            def _():
+                kv_next[:, pl.ds(pl.multiple_of((j - 4) * TN, TN), TN)] = tile
+
+            @pl.when((j > 0) & (j < 5))
             def _():
                 to_across(j - 1).start()
                 to_partner(j - 1).start()
             return carry
 
-        lax.fori_loop(0, 4, query, 0)
-        to_across(3).start()
-        to_partner(3).start()
-
-        def key_value(j, carry):
-            kv_next[:, pl.ds(pl.multiple_of(j * TN, TN), TN)] = project_next(j + 4, 4)
-            return carry
-
-        lax.fori_loop(0, 2, key_value, 0)
+        lax.fori_loop(0, 6, project_next, 0)
         for j in range(4):
             to_across(j).wait_recv()
             forward(j).start()
@@ -847,7 +874,7 @@
 AHEAD = RING // 2
 
 
-def finish_kernel(meta, moved, gone, rows, inbox, spare, kv0, kv1, k_in, v_in, k_out, v_out, wide, row_buf, zeros, buf, in_sem, out_sem, zero_sem, row_sem):
+def finish_kernel(meta, moved, gone, rows, inbox, spare, late, kv0, kv1, k_in, v_in, k_out, v_out, wide, row_buf, zeros, buf, in_sem, out_sem, zero_sem, row_sem):
     del k_in, v_in
     outs = (k_out, v_out)
     count = meta[2]
@@ -858,13 +885,21 @@
     def clear(i):
         return [pltpu.make_async_copy(zeros, out.at[gone[i]], zero_sem) for out in outs]
 
+    def is_late(i):
+        return (moved[1, i] >= 2 * MIG + LATE) & (meta[1] < 2)
+
     def load(i, box):
         slot = lax.rem(i, RING)
-        return [pltpu.make_async_copy(box.at[moved[1, i], p], buf.at[slot, p], in_sem.at[slot, p]) for p in range(2)]
-
-    def store(i):
+        return [pltpu.make_async_copy(box.at[moved[1, i], p], buf.at[slot, 1, p], in_sem.at[slot, 1, p]) for p in range(2)]
+
+    def load_late(i):
         slot = lax.rem(i, RING)
-        return [pltpu.make_async_copy(buf.at[slot, p], outs[p].at[moved[0, i], 1], out_sem.at[slot, p]) for p in range(2)]
+        rank = moved[1, i] - (2 * MIG + LATE)
+        return [pltpu.make_async_copy(late.at[l, rank, p], buf.at[slot, l, p], in_sem.at[slot, l, p]) for l in range(LAYERS) for p in range(2)]
+
+    def store(i, layers):
+        slot = lax.rem(i, RING)
+        return [pltpu.make_async_copy(buf.at[slot, l, p], outs[p].at[moved[0, i], l], out_sem.at[slot, l, p]) for l in layers for p in range(2)]
 
     def begin(group):
         for copy in group:
@@ -875,8 +910,24 @@
             copy.wait()
 
     def begin_load(i):
-        pl.when(meta[1] < 2)(lambda: begin(load(i, inbox)))
+        pl.when((meta[1] < 2) & jnp.logical_not(is_late(i)))(lambda: begin(load(i, inbox)))
+        pl.when(is_late(i))(lambda: begin(load_late(i)))
         pl.when(meta[1] == 2)(lambda: begin(load(i, spare)))
+
+    def begin_store(i):
+        @pl.when(is_late(i))
+        def _():
+            end(load_late(i))
+            begin(store(i, (0, 1)))
+
+        @pl.when(jnp.logical_not(is_late(i)))
+        def _():
+            end(load(i, inbox))
+            begin(store(i, (1,)))
+
+    def end_store(i):
+        pl.when(is_late(i))(lambda: end(store(i, (0, 1))))
+        pl.when(jnp.logical_not(is_late(i)))(lambda: end(store(i, (1,))))
 
     loop(0, jnp.minimum(count, AHEAD), begin_load)
     zeros[...] = jnp.zeros_like(zeros)
@@ -891,18 +942,15 @@
             row_buf[p, l] = wide[...].astype(BF16)
 
     def page(i):
-        end(load(i, inbox))
-        begin(store(i))
+        begin_store(i)
 
         @pl.when(i + AHEAD < count)
         def _():
-            @pl.when(i >= AHEAD)
-            def _():
-                end(store(i - AHEAD))
+            pl.when(i >= AHEAD)(lambda: end_store(i - AHEAD))
             begin_load(i + AHEAD)
 
     loop(0, count, page)
-    loop(jnp.maximum(count - RING, 0), count, lambda i: end(store(i)))
+    loop(jnp.maximum(count - RING, 0), count, end_store)
 
     def row(i):
         at = pl.ds(pl.multiple_of(rows[1, i] * KV_HEADS, KV_HEADS), KV_HEADS)
@@ -920,19 +968,19 @@
         finish_kernel,
         name='finish',
         out_shape=[shape, shape],
-        in_specs=[SMEM] * 4 + [ANY, ANY, VMEM, VMEM, ANY, ANY],
+        in_specs=[SMEM] * 4 + [ANY, ANY, ANY, VMEM, VMEM, ANY, ANY],
         out_specs=[ANY, ANY],
         scratch_shapes=[
             pltpu.VMEM((2 * TOK * KV_HEADS, HEAD), F32),
             pltpu.VMEM((2, LAYERS, 2 * TOK * KV_HEADS, HEAD), BF16),
             pltpu.VMEM(k_part.shape[1:], BF16),
-            pltpu.VMEM((RING, 2) + k_part.shape[2:], BF16),
-            DMA((RING, 2)),
-            DMA((RING, 2)),
+            pltpu.VMEM((RING,) + (LAYERS, 2) + k_part.shape[2:], BF16),
+            DMA((RING, LAYERS, 2)),
+            DMA((RING, LAYERS, 2)),
             DMA,
             DMA((2, LAYERS)),
         ],
-        input_output_aliases={8: 0, 9: 1},
+        input_output_aliases={9: 0, 10: 1},
         cost_estimate=pl.CostEstimate(flops=10 ** 10, bytes_accessed=16 * 2 ** 20, transcendentals=0),
         compiler_params=pltpu.CompilerParams(vmem_limit_bytes=VMEM_LIMIT),
     )(meta, moved, gone, rows, *boxes, *kvs, k_part, v_part)
@@ -946,21 +994,25 @@
         me = lax.axis_index('kv')
         weights = (w_query, w_key, w_value)
         k_flat, v_flat = flat_pool(k_pool), flat_pool(v_pool)
-        meta, items, slots, gone, moved, where = run_plan(new_table, seq_lens, mig_src, mig_dst)
-        lane_core = jnp.minimum(meta[1], 1)
+        meta, items, slots, gone, moved, where, lates = run_plan(new_table, seq_lens, mig_src, mig_dst)
         q_all, kv, h = run_qkv(0, embeds, weights, True)
-        kvs, boxes, pools = [], (), ()
-        for layer in range(LAYERS):
-            extra = (moved, *boxes, *pools) if layer else ()
-            part_o, part_l, outbox, *pools = run_attend(layer, meta, items, slots, q_all, k_flat, v_flat, extra)
-            forms = [functools.partial(run_rest, layer, core) for core in range(2)]
-            more = weights if layer == 0 else ()
-            h, kv_all, inbox, *more = lax.switch(lane_core, forms, h, q_all, kv, part_o, part_l, outbox, w_out, w_up, w_down, *more)
-            kvs.append(kv_all)
-            if more:
-                q_all, kv = more
-            boxes = inbox, lax.cond(meta[1] == 2, functools.partial(run_move, layer), lambda box: run_blank(layer), outbox)
-        k_out, v_out = run_finish(meta, moved, gone, where, boxes, kvs, pools[1], pools[0])
+        part_o, part_l, outbox, k_kept, late_box = run_attend(0, meta, items, slots, q_all, k_flat, v_flat, lates)
+
+        def extra_boxes(layer, outbox):
+            return lax.cond(meta[1] == 2, functools.partial(run_move, layer), lambda box: run_blank(layer), outbox)
+
+        def layers(core, h, q_all, kv, part_o, part_l, outbox, late_box, k_kept):
+            h, kv_all0, inbox, q_all, kv = run_rest(0, core, h, q_all, kv, part_o, part_l, outbox, w_out, w_up, w_down, *weights)
+            spare = extra_boxes(0, outbox)
+            late_box, q_all = lax.optimization_barrier((late_box, q_all))
+            late = lax.ppermute(late_box, 'kv', [(core, 3 - core), (2 + core, 1 - core)])
+            part_o, part_l, outbox, v_kept, k_kept = run_attend(1, meta, items, slots, q_all, k_flat, v_flat, moved, inbox, spare, k_kept)
+            h, kv_all1, inbox = run_rest(1, core, h, q_all, kv, part_o, part_l, outbox, w_out, w_up, w_down)
+            return h, kv_all0, kv_all1, inbox, extra_boxes(1, outbox), late, k_kept, v_kept
+
+        forms = [functools.partial(layers, core) for core in range(2)]
+        h, kv_all0, kv_all1, inbox, spare, late, k_kept, v_kept = lax.switch(jnp.minimum(meta[1], 1), forms, h, q_all, kv, part_o, part_l, outbox, late_box, k_kept)
+        k_out, v_out = run_finish(meta, moved, gone, where, (inbox, spare, late), (kv_all0, kv_all1), k_kept, v_kept)
         k_out, v_out = k_out.reshape(k_pool.shape), v_out.reshape(v_pool.shape)
         y = lax.dynamic_slice_in_dim(h.reshape(2, 32, D), (me % 2) * 16, 16, axis=1)
         return y, k_out, v_out

time: 242 us -> 232 us (0.959)
  the two profiles are of different devices: /device:TPU:5 before, /device:TPU:0 now
where the time goes in v5:
time: 232 us; the launch traced here: 229 us
  Pallas kernels  220 us (95%)
  starting transfers between devices  3.29 us (1%)
  local copies, waits for them, and re-layouts  3.21 us (1%)
    pallas_call x2, Pallas kernels, run_rest(): pl.pallas_call(functools.partial(rest_kernel, layer, lane_core), name=f'r...  142 us
    pallas_call x2, Pallas kernels, run_attend(): pl.pallas_call(functools.partial(attend_kernel, layer), name=f'attend{lay...  49.2 us
    pallas_call x1, Pallas kernels, run_qkv(): pl.pallas_call(functools.partial(qkv_kernel, layer, first), name=f'qkv{la...  17.5 us
    pallas_call x1, Pallas kernels, run_plan(): pl.pallas_call(plan_kernel, name='plan', out_shape=[jax.ShapeDtypeStruct(...  6.01 us
    pallas_call x1, Pallas kernels, run_finish(): pl.pallas_call(finish_kernel, name='finish', out_shape=[shape, shape], in...  5.39 us
  transfers between devices with their start and end apart: 1, of which 0 were waited for; matrix products, arithmetic and copies ran while one was open for 1% of the time, Pallas kernels for 39%

profile of v5, /device:TPU:0, one launch (start us, length us, event | category | flops | bytes accessed | tf_op | source)
XLA Modules:
  0.0 229.2 jit_solution(4624356442853998191)
XLA Ops:
  0.6 6.0 %plan.1 = (s32[5]{0:T(128)S(1)}, s32[7,68]{1,0:T(8,128)S(1)}, s32[97]{0:T(128)S(1)}, s32[65]{0:T(128)}, s32[2,65]{1,0:T(2,128)}, /*index=5*/s32[3,129]{1,0:T(4,128)}, s32[10]{0:T(128)}) custom-call(s32[2,64]{1,0:T(2,128)} %bitcast.18, s32[64]{0:T(128)} %seq_lens.1, s32[64]{0:T(128)} %mig_src.1, s32[64]{0:T(128)} %mig_dst.1), custom_call_target="tpu_custom_call" | custom-call | tf_op jit(solution)/shard_map/plan/pallas_call | solution.py:264
  6.6 0.0 copy-start.1
  6.7 0.0 copy-start.9
  6.7 0.0 copy-start.6
  6.7 17.5 %qkv0.1 = (bf16[2,8,64,512]{3,2,1,0:T(8,128)(2,1)}, bf16[64,1024]{1,0:T(8,128)(2,1)}, bf16[64,4096]{1,0:T(8,128)(2,1)}) custom-call(bf16[2,16,4096]{2,1,0:T(8,128)(2,1)} %refs_0_.1, bf16[2,4096,4096]{2,1,0:T(8,128)(2,1)} %refs_1_.1, bf16[2,4096,1024]{2,1,0:T(8,128)(2,1)} %refs_2_.1, bf16[2,4096,1024]{2,1,0:T(8,128)(2,1)} %refs_3_.1), custom_call_target="tpu_custom_call" | custom-call | flops 12884901888 | bytes 25165824 | tf_op jit(solution)/shard_map/qkv0/pallas_call | solution.py:154
  24.2 0.0 copy-done.1
  24.2 0.0 copy-done.9
  24.2 24.6 %attend0.1 = (f32[2,2,64,16,128]{4,3,2,1,0:T(8,128)}, f32[2,2,64,16,128]{4,3,2,1,0:T(8,128)}, bf16[192,2,256,128]{3,2,1,0:T(8,128)(2,1)}, bf16[96,2,256,128]{3,2,1,0:T(8,128)(2,1)}, bf16[2,9,2,256,128]{4,3,2,1,0:T(8,128)(2,1)}) custom-call(s32[5]{0:T(128)S(1)} %get-tuple-element.194.meta, s32[7,68]{1,0:T(8,128)S(1)} %get-tuple-element.198.table, ...), custom_call_target="tpu_custom_call" | custom-call | flops 20000000000 | bytes 16777216 | tf_op jit(solution)/shard_map/attend0/pallas_call | solution.py:466
  48.8 0.0 copy-done.6
  48.9 0.6 slice.11
  50.1 173.0 %conditional.5 = (bf16[64,4096]{1,0:T(8,128)(2,1)}, bf16[4,64,1024]{2,1,0:T(8,128)(2,1)}, bf16[4,64,1024]{2,1,0:T(8,128)(2,1)}, bf16[192,2,256,128]{3,2,1,0:T(8,...) conditional(s32[]{:T(128)} %bitcast.3, ...), branch_computations={%region_0.0_spmd, %region_5.0_spmd} | conditional | flops 140259082240 | bytes 261107008 | solution.py:1014
  50.1 76.2 %rest0_0.1 = (bf16[64,4096]{1,0:T(8,128)(2,1)}, bf16[4,64,1024]{2,1,0:T(8,128)(2,1)}, bf16[192,2,256,128]{3,2,1,0:T(8,128)(2,1)}, bf16[2,8,64,512]{3,2,1,0:T(8,128)(2,1)}, bf16[64,1024]{1,0:T(8,128)(2,1)}) custom-call(bf16[64,4096]{1,0:T(8,128)(2,1)} %get-tuple-element.96.h_in, bf16[2,8,64,512]{3,2,1,0:T(8,128)(2,1)} %get-tuple-element.97.q_all, ...), custom_call_target="tpu_custom_call" | custom-call | flops 60129542144 | bytes 117440512 | tf_op jit(solution)/shard_map/cond/branch_0_fun/rest0_0/pallas_call | solution.py:805
  126.3 3.3 %collective-permute-start = (bf16[2,9,2,256,128]{4,3,2,1,0:T(8,128)(2,1)}, bf16[2,9,2,256,128]{4,3,2,1,0:T(8,128)(2,1)}, u32[]{:S(2)}, u32[]{:S(2)}) collective-permute-start(bf16[2,9,2,256,128]{4,3,2,1,0:T(8,128)(2,1)} %get-tuple-element.128), channel_id=1, source_target_pairs={{0,3},{2,1},{4,7},{6,5}} | collective-permute-start | bytes 7077896 | tf_op jit(solution)/shard_map/cond/branch_0_fun/ppermute | solution.py:1008
  129.6 1.3 slice.1
  131.5 0.0 copy-start.2
  131.5 0.0 copy-start.4
  131.6 0.6 copy-done.2
  132.2 0.0 copy-done.4
  132.2 0.0 copy-done.7
  132.2 24.5 %attend1.2 = (f32[2,2,64,16,128]{4,3,2,1,0:T(8,128)}, f32[2,2,64,16,128]{4,3,2,1,0:T(8,128)}, bf16[192,2,256,128]{3,2,1,0:T(8,128)(2,1)}, bf16[96,2,256,128]{3,2,1,0:T(8,128)(2,1)}, bf16[96,2,256,128]{3,2,1,0:T(8,128)(2,1)}) custom-call(s32[5]{0:T(128)S(1)} %copy-done.7, s32[7,68]{1,0:T(8,128)S(1)} %copy-done.2, ...), custom_call_target="tpu_custom_call", output_to_operand_aliasing={{4}: (9, {})} | custom-call | flops 20000000000 | bytes 16777216 | tf_op jit(solution)/shard_map/cond/branch_0_fun/attend1/pallas_call | solution.py:466
  156.7 65.7 %rest1_0.1 = (bf16[64,4096]{1,0:T(8,128)(2,1)}, bf16[4,64,1024]{2,1,0:T(8,128)(2,1)}, bf16[192,2,256,128]{3,2,1,0:T(8,128)(2,1)}) custom-call(bf16[64,4096]{1,0:T(8,128)(2,1)} %get-tuple-element.108.h_in, bf16[2,8,64,512]{3,2,1,0:T(8,128)(2,1)} %get-tuple-element.111.q_all, bf16[64,1024]{1,0:T(8,128)(2,1)} %get-tuple-element.112.kv, ...), custom_call_target="tpu_custom_call" | custom-call | flops 60129542144 | bytes 117440512 | tf_op jit(solution)/shard_map/cond/branch_0_fun/rest1_0/pallas_call | solution.py:805
  222.5 0.0 collective-permute-done
  223.1 5.4 %finish.1 = (bf16[96,2,256,128]{3,2,1,0:T(8,128)(2,1)}, bf16[96,2,256,128]{3,2,1,0:T(8,128)(2,1)}) custom-call(s32[5]{0:T(128)} %copy-done.6, s32[2,65]{1,0:T(2,128)} %get-tuple-element.205.moved, s32[65]{0:T(128)} %get-tuple-element.208.gone, s32[3,129]{1,0:T(4,128)} %get-tuple-element.209.rows, ...), custom_call_target="tpu_custom_call", output_to_operand_aliasing={{0}: (9, {}), {1}: (10, {})} | custom-call | flops 10000000000 | bytes 16777216 | tf_op jit(solution)/shard_map/finish/pallas_call | solution.py:967
  228.5 0.7 constant_dynamic-slice_fusion
  (9 shorter events, 0.1 us)
Async XLA Ops:
  6.6 17.5 %copy-start.1 = (s32[7,68]{1,0:T(8,128)}, s32[7,68]{1,0:T(8,128)S(1)}, u32[]{:S(2)}) copy-start(s32[7,68]{1,0:T(8,128)S(1)} %get-tuple-element.198.table) | copy-start | bytes 5716
  6.7 17.5 %copy-start.9 = (s32[97]{0:T(128)}, s32[97]{0:T(128)S(1)}, u32[]{:S(2)}) copy-start(s32[97]{0:T(128)S(1)} %get-tuple-element.199.slots) | copy-start | bytes 1168
  6.7 42.2 %copy-start.6 = (s32[5]{0:T(128)}, s32[5]{0:T(128)S(1)}, u32[]{:S(2)}) copy-start(s32[5]{0:T(128)S(1)} %get-tuple-element.194.meta) | copy-start | bytes 64
  126.3 96.2 %collective-permute-start = (bf16[2,9,2,256,128]{4,3,2,1,0:T(8,128)(2,1)}, bf16[2,9,2,256,128]{4,3,2,1,0:T(8,128)(2,1)}, u32[]{:S(2)}, u32[]{:S(2)}) collective-permute-start(bf16[2,9,2,256,128]{4,3,2,1,0:T(8,128)(2,1)} %get-tuple-element.128), channel_id=1, source_target_pairs={{0,3},{2,1},{4,7},{6,5}} | collective-permute-start | bytes 7077896 | tf_op jit(solution)/shard_map/cond/branch_0_fun/ppermute | solution.py:1008
  131.5 0.7 copy-start.2
  131.5 0.7 copy-start.4
  131.5 0.7 copy-start.7
  131.6 0.7 copy-start.10
  223.1 5.4 %copy-start = (bf16[64,4096]{1,0:T(8,128)(2,1)S(1)}, bf16[64,4096]{1,0:T(8,128)(2,1)}, u32[]{:S(2)}) copy-start(bf16[64,4096]{1,0:T(8,128)(2,1)} %get-tuple-element.207) | copy-start | bytes 1572868

commit v6 on v5

--- a/solution.py
+++ b/solution.py
@@ -163,7 +163,7 @@
     )(h, wq, wk, wv)
 
 
-def plan_kernel(new_table, seq_lens, mig_src, mig_dst, meta, items, slots, gone, moved, rows, lates, source, place_of, counts):
+def plan_kernel(new_table, seq_lens, mig_src, mig_dst, meta, items, slots, gone, moved, rows, lates, lane, general, source, place_of, counts):
     me = lax.axis_index('kv')
     base = me * SLOTS
 
@@ -233,14 +233,11 @@
         items[4, n] = jnp.where(own[1], jnp.maximum(length - PAGE, 0), 0)
         items[5, n] = place[0]
         items[6, n] = place[1]
-        for t in range(2):
-            pos = length + t
-            second = pos >= PAGE
-            here = jnp.where(second, new_table[1, b], new_table[0, b]) - base
-            rows[0, m] = here
-            rows[1, m] = jnp.where(second, pos - PAGE, pos)
-            rows[2, m] = (b // 32) * TOK + t * 32 + b % 32
-            m = m + ((here >= 0) & (here < SLOTS)).astype(jnp.int32)
+        here = new_table[1, b] - base
+        rows[0, m] = here
+        rows[1, m] = length - PAGE
+        rows[2, m] = b
+        m = m + ((here >= 0) & (here < SLOTS)).astype(jnp.int32)
         return n + (own[0] | own[1]).astype(jnp.int32), m
 
     n_items, n_rows = lax.fori_loop(0, SEQS, sequence, (zero, zero), unroll=8)
@@ -254,13 +251,15 @@
                 items[f, n_items + i] = -1
     meta[0] = n_items
     meta[1] = jnp.where(even == 0, 0, jnp.where(odd == 0, 1, 2))
+    lane[0] = jnp.where(even == 0, 0, 1)
+    general[0] = jnp.where((even == 0) | (odd == 0), 0, 1)
     meta[2] = n_moved
     meta[3] = n_rows
     meta[4] = n_gone
 
 
 def run_plan(new_table, seq_lens, mig_src, mig_dst):
-    shapes = [(5,), (7, SEQS + UNROLL), (SLOTS + 1,), (MIG + 1,), (2, MIG + 1), (3, 2 * SEQS + 1), (LATES + 1,)]
+    shapes = [(5,), (7, SEQS + UNROLL), (SLOTS + 1,), (MIG + 1,), (2, MIG + 1), (3, SEQS + 1), (LATES + 1,), (1,), (1,)]
     return pl.pallas_call(
         plan_kernel,
         name='plan',
@@ -352,13 +351,14 @@
         def one(i, carry):
             @pl.when(lates[i] >= 0)
             def _():
-                for l in range(LAYERS):
+                if phase == 0:
                     for p, ref in enumerate((k_pool, v_pool)):
-                        if phase < 2:
-                            copy = pltpu.make_async_copy(ref.at[lates[i], l], late_buf.at[l, i, p], late_in)
-                        else:
-                            copy = pltpu.make_async_copy(late_buf.at[l, i, p], late_box.at[l, i, p], late_out)
-                        copy.wait() if phase % 2 else copy.start()
+                        pltpu.make_async_copy(ref.at[lates[i]], late_buf.at[i, p], late_in).start()
+                elif phase == 1:
+                    pltpu.make_async_copy(late_box.at[i], late_buf.at[i], late_in).wait()
+                else:
+                    copy = pltpu.make_async_copy(late_buf.at[i], late_box.at[i], late_out)
+                    copy.wait() if phase == 3 else copy.start()
             return carry
 
         lax.fori_loop(0, LATES, one, 0)
@@ -461,7 +461,7 @@
 def run_attend(layer, meta, table, slots, q_all, k_flat, v_flat, *extra):
     shape = jax.ShapeDtypeStruct((2, 2, TOK, HALF_HEADS, HEAD), F32)
     page = (PAGE * KV_HEADS, HEAD)
-    late = (LAYERS, LATES, 2) + page
+    late = (LATES, 2, LAYERS) + page
     more = [jax.ShapeDtypeStruct(k_flat.shape if layer else late, BF16)]
     return pl.pallas_call(
         functools.partial(attend_kernel, layer),
@@ -531,7 +531,8 @@
         self.each(False, lambda copy: copy.wait_recv())
 
 
-RING_W = 18
+RING_W = 20
+SOON = 4
 TK = 2048
 UP_TILES = FF // 2 // TN
 TD = FF // 8
@@ -596,11 +597,12 @@
             send(part_o.at[owner, 1 - core, rows], got_o.at[at], dsend.at[which, 0], drecv.at[which, 0], partner),
             send(part_l.at[owner, 1 - core, rows], got_l.at[at], dsend.at[which, 1], drecv.at[which, 1], partner),
         ])
+    lax.fori_loop(0, SOON, lambda t, carry: (fetch(t), carry)[1], 0)
     meet((partner, across, diag))
     for pair in near:
         for copy in pair:
             copy.start()
-    lax.fori_loop(0, RING_W, lambda t, carry: (fetch(t), carry)[1], 0)
+    lax.fori_loop(SOON, RING_W, lambda t, carry: (fetch(t), carry)[1], 0)
 
     lane = lax.broadcasted_iota(jnp.int32, (8, HEAD), 1)
     far = []
@@ -890,16 +892,19 @@
 
     def load(i, box):
         slot = lax.rem(i, RING)
-        return [pltpu.make_async_copy(box.at[moved[1, i], p], buf.at[slot, 1, p], in_sem.at[slot, 1, p]) for p in range(2)]
+        return [pltpu.make_async_copy(box.at[moved[1, i], p], buf.at[slot, p, 1], in_sem.at[slot, p]) for p in range(2)]
 
     def load_late(i):
         slot = lax.rem(i, RING)
-        rank = moved[1, i] - (2 * MIG + LATE)
-        return [pltpu.make_async_copy(late.at[l, rank, p], buf.at[slot, l, p], in_sem.at[slot, l, p]) for l in range(LAYERS) for p in range(2)]
-
-    def store(i, layers):
+        return [pltpu.make_async_copy(late.at[moved[1, i] - (2 * MIG + LATE), p], buf.at[slot, p], in_sem.at[slot, p]) for p in range(2)]
+
+    def store(i):
         slot = lax.rem(i, RING)
-        return [pltpu.make_async_copy(buf.at[slot, l, p], outs[p].at[moved[0, i], l], out_sem.at[slot, l, p]) for l in layers for p in range(2)]
+        return [pltpu.make_async_copy(buf.at[slot, p, 1], outs[p].at[moved[0, i], 1], out_sem.at[slot, p]) for p in range(2)]
+
+    def store_late(i):
+        slot = lax.rem(i, RING)
+        return [pltpu.make_async_copy(buf.at[slot, p], outs[p].at[moved[0, i]], out_sem.at[slot, p]) for p in range(2)]
 
     def begin(group):
         for copy in group:
@@ -918,16 +923,16 @@
         @pl.when(is_late(i))
         def _():
             end(load_late(i))
-            begin(store(i, (0, 1)))
+            begin(store_late(i))
 
         @pl.when(jnp.logical_not(is_late(i)))
         def _():
             end(load(i, inbox))
-            begin(store(i, (1,)))
+            begin(store(i))
 
     def end_store(i):
-        pl.when(is_late(i))(lambda: end(store(i, (0, 1))))
-        pl.when(jnp.logical_not(is_late(i)))(lambda: end(store(i, (1,))))
+        pl.when(is_late(i))(lambda: end(store_late(i)))
+        pl.when(jnp.logical_not(is_late(i)))(lambda: end(store(i)))
 
     loop(0, jnp.minimum(count, AHEAD), begin_load)
     zeros[...] = jnp.zeros_like(zeros)
@@ -937,8 +942,9 @@
         for p in range(2):
             for dev in range(4):
                 for i in range(4):
-                    at = pl.ds((dev // 2) * TOK * KV_HEADS + (dev % 2) * 4 + i, TOK, stride=KV_HEADS)
-                    wide[at, :] = kv[dev, :, (p * 4 + i) * HEAD:(p * 4 + i + 1) * HEAD].astype(F32)
+                    for t in range(2):
+                        at = pl.ds((dev // 2) * TOK * KV_HEADS + t * KV_HEADS + (dev % 2) * 4 + i, TOK // 2, stride=2 * KV_HEADS)
+                        wide[at, :] = kv[dev, t * 32:(t + 1) * 32, (p * 4 + i) * HEAD:(p * 4 + i + 1) * HEAD].astype(F32)
             row_buf[p, l] = wide[...].astype(BF16)
 
     def page(i):
@@ -953,9 +959,9 @@
     loop(jnp.maximum(count - RING, 0), count, end_store)
 
     def row(i):
-        at = pl.ds(pl.multiple_of(rows[1, i] * KV_HEADS, KV_HEADS), KV_HEADS)
-        src = pl.ds(pl.multiple_of(rows[2, i] * KV_HEADS, KV_HEADS), KV_HEADS)
-        return [pltpu.make_async_copy(row_buf.at[p, l, src, :], outs[p].at[rows[0, i], l, at, :], row_sem.at[p, l]) for p in range(2) for l in range(LAYERS)]
+        at = pl.ds(pl.multiple_of(rows[1, i] * KV_HEADS, KV_HEADS), 2 * KV_HEADS)
+        src = pl.ds(pl.multiple_of(rows[2, i] * 2 * KV_HEADS, 2 * KV_HEADS), 2 * KV_HEADS)
+        return [pltpu.make_async_copy(row_buf.at[p, :, src, :], outs[p].at[rows[0, i], :, at, :], row_sem.at[p]) for p in range(2)]
 
     loop(0, meta[3], lambda i: begin(row(i)))
     loop(0, meta[3], lambda i: end(row(i)))
@@ -974,11 +980,11 @@
             pltpu.VMEM((2 * TOK * KV_HEADS, HEAD), F32),
             pltpu.VMEM((2, LAYERS, 2 * TOK * KV_HEADS, HEAD), BF16),
             pltpu.VMEM(k_part.shape[1:], BF16),
-            pltpu.VMEM((RING,) + (LAYERS, 2) + k_part.shape[2:], BF16),
-            DMA((RING, LAYERS, 2)),
-            DMA((RING, LAYERS, 2)),
+            pltpu.VMEM((RING, 2) + k_part.shape[1:], BF16),
+            DMA((RING, 2)),
+            DMA((RING, 2)),
             DMA,
-            DMA((2, LAYERS)),
+            DMA((2,)),
         ],
         input_output_aliases={9: 0, 10: 1},
         cost_estimate=pl.CostEstimate(flops=10 ** 10, bytes_accessed=16 * 2 ** 20, transcendentals=0),
@@ -994,12 +1000,12 @@
         me = lax.axis_index('kv')
         weights = (w_query, w_key, w_value)
         k_flat, v_flat = flat_pool(k_pool), flat_pool(v_pool)
-        meta, items, slots, gone, moved, where, lates = run_plan(new_table, seq_lens, mig_src, mig_dst)
+        meta, items, slots, gone, moved, where, lates, lane, general = run_plan(new_table, seq_lens, mig_src, mig_dst)
         q_all, kv, h = run_qkv(0, embeds, weights, True)
         part_o, part_l, outbox, k_kept, late_box = run_attend(0, meta, items, slots, q_all, k_flat, v_flat, lates)
 
         def extra_boxes(layer, outbox):
-            return lax.cond(meta[1] == 2, functools.partial(run_move, layer), lambda box: run_blank(layer), outbox)
+            return lax.switch(general.reshape(()), [lambda box: run_blank(layer), functools.partial(run_move, layer)], outbox)
 
         def layers(core, h, q_all, kv, part_o, part_l, outbox, late_box, k_kept):
             h, kv_all0, inbox, q_all, kv = run_rest(0, core, h, q_all, kv, part_o, part_l, outbox, w_out, w_up, w_down, *weights)
@@ -1011,7 +1017,7 @@
             return h, kv_all0, kv_all1, inbox, extra_boxes(1, outbox), late, k_kept, v_kept
 
         forms = [functools.partial(layers, core) for core in range(2)]
-        h, kv_all0, kv_all1, inbox, spare, late, k_kept, v_kept = lax.switch(jnp.minimum(meta[1], 1), forms, h, q_all, kv, part_o, part_l, outbox, late_box, k_kept)
+        h, kv_all0, kv_all1, inbox, spare, late, k_kept, v_kept = lax.switch(lane.reshape(()), forms, h, q_all, kv, part_o, part_l, outbox, late_box, k_kept)
         k_out, v_out = run_finish(meta, moved, gone, where, (inbox, spare, late), (kv_all0, kv_all1), k_kept, v_kept)
         k_out, v_out = k_out.reshape(k_pool.shape), v_out.reshape(v_pool.shape)
         y = lax.dynamic_slice_in_dim(h.reshape(2, 32, D), (me % 2) * 16, 16, axis=1)

time: 232 us -> 229 us (0.987)
  the two profiles are of different devices: /device:TPU:0 before, /device:TPU:5 now
where the time goes in v6:
time: 229 us; the launch traced here: 227 us
  Pallas kernels  221 us (97%)
    pallas_call x2, Pallas kernels, run_rest(): pl.pallas_call(functools.partial(rest_kernel, layer, lane_core), name=f'r...  163 us
    pallas_call x2, Pallas kernels, run_attend(): pl.pallas_call(functools.partial(attend_kernel, layer), name=f'attend{lay...  29.3 us
    pallas_call x1, Pallas kernels, run_qkv(): pl.pallas_call(functools.partial(qkv_kernel, layer, first), name=f'qkv{la...  16.2 us
    pallas_call x1, Pallas kernels, run_finish(): pl.pallas_call(finish_kernel, name='finish', out_shape=[shape, shape], in...  7.82 us
    pallas_call x1, Pallas kernels, run_plan(): pl.pallas_call(plan_kernel, name='plan', out_shape=[jax.ShapeDtypeStruct(...  5.17 us
  transfers between devices with their start and end apart: 1, of which 0 were waited for; matrix products, arithmetic and copies ran while one was open for 0% of the time, Pallas kernels for 41%

profile of v6, /device:TPU:5, one launch (start us, length us, event | category | flops | bytes accessed | tf_op | source)
XLA Modules:
  0.0 226.6 jit_solution(14764490811195863315)
XLA Ops:
  0.6 5.2 %plan.1 = (s32[5]{0:T(128)S(1)}, s32[7,68]{1,0:T(8,128)S(1)}, s32[97]{0:T(128)S(1)}, s32[65]{0:T(128)}, s32[2,65]{1,0:T(2,128)}, /*index=5*/s32[3,65]{1,0:T(4,128)}, s32[10]{0:T(128)}, s32[1]{0:T(128)}, s32[1]{0:T(128)}) custom-call(s32[2,64]{1,0:T(2,128)} %bitcast.18, s32[64]{0:T(128)} %seq_lens.1, s32[64]{0:T(128)} %mig_src.1, s32[64]{0:T(128)} %mig_dst.1), custom_call_target="tpu_custom_call" | custom-call | tf_op jit(solution)/shard_map/plan/pallas_call | solution.py:263
  5.8 0.0 copy-start.1
  5.8 0.0 copy-start.6
  5.8 0.0 copy-start.9
  5.8 16.2 %qkv0.1 = (bf16[2,8,64,512]{3,2,1,0:T(8,128)(2,1)}, bf16[64,1024]{1,0:T(8,128)(2,1)}, bf16[64,4096]{1,0:T(8,128)(2,1)}) custom-call(bf16[2,16,4096]{2,1,0:T(8,128)(2,1)} %refs_0_.1, bf16[2,4096,4096]{2,1,0:T(8,128)(2,1)} %refs_1_.1, bf16[2,4096,1024]{2,1,0:T(8,128)(2,1)} %refs_2_.1, bf16[2,4096,1024]{2,1,0:T(8,128)(2,1)} %refs_3_.1), custom_call_target="tpu_custom_call" | custom-call | flops 12884901888 | bytes 25165824 | tf_op jit(solution)/shard_map/qkv0/pallas_call | solution.py:154
  22.0 0.0 copy-done.1
  22.0 0.0 copy-done.6
  22.0 0.0 copy-done.9
  22.0 13.3 %attend0.1 = (f32[2,2,64,16,128]{4,3,2,1,0:T(8,128)}, f32[2,2,64,16,128]{4,3,2,1,0:T(8,128)}, bf16[192,2,256,128]{3,2,1,0:T(8,128)(2,1)}, bf16[96,2,256,128]{3,2,1,0:T(8,128)(2,1)}, bf16[9,2,2,256,128]{4,3,2,1,0:T(8,128)(2,1)}) custom-call(s32[5]{0:T(128)S(1)} %get-tuple-element.206.meta, s32[7,68]{1,0:T(8,128)S(1)} %get-tuple-element.207.table, ...), custom_call_target="tpu_custom_call" | custom-call | flops 20000000000 | bytes 16777216 | tf_op jit(solution)/shard_map/attend0/pallas_call | solution.py:466
  36.0 182.1 %conditional.5 = (bf16[64,4096]{1,0:T(8,128)(2,1)}, bf16[4,64,1024]{2,1,0:T(8,128)(2,1)}, bf16[4,64,1024]{2,1,0:T(8,128)(2,1)}, bf16[192,2,256,128]{3,2,1,0:T(8,...) conditional(s32[]{:T(128)} %bitcast.3, ...), branch_computations={%region_0.0_spmd, %region_5.0_spmd} | conditional | flops 140259082240 | bytes 261106976 | solution.py:1020
  36.0 85.6 %rest0_0.1 = (bf16[64,4096]{1,0:T(8,128)(2,1)}, bf16[4,64,1024]{2,1,0:T(8,128)(2,1)}, bf16[192,2,256,128]{3,2,1,0:T(8,128)(2,1)}, bf16[2,8,64,512]{3,2,1,0:T(8,128)(2,1)}, bf16[64,1024]{1,0:T(8,128)(2,1)}) custom-call(bf16[64,4096]{1,0:T(8,128)(2,1)} %get-tuple-element.100.h_in, bf16[2,8,64,512]{3,2,1,0:T(8,128)(2,1)} %get-tuple-element.101.q_all, ...), custom_call_target="tpu_custom_call" | custom-call | flops 60129542144 | bytes 117440512 | tf_op jit(solution)/shard_map/cond/branch_0_fun/rest0_0/pallas_call | solution.py:807
  121.6 1.3 collective-permute-start
  123.6 0.0 copy-start.2
  123.6 0.0 copy-start.4
  123.6 0.0 copy-start.7
  123.6 0.0 copy-start.10
  123.7 0.6 copy-done.2
  124.3 0.0 copy-done.4
  124.3 0.0 copy-done.7
  124.3 16.0 %attend1.2 = (f32[2,2,64,16,128]{4,3,2,1,0:T(8,128)}, f32[2,2,64,16,128]{4,3,2,1,0:T(8,128)}, bf16[192,2,256,128]{3,2,1,0:T(8,128)(2,1)}, bf16[96,2,256,128]{3,2,1,0:T(8,128)(2,1)}, bf16[96,2,256,128]{3,2,1,0:T(8,128)(2,1)}) custom-call(s32[5]{0:T(128)S(1)} %copy-done.7, s32[7,68]{1,0:T(8,128)S(1)} %copy-done.2, ...), custom_call_target="tpu_custom_call", output_to_operand_aliasing={{4}: (9, {})} | custom-call | flops 20000000000 | bytes 16777216 | tf_op jit(solution)/shard_map/cond/branch_0_fun/attend1/pallas_call | solution.py:466
  140.3 77.2 %rest1_0.1 = (bf16[64,4096]{1,0:T(8,128)(2,1)}, bf16[4,64,1024]{2,1,0:T(8,128)(2,1)}, bf16[192,2,256,128]{3,2,1,0:T(8,128)(2,1)}) custom-call(bf16[64,4096]{1,0:T(8,128)(2,1)} %get-tuple-element.112.h_in, bf16[2,8,64,512]{3,2,1,0:T(8,128)(2,1)} %get-tuple-element.115.q_all, bf16[64,1024]{1,0:T(8,128)(2,1)} %get-tuple-element.116.kv, ...), custom_call_target="tpu_custom_call" | custom-call | flops 60129542144 | bytes 117440512 | tf_op jit(solution)/shard_map/cond/branch_0_fun/rest1_0/pallas_call | solution.py:807
  217.5 0.0 collective-permute-done
  218.1 7.8 %finish.1 = (bf16[96,2,256,128]{3,2,1,0:T(8,128)(2,1)}, bf16[96,2,256,128]{3,2,1,0:T(8,128)(2,1)}) custom-call(s32[5]{0:T(128)} %copy-done.6, s32[2,65]{1,0:T(2,128)} %get-tuple-element.215.moved, s32[65]{0:T(128)} %get-tuple-element.218.gone, s32[3,65]{1,0:T(4,128)} %get-tuple-element.219.rows, ...), custom_call_target="tpu_custom_call", output_to_operand_aliasing={{0}: (9, {}), {1}: (10, {})} | custom-call | flops 10000000000 | bytes 16777216 | tf_op jit(solution)/shard_map/finish/pallas_call | solution.py:973
  225.9 0.7 constant_dynamic-slice_fusion
  (7 shorter events, 0.1 us)
Async XLA Ops:
  5.8 16.2 %copy-start.1 = (s32[7,68]{1,0:T(8,128)}, s32[7,68]{1,0:T(8,128)S(1)}, u32[]{:S(2)}) copy-start(s32[7,68]{1,0:T(8,128)S(1)} %get-tuple-element.207.table) | copy-start | bytes 5716
  5.8 16.2 %copy-start.6 = (s32[5]{0:T(128)}, s32[5]{0:T(128)S(1)}, u32[]{:S(2)}) copy-start(s32[5]{0:T(128)S(1)} %get-tuple-element.206.meta) | copy-start | bytes 64
  5.8 16.2 %copy-start.9 = (s32[97]{0:T(128)}, s32[97]{0:T(128)S(1)}, u32[]{:S(2)}) copy-start(s32[97]{0:T(128)S(1)} %get-tuple-element.208.slots) | copy-start | bytes 1168
  121.6 95.9 %collective-permute-start = (bf16[9,2,2,256,128]{4,3,2,1,0:T(8,128)(2,1)}, bf16[9,2,2,256,128]{4,3,2,1,0:T(8,128)(2,1)}, u32[]{:S(2)}, u32[]{:S(2)}) collective-permute-start(bf16[9,2,2,256,128]{4,3,2,1,0:T(8,128)(2,1)} %get-tuple-element.133), channel_id=1, source_target_pairs={{0,3},{2,1},{4,7},{6,5}} | collective-permute-start | bytes 7077896 | tf_op jit(solution)/shard_map/cond/branch_0_fun/ppermute | solution.py:1014
  123.6 0.7 copy-start.2
  123.6 0.7 copy-start.4
  123.6 0.7 copy-start.7
  123.6 0.7 copy-start.10
  218.1 7.9 %copy-start = (bf16[64,4096]{1,0:T(8,128)(2,1)S(1)}, bf16[64,4096]{1,0:T(8,128)(2,1)}, u32[]{:S(2)}) copy-start(bf16[64,4096]{1,0:T(8,128)(2,1)} %get-tuple-element.217) | copy-start | bytes 1572868

commit v7 on v6

--- a/solution.py
+++ b/solution.py
@@ -31,7 +31,7 @@
 SLOTS = 96
 UNROLL = 4
 FAST_PAGES = 32
-LATE = 23
+LATE = 21
 LATES = FAST_PAGES - LATE
 BOX = jax.ShapeDtypeStruct((3 * MIG, 2, PAGE * KV_HEADS, HEAD), BF16)
 
@@ -121,19 +121,14 @@
             if i + WINDOW < 6:
                 pl.when(j == i)(lambda i=i: fetch(i + WINDOW).start())
 
-        @pl.when(j > 0)
-        def _():
-            to_across(j - 1).start()
-            to_partner(j - 1).start()
+        to_across(j).start()
+        to_partner(j).start()
         return carry
 
     lax.fori_loop(0, 4, tile, 0)
     for j in range(4, 6):
         fetch(j).wait()
         kv[:, (j - 4) * TN:(j - 3) * TN] = dot(h[...], wbuf[j]).astype(BF16)
-        if j == 4:
-            to_across(3).start()
-            to_partner(3).start()
     for j in range(4):
         to_across(j).wait_recv()
         forward(j).start()
@@ -270,8 +265,8 @@
     )(new_table.T, seq_lens, mig_src, mig_dst)
 
 
-NBUF = 6
-AFTER = 2
+NBUF = 4
+AFTER = 1
 DIST = NBUF - AFTER
 STEPS = SEQS // UNROLL
 SLOTS_STEP = SLOTS // STEPS
@@ -367,7 +362,7 @@
         settle(0)
     else:
         late(0)
-    kvbuf[...] = jnp.zeros_like(kvbuf)
+    kvbuf[:, :, :, 1] = jnp.zeros((NBUF, UNROLL, 2) + kvbuf.shape[4:], BF16)
     for g in range(DIST):
         @pl.when(g < groups)
         def _():
@@ -776,10 +771,10 @@
             def _():
                 kv_next[:, pl.ds(pl.multiple_of((j - 4) * TN, TN), TN)] = tile
 
-            @pl.when((j > 0) & (j < 5))
+            @pl.when(j < 4)
             def _():
-                to_across(j - 1).start()
-                to_partner(j - 1).start()
+                to_across(j).start()
+                to_partner(j).start()
             return carry
 
         lax.fori_loop(0, 6, project_next, 0)

time: 229 us -> 226 us (0.987)
  the two profiles are of different devices: /device:TPU:5 before, /device:TPU:0 now
where the time goes in v7:
time: 226 us
  Pallas kernels  217 us (96%)
  starting transfers between devices  5.44 us (2%)
    pallas_call x2, Pallas kernels, run_rest(): pl.pallas_call(functools.partial(rest_kernel, layer, lane_core), name=f'r...  129 us
    pallas_call x2, Pallas kernels, run_attend(): pl.pallas_call(functools.partial(attend_kernel, layer), name=f'attend{lay...  58.5 us
    pallas_call x1, Pallas kernels, run_qkv(): pl.pallas_call(functools.partial(qkv_kernel, layer, first), name=f'qkv{la...  16.2 us
    pallas_call x1, Pallas kernels, run_finish(): pl.pallas_call(finish_kernel, name='finish', out_shape=[shape, shape], in...  7.97 us
    ppermute x1, starting transfers between devices, layers(): lax.ppermute(late_box, 'kv', [(core, 3 - core), (2 + core, 1 - core)])  5.44 us
    pallas_call x1, Pallas kernels, run_plan(): pl.pallas_call(plan_kernel, name='plan', out_shape=[jax.ShapeDtypeStruct(...  5.18 us
  transfers between devices with their start and end apart: 1, of which 0 were waited for; matrix products, arithmetic and copies ran while one was open for 0% of the time, Pallas kernels for 40%

profile of v7, /device:TPU:0, one launch (start us, length us, event | category | flops | bytes accessed | tf_op | source)
XLA Modules:
  0.0 226.3 jit_solution(1344486082052096387)
XLA Ops:
  0.6 5.2 %plan.1 = (s32[5]{0:T(128)S(1)}, s32[7,68]{1,0:T(8,128)S(1)}, s32[97]{0:T(128)S(1)}, s32[65]{0:T(128)}, s32[2,65]{1,0:T(2,128)}, /*index=5*/s32[3,65]{1,0:T(4,128)}, s32[12]{0:T(128)}, s32[1]{0:T(128)}, s32[1]{0:T(128)}) custom-call(s32[2,64]{1,0:T(2,128)} %bitcast.18, s32[64]{0:T(128)} %seq_lens.1, s32[64]{0:T(128)} %mig_src.1, s32[64]{0:T(128)} %mig_dst.1), custom_call_target="tpu_custom_call" | custom-call | tf_op jit(solution)/shard_map/plan/pallas_call | solution.py:258
  5.8 0.0 copy-start.1
  5.8 0.0 copy-start.6
  5.8 0.0 copy-start.9
  5.8 16.2 %qkv0.1 = (bf16[2,8,64,512]{3,2,1,0:T(8,128)(2,1)}, bf16[64,1024]{1,0:T(8,128)(2,1)}, bf16[64,4096]{1,0:T(8,128)(2,1)}) custom-call(bf16[2,16,4096]{2,1,0:T(8,128)(2,1)} %refs_0_.1, bf16[2,4096,4096]{2,1,0:T(8,128)(2,1)} %refs_1_.1, bf16[2,4096,1024]{2,1,0:T(8,128)(2,1)} %refs_2_.1, bf16[2,4096,1024]{2,1,0:T(8,128)(2,1)} %refs_3_.1), custom_call_target="tpu_custom_call" | custom-call | flops 12884901888 | bytes 25165824 | tf_op jit(solution)/shard_map/qkv0/pallas_call | solution.py:149
  22.1 0.0 copy-done.1
  22.1 0.0 copy-done.6
  22.1 0.0 copy-done.9
  22.1 29.3 %attend0.1 = (f32[2,2,64,16,128]{4,3,2,1,0:T(8,128)}, f32[2,2,64,16,128]{4,3,2,1,0:T(8,128)}, bf16[192,2,256,128]{3,2,1,0:T(8,128)(2,1)}, bf16[96,2,256,128]{3,2,1,0:T(8,128)(2,1)}, bf16[11,2,2,256,128]{4,3,2,1,0:T(8,128)(2,1)}) custom-call(s32[5]{0:T(128)S(1)} %get-tuple-element.206.meta, s32[7,68]{1,0:T(8,128)S(1)} %get-tuple-element.207.table, ...), custom_call_target="tpu_custom_call" | custom-call | flops 20000000000 | bytes 16777216 | tf_op jit(solution)/shard_map/attend0/pallas_call | solution.py:461
  52.0 165.5 %conditional.5 = (bf16[64,4096]{1,0:T(8,128)(2,1)}, bf16[4,64,1024]{2,1,0:T(8,128)(2,1)}, bf16[4,64,1024]{2,1,0:T(8,128)(2,1)}, bf16[192,2,256,128]{3,2,1,0:T(8,...) conditional(s32[]{:T(128)} %bitcast.3, ...), branch_computations={%region_0.0_spmd, %region_5.0_spmd} | conditional | flops 140259082240 | bytes 263204128 | solution.py:1015
  52.0 68.8 %rest0_0.1 = (bf16[64,4096]{1,0:T(8,128)(2,1)}, bf16[4,64,1024]{2,1,0:T(8,128)(2,1)}, bf16[192,2,256,128]{3,2,1,0:T(8,128)(2,1)}, bf16[2,8,64,512]{3,2,1,0:T(8,128)(2,1)}, bf16[64,1024]{1,0:T(8,128)(2,1)}) custom-call(bf16[64,4096]{1,0:T(8,128)(2,1)} %get-tuple-element.100.h_in, bf16[2,8,64,512]{3,2,1,0:T(8,128)(2,1)} %get-tuple-element.101.q_all, ...), custom_call_target="tpu_custom_call" | custom-call | flops 60129542144 | bytes 117440512 | tf_op jit(solution)/shard_map/cond/branch_0_fun/rest0_0/pallas_call | solution.py:802
  120.8 5.4 %collective-permute-start = (bf16[11,2,2,256,128]{4,3,2,1,0:T(8,128)(2,1)}, bf16[11,2,2,256,128]{4,3,2,1,0:T(8,128)(2,1)}, u32[]{:S(2)}, u32[]{:S(2)}) collective-permute-start(bf16[11,2,2,256,128]{4,3,2,1,0:T(8,128)(2,1)} %get-tuple-element.133), channel_id=1, source_target_pairs={{0,3},{2,1},{4,7},{6,5}} | collective-permute-start | bytes 8650760 | tf_op jit(solution)/shard_map/cond/branch_0_fun/ppermute | solution.py:1009
  126.8 0.0 copy-start.2
  126.8 0.0 copy-start.4
  126.8 0.0 copy-start.7
  126.8 0.0 copy-start.10
  126.9 0.6 copy-done.2
  127.5 0.0 copy-done.4
  127.5 0.0 copy-done.7
  127.5 29.2 %attend1.2 = (f32[2,2,64,16,128]{4,3,2,1,0:T(8,128)}, f32[2,2,64,16,128]{4,3,2,1,0:T(8,128)}, bf16[192,2,256,128]{3,2,1,0:T(8,128)(2,1)}, bf16[96,2,256,128]{3,2,1,0:T(8,128)(2,1)}, bf16[96,2,256,128]{3,2,1,0:T(8,128)(2,1)}) custom-call(s32[5]{0:T(128)S(1)} %copy-done.7, s32[7,68]{1,0:T(8,128)S(1)} %copy-done.2, ...), custom_call_target="tpu_custom_call", output_to_operand_aliasing={{4}: (9, {})} | custom-call | flops 20000000000 | bytes 16777216 | tf_op jit(solution)/shard_map/cond/branch_0_fun/attend1/pallas_call | solution.py:461
  156.7 60.3 %rest1_0.1 = (bf16[64,4096]{1,0:T(8,128)(2,1)}, bf16[4,64,1024]{2,1,0:T(8,128)(2,1)}, bf16[192,2,256,128]{3,2,1,0:T(8,128)(2,1)}) custom-call(bf16[64,4096]{1,0:T(8,128)(2,1)} %get-tuple-element.112.h_in, bf16[2,8,64,512]{3,2,1,0:T(8,128)(2,1)} %get-tuple-element.115.q_all, bf16[64,1024]{1,0:T(8,128)(2,1)} %get-tuple-element.116.kv, ...), custom_call_target="tpu_custom_call" | custom-call | flops 60129542144 | bytes 117440512 | tf_op jit(solution)/shard_map/cond/branch_0_fun/rest1_0/pallas_call | solution.py:802
  217.0 0.0 collective-permute-done
  217.5 8.0 %finish.1 = (bf16[96,2,256,128]{3,2,1,0:T(8,128)(2,1)}, bf16[96,2,256,128]{3,2,1,0:T(8,128)(2,1)}) custom-call(s32[5]{0:T(128)} %copy-done.6, s32[2,65]{1,0:T(2,128)} %get-tuple-element.215.moved, s32[65]{0:T(128)} %get-tuple-element.218.gone, s32[3,65]{1,0:T(4,128)} %get-tuple-element.219.rows, ...), custom_call_target="tpu_custom_call", output_to_operand_aliasing={{0}: (9, {}), {1}: (10, {})} | custom-call | flops 10000000000 | bytes 16777216 | tf_op jit(solution)/shard_map/finish/pallas_call | solution.py:968
  225.5 0.7 constant_dynamic-slice_fusion
  (7 shorter events, 0.1 us)
Async XLA Ops:
  5.8 16.2 %copy-start.1 = (s32[7,68]{1,0:T(8,128)}, s32[7,68]{1,0:T(8,128)S(1)}, u32[]{:S(2)}) copy-start(s32[7,68]{1,0:T(8,128)S(1)} %get-tuple-element.207.table) | copy-start | bytes 5716
  5.8 16.2 %copy-start.6 = (s32[5]{0:T(128)}, s32[5]{0:T(128)S(1)}, u32[]{:S(2)}) copy-start(s32[5]{0:T(128)S(1)} %get-tuple-element.206.meta) | copy-start | bytes 64
  5.8 16.2 %copy-start.9 = (s32[97]{0:T(128)}, s32[97]{0:T(128)S(1)}, u32[]{:S(2)}) copy-start(s32[97]{0:T(128)S(1)} %get-tuple-element.208.slots) | copy-start | bytes 1168
  120.8 96.2 %collective-permute-start = (bf16[11,2,2,256,128]{4,3,2,1,0:T(8,128)(2,1)}, bf16[11,2,2,256,128]{4,3,2,1,0:T(8,128)(2,1)}, u32[]{:S(2)}, u32[]{:S(2)}) collective-permute-start(bf16[11,2,2,256,128]{4,3,2,1,0:T(8,128)(2,1)} %get-tuple-element.133), channel_id=1, source_target_pairs={{0,3},{2,1},{4,7},{6,5}} | collective-permute-start | bytes 8650760 | tf_op jit(solution)/shard_map/cond/branch_0_fun/ppermute | solution.py:1009
  126.8 0.7 copy-start.2
  126.8 0.7 copy-start.4
  126.8 0.7 copy-start.7
  126.8 0.7 copy-start.10
  217.5 8.0 %copy-start = (bf16[64,4096]{1,0:T(8,128)(2,1)S(1)}, bf16[64,4096]{1,0:T(8,128)(2,1)}, u32[]{:S(2)}) copy-start(bf16[64,4096]{1,0:T(8,128)(2,1)} %get-tuple-element.217) | copy-start | bytes 1572868

commit v8 on v7

--- a/solution.py
+++ b/solution.py
@@ -31,7 +31,7 @@
 SLOTS = 96
 UNROLL = 4
 FAST_PAGES = 32
-LATE = 21
+LATE = 20
 LATES = FAST_PAGES - LATE
 BOX = jax.ShapeDtypeStruct((3 * MIG, 2, PAGE * KV_HEADS, HEAD), BF16)
 
@@ -492,7 +492,7 @@
 
 LANES = ([((0,), 2, LATE), ((0,), 0, FAST_PAGES)], [((1,), 2, LATE), ((1,), 0, FAST_PAGES)])
 EVERYTHING = [((0, 1), i, MIG) for i in range(3)]
-CHUNK = 1
+CHUNK = 4
 
 
 class Boxes:
@@ -614,7 +614,7 @@
             compact = jnp.where(lane == 2 * i, l[:8], compact)
             return jnp.where(lane == 2 * i + 1, l[8:], compact)
 
-        give_l[part] = lax.fori_loop(0, PART, chip_merge, jnp.zeros((8, HEAD), F32), unroll=4)
+        give_l[part] = lax.fori_loop(0, PART, chip_merge, jnp.zeros((8, HEAD), F32), unroll=8)
         rows = pl.ds(part * PART, PART)
         pair = [
             send(give_l.at[part], far_l.at[part], xsend.at[part, 0], xrecv.at[part, 0], across),
@@ -680,7 +680,7 @@
             q_rows[pl.ds(pl.multiple_of(j * HALF_HEADS, HALF_HEADS), HALF_HEADS), :] = o
             return carry
 
-        lax.fori_loop(0, PART, last_merge, 0, unroll=4)
+        lax.fori_loop(0, PART, last_merge, 0, unroll=8)
     for head in range(HALF_HEADS):
         attn[:, head * HEAD:(head + 1) * HEAD] = q_rows[pl.ds(head, TOK, stride=HALF_HEADS), :].astype(BF16)
 

time: 226 us -> 220 us (0.973)
  Pallas kernels: 217 us -> 209 us
    pallas_call x2, Pallas kernels: 129 us -> 123 us  [run_rest(): pl.pallas_call(functools.partial(rest_kernel, layer, lane_core), name=f'r...]
  transfers between devices with their start and end apart: 1 -> 1, of which waited for: 0 -> 0; matrix products, arithmetic and copies ran while one was open for 0% -> 0% of each run, Pallas kernels for 40% -> 39%
where the time goes in v8:
time: 220 us; the launch traced here: 219 us
  Pallas kernels  209 us (95%)
  starting transfers between devices  5.49 us (2%)
    pallas_call x2, Pallas kernels, run_rest(): pl.pallas_call(functools.partial(rest_kernel, layer, lane_core), name=f'r...  123 us
    pallas_call x2, Pallas kernels, run_attend(): pl.pallas_call(functools.partial(attend_kernel, layer), name=f'attend{lay...  56.8 us
    pallas_call x1, Pallas kernels, run_qkv(): pl.pallas_call(functools.partial(qkv_kernel, layer, first), name=f'qkv{la...  16.2 us
    pallas_call x1, Pallas kernels, run_finish(): pl.pallas_call(finish_kernel, name='finish', out_shape=[shape, shape], in...  7.97 us
    ppermute x1, starting transfers between devices, layers(): lax.ppermute(late_box, 'kv', [(core, 3 - core), (2 + core, 1 - core)])  5.49 us
    pallas_call x1, Pallas kernels, run_plan(): pl.pallas_call(plan_kernel, name='plan', out_shape=[jax.ShapeDtypeStruct(...  5.18 us
  transfers between devices with their start and end apart: 1, of which 0 were waited for; matrix products, arithmetic and copies ran while one was open for 0% of the time, Pallas kernels for 39%

profile of v8, /device:TPU:0, one launch (start us, length us, event | category | flops | bytes accessed | tf_op | source)
XLA Modules:
  0.0 218.6 jit_solution(4248208230123755206)
XLA Ops:
  0.6 5.2 %plan.1 = (s32[5]{0:T(128)S(1)}, s32[7,68]{1,0:T(8,128)S(1)}, s32[97]{0:T(128)S(1)}, s32[65]{0:T(128)}, s32[2,65]{1,0:T(2,128)}, /*index=5*/s32[3,65]{1,0:T(4,128)}, s32[13]{0:T(128)}, s32[1]{0:T(128)}, s32[1]{0:T(128)}) custom-call(s32[2,64]{1,0:T(2,128)} %bitcast.18, s32[64]{0:T(128)} %seq_lens.1, s32[64]{0:T(128)} %mig_src.1, s32[64]{0:T(128)} %mig_dst.1), custom_call_target="tpu_custom_call" | custom-call | tf_op jit(solution)/shard_map/plan/pallas_call | solution.py:258
  5.8 0.0 copy-start.1
  5.8 0.0 copy-start.6
  5.8 0.0 copy-start.9
  5.8 16.2 %qkv0.1 = (bf16[2,8,64,512]{3,2,1,0:T(8,128)(2,1)}, bf16[64,1024]{1,0:T(8,128)(2,1)}, bf16[64,4096]{1,0:T(8,128)(2,1)}) custom-call(bf16[2,16,4096]{2,1,0:T(8,128)(2,1)} %refs_0_.1, bf16[2,4096,4096]{2,1,0:T(8,128)(2,1)} %refs_1_.1, bf16[2,4096,1024]{2,1,0:T(8,128)(2,1)} %refs_2_.1, bf16[2,4096,1024]{2,1,0:T(8,128)(2,1)} %refs_3_.1), custom_call_target="tpu_custom_call" | custom-call | flops 12884901888 | bytes 25165824 | tf_op jit(solution)/shard_map/qkv0/pallas_call | solution.py:149
  22.0 0.0 copy-done.1
  22.0 0.0 copy-done.6
  22.0 0.0 copy-done.9
  22.0 28.4 %attend0.1 = (f32[2,2,64,16,128]{4,3,2,1,0:T(8,128)}, f32[2,2,64,16,128]{4,3,2,1,0:T(8,128)}, bf16[192,2,256,128]{3,2,1,0:T(8,128)(2,1)}, bf16[96,2,256,128]{3,2,1,0:T(8,128)(2,1)}, bf16[12,2,2,256,128]{4,3,2,1,0:T(8,128)(2,1)}) custom-call(s32[5]{0:T(128)S(1)} %get-tuple-element.206.meta, s32[7,68]{1,0:T(8,128)S(1)} %get-tuple-element.207.table, ...), custom_call_target="tpu_custom_call" | custom-call | flops 20000000000 | bytes 16777216 | tf_op jit(solution)/shard_map/attend0/pallas_call | solution.py:461
  51.1 158.7 %conditional.5 = (bf16[64,4096]{1,0:T(8,128)(2,1)}, bf16[4,64,1024]{2,1,0:T(8,128)(2,1)}, bf16[4,64,1024]{2,1,0:T(8,128)(2,1)}, bf16[192,2,256,128]{3,2,1,0:T(8,...) conditional(s32[]{:T(128)} %bitcast.3, ...), branch_computations={%region_0.0_spmd, %region_5.0_spmd} | conditional | flops 140259082240 | bytes 264252704 | solution.py:1015
  51.1 65.8 %rest0_0.1 = (bf16[64,4096]{1,0:T(8,128)(2,1)}, bf16[4,64,1024]{2,1,0:T(8,128)(2,1)}, bf16[192,2,256,128]{3,2,1,0:T(8,128)(2,1)}, bf16[2,8,64,512]{3,2,1,0:T(8,128)(2,1)}, bf16[64,1024]{1,0:T(8,128)(2,1)}) custom-call(bf16[64,4096]{1,0:T(8,128)(2,1)} %get-tuple-element.100.h_in, bf16[2,8,64,512]{3,2,1,0:T(8,128)(2,1)} %get-tuple-element.101.q_all, ...), custom_call_target="tpu_custom_call" | custom-call | flops 60129542144 | bytes 117440512 | tf_op jit(solution)/shard_map/cond/branch_0_fun/rest0_0/pallas_call | solution.py:802
  116.9 5.5 %collective-permute-start = (bf16[12,2,2,256,128]{4,3,2,1,0:T(8,128)(2,1)}, bf16[12,2,2,256,128]{4,3,2,1,0:T(8,128)(2,1)}, u32[]{:S(2)}, u32[]{:S(2)}) collective-permute-start(bf16[12,2,2,256,128]{4,3,2,1,0:T(8,128)(2,1)} %get-tuple-element.133), channel_id=1, source_target_pairs={{0,3},{2,1},{4,7},{6,5}} | collective-permute-start | bytes 9437192 | tf_op jit(solution)/shard_map/cond/branch_0_fun/ppermute | solution.py:1009
  123.1 0.0 copy-start.2
  123.1 0.0 copy-start.4
  123.1 0.0 copy-start.7
  123.1 0.0 copy-start.10
  123.2 0.6 copy-done.2
  123.8 0.0 copy-done.4
  123.8 0.0 copy-done.10
  123.8 28.4 %attend1.2 = (f32[2,2,64,16,128]{4,3,2,1,0:T(8,128)}, f32[2,2,64,16,128]{4,3,2,1,0:T(8,128)}, bf16[192,2,256,128]{3,2,1,0:T(8,128)(2,1)}, bf16[96,2,256,128]{3,2,1,0:T(8,128)(2,1)}, bf16[96,2,256,128]{3,2,1,0:T(8,128)(2,1)}) custom-call(s32[5]{0:T(128)S(1)} %copy-done.7, s32[7,68]{1,0:T(8,128)S(1)} %copy-done.2, ...), custom_call_target="tpu_custom_call", output_to_operand_aliasing={{4}: (9, {})} | custom-call | flops 20000000000 | bytes 16777216 | tf_op jit(solution)/shard_map/cond/branch_0_fun/attend1/pallas_call | solution.py:461
  152.2 57.4 %rest1_0.1 = (bf16[64,4096]{1,0:T(8,128)(2,1)}, bf16[4,64,1024]{2,1,0:T(8,128)(2,1)}, bf16[192,2,256,128]{3,2,1,0:T(8,128)(2,1)}) custom-call(bf16[64,4096]{1,0:T(8,128)(2,1)} %get-tuple-element.112.h_in, bf16[2,8,64,512]{3,2,1,0:T(8,128)(2,1)} %get-tuple-element.115.q_all, bf16[64,1024]{1,0:T(8,128)(2,1)} %get-tuple-element.116.kv, ...), custom_call_target="tpu_custom_call" | custom-call | flops 60129542144 | bytes 117440512 | tf_op jit(solution)/shard_map/cond/branch_0_fun/rest1_0/pallas_call | solution.py:802
  209.6 0.0 collective-permute-done
  209.9 8.0 %finish.1 = (bf16[96,2,256,128]{3,2,1,0:T(8,128)(2,1)}, bf16[96,2,256,128]{3,2,1,0:T(8,128)(2,1)}) custom-call(s32[5]{0:T(128)} %copy-done.6, s32[2,65]{1,0:T(2,128)} %get-tuple-element.215.moved, s32[65]{0:T(128)} %get-tuple-element.218.gone, s32[3,65]{1,0:T(4,128)} %get-tuple-element.219.rows, ...), custom_call_target="tpu_custom_call", output_to_operand_aliasing={{0}: (9, {}), {1}: (10, {})} | custom-call | flops 10000000000 | bytes 16777216 | tf_op jit(solution)/shard_map/finish/pallas_call | solution.py:968
  217.9 0.7 constant_dynamic-slice_fusion
  (7 shorter events, 0.1 us)
Async XLA Ops:
  5.8 16.2 %copy-start.1 = (s32[7,68]{1,0:T(8,128)}, s32[7,68]{1,0:T(8,128)S(1)}, u32[]{:S(2)}) copy-start(s32[7,68]{1,0:T(8,128)S(1)} %get-tuple-element.207.table) | copy-start | bytes 5716
  5.8 16.2 %copy-start.6 = (s32[5]{0:T(128)}, s32[5]{0:T(128)S(1)}, u32[]{:S(2)}) copy-start(s32[5]{0:T(128)S(1)} %get-tuple-element.206.meta) | copy-start | bytes 64
  5.8 16.2 %copy-start.9 = (s32[97]{0:T(128)}, s32[97]{0:T(128)S(1)}, u32[]{:S(2)}) copy-start(s32[97]{0:T(128)S(1)} %get-tuple-element.208.slots) | copy-start | bytes 1168
  116.9 92.7 %collective-permute-start = (bf16[12,2,2,256,128]{4,3,2,1,0:T(8,128)(2,1)}, bf16[12,2,2,256,128]{4,3,2,1,0:T(8,128)(2,1)}, u32[]{:S(2)}, u32[]{:S(2)}) collective-permute-start(bf16[12,2,2,256,128]{4,3,2,1,0:T(8,128)(2,1)} %get-tuple-element.133), channel_id=1, source_target_pairs={{0,3},{2,1},{4,7},{6,5}} | collective-permute-start | bytes 9437192 | tf_op jit(solution)/shard_map/cond/branch_0_fun/ppermute | solution.py:1009
  123.1 0.7 copy-start.2
  123.1 0.7 copy-start.4
  123.1 0.7 copy-start.7
  123.1 0.7 copy-start.10
  209.9 8.0 %copy-start = (bf16[64,4096]{1,0:T(8,128)(2,1)S(1)}, bf16[64,4096]{1,0:T(8,128)(2,1)}, u32[]{:S(2)}) copy-start(bf16[64,4096]{1,0:T(8,128)(2,1)} %get-tuple-element.217) | copy-start | bytes 1572868
